TPU v7x, 32 devices: a whole 2x2x4 slice. The times are simulated.
32 devices in a mesh: dp: 2 (over x), tp: 4 (over z), sp: 4 (over y, core).
Axes of the slice: x: 2, y: 2, z: 4, core: 2. Of those that a mesh axis runs over, the one named last changes fastest.
Arguments:
- x_in: bfloat16 [256, 3840], P('dp'), parts along dimension 0
- cur_pos: int32 [256], P('dp'), parts along dimension 0
- w_pre: float32 [3840], replicated
- w_q: bfloat16 [3840, 4096], P(None, 'tp')
- w_k: bfloat16 [3840, 2048], P(None, 'tp')
- w_v: bfloat16 [3840, 2048], P(None, 'tp')
- w_o: bfloat16 [4096, 3840], P('tp')
- w_post: float32 [3840], replicated
- k_cache: bfloat16 [256, 256, 8, 256], P('dp', 'sp', 'tp'), parts along dimension 0
- v_cache: bfloat16 [256, 256, 8, 256], P('dp', 'sp', 'tp'), parts along dimension 0
Outputs:
- output 1: bfloat16 [256, 3840], P('dp'), parts along dimension 0
- output 2: bfloat16 [256, 256, 8, 256], P('dp', 'sp', 'tp'), parts along dimension 0
- output 3: bfloat16 [256, 256, 8, 256], P('dp', 'sp', 'tp'), parts along dimension 0
There are 2 independent parts. A program takes and returns all parts, laid end to end along the dimension named above; an argument that names none is the same for every part.
All inputs are finite; a program needn't handle non-finite values.
Results may differ from a plain program's by a relative error of at most 0.00644205.
Values sent between devices are 32-bit elements.
A program may use at most 1 GiB of HBM per device.

v0:
```python
import jax
import jax.numpy as jnp
from jax import lax
from jax.sharding import PartitionSpec as P

SOFT_CAP = 50.0
ROPE_BASE = 10000.0
NORM_EPS = 1e-6
NEG_FILL = -1e30


def rms_scale(tensor, gain_w):
    mean_sq = jnp.mean(tensor * tensor, axis=-1, keepdims=True)
    return tensor * lax.rsqrt(mean_sq + NORM_EPS) * (1.0 + gain_w)


def rotary(tensor, positions):
    half_dim = tensor.shape[-1] // 2
    inv_freq = ROPE_BASE ** (-2.0 * jnp.arange(half_dim, dtype=jnp.float32) / (2 * half_dim))
    angles = positions.astype(jnp.float32)[:, None] * inv_freq[None, :]
    angles = angles.reshape((angles.shape[0],) + (1,) * (tensor.ndim - 2) + (half_dim,))
    cos_tab = jnp.cos(angles)
    sin_tab = jnp.sin(angles)
    lo_half = tensor[..., :half_dim]
    hi_half = tensor[..., half_dim:]
    return jnp.concatenate([lo_half * cos_tab - hi_half * sin_tab, hi_half * cos_tab + lo_half * sin_tab], axis=-1)


def solution(mesh):
    cache_spec = P('dp', 'sp', 'tp', None)

    def local_step(x_in, cur_pos, w_pre, w_q, w_k, w_v, w_o, w_post, k_cache, v_cache):
        row_count, seq_block, kv_local, head_dim = k_cache.shape
        heads_local = w_q.shape[1] // head_dim
        group_size = heads_local // kv_local
        sp_index = lax.axis_index('sp')
        normed = rms_scale(x_in.astype(jnp.float32), w_pre).astype(jnp.bfloat16)
        q_proj = jnp.dot(normed, w_q, preferred_element_type=jnp.float32)
        q_rot = rotary(q_proj.reshape(row_count, kv_local, group_size, head_dim), cur_pos).astype(jnp.bfloat16)
        k_proj = jnp.dot(normed, w_k, preferred_element_type=jnp.float32)
        k_new = rotary(k_proj.reshape(row_count, kv_local, head_dim), cur_pos).astype(jnp.bfloat16)
        v_new = jnp.dot(normed, w_v, preferred_element_type=jnp.float32).reshape(row_count, kv_local, head_dim).astype(jnp.bfloat16)
        block_pos = sp_index * seq_block + jnp.arange(seq_block)
        slot_hit = (block_pos[None, :] == cur_pos[:, None])[:, :, None, None]
        k_out = jnp.where(slot_hit, k_new[:, None], k_cache)
        v_out = jnp.where(slot_hit, v_new[:, None], v_cache)
        raw_score = jnp.einsum('bgrd,btgd->bgrt', q_rot, k_out, preferred_element_type=jnp.float32)
        capped = SOFT_CAP * jnp.tanh(raw_score * (head_dim ** -0.5 / SOFT_CAP))
        is_valid = (block_pos[None, :] <= cur_pos[:, None])[:, None, None, :]
        capped = jnp.where(is_valid, capped, NEG_FILL)
        block_max = jnp.max(capped, axis=-1)
        exp_w = jnp.where(is_valid, jnp.exp(capped - block_max[..., None]), 0.0)
        block_sum = jnp.sum(exp_w, axis=-1)
        block_out = jnp.einsum('bgrt,btgd->bgrd', exp_w.astype(jnp.bfloat16), v_out, preferred_element_type=jnp.float32)
        global_max = lax.pmax(block_max, 'sp')
        factor = jnp.exp(block_max - global_max)
        packed = jnp.concatenate([block_out * factor[..., None], (block_sum * factor)[..., None]], axis=-1)
        merged = lax.psum(packed, 'sp')
        attn_out = (merged[..., :head_dim] / merged[..., head_dim:]).reshape(row_count, heads_local * head_dim)
        proj_part = jnp.dot(attn_out.astype(jnp.bfloat16), w_o, preferred_element_type=jnp.float32)
        proj_sum = lax.psum(proj_part, 'tp')
        x_out = (x_in.astype(jnp.float32) + rms_scale(proj_sum, w_post)).astype(jnp.bfloat16)
        return x_out, k_out, v_out

    return jax.shard_map(local_step, mesh=mesh,
                         in_specs=(P('dp', None), P('dp'), P(None), P(None, 'tp'), P(None, 'tp'), P(None, 'tp'), P('tp', None), P(None), cache_spec, cache_spec),
                         out_specs=(P('dp', None), cache_spec, cache_spec), check_vma=False)
```

profile of v0, /device:TPU:0, one launch (start us, length us, event | category | flops | bytes accessed | tf_op | source)
XLA Modules:
  0.0 208.1 jit_solution(10802535459351739475)
XLA Ops:
  7.2 0.0 copy-start
  7.2 0.0 copy-start.3
  7.2 0.0 all-reduce.3.cloned.1.call-start
  7.2 0.8 broadcast_add_fusion.1
  8.0 1.5 fusion.4
  9.5 3.1 %fusion.32 = f32[128,512]{1,0:T(8,128)S(1)} fusion(bf16[3840,512]{1,0:T(8,128)(2,1)} %param.14, bf16[128,3840]{1,0:T(8,128)(2,1)} %param.10, f32[3840]{0:T(1024)S(1)} %broadcast_add_fusion.1, f32[128]{0:T(128)S(1)} %add_rsqrt_fusion.1), kind=kOutput, calls=%fused_computation.48 | convolution fusion | flops 505282560 | bytes 5193216 | tf_op jit(solution)/shard_map/dot_general | solution.py:40
  12.7 0.2 reshape.209
  12.9 0.0 copy-done.3
  12.9 0.0 copy-done
  12.9 2.8 %convolution_convert_fusion = bf16[128,512]{1,0:T(8,128)(2,1)S(1)} fusion(bf16[3840,512]{1,0:T(8,128)(2,1)} %param.15, bf16[128,3840]{1,0:T(8,128)(2,1)S(1)} %copy-done, f32[3840]{0:T(1024)S(1)} %broadcast_add_fusion.1, f32[128]{0:T(128)S(1)} %add_rsqrt_fusion.1), kind=kOutput, calls=%fused_computation.14 | convolution fusion | flops 505348096 | bytes 5062144 | tf_op jit(solution)/shard_map/dot_general | solution.py:42
  15.8 0.1 broadcast_compare_fusion.1
  15.9 4.5 %fusion.34 = f32[128,1024]{1,0:T(8,128)S(1)} fusion(bf16[3840,1024]{1,0:T(8,128)(2,1)} %param.13, bf16[128,3840]{1,0:T(8,128)(2,1)S(1)} %copy-done, f32[3840]{0:T(1024)S(1)} %broadcast_add_fusion.1, f32[128]{0:T(128)S(1)} %add_rsqrt_fusion.1), kind=kOutput, calls=%fused_computation.49 | convolution fusion | flops 1008599040 | bytes 9387520 | tf_op jit(solution)/shard_map/dot_general | solution.py:38
  20.4 0.4 reshape.208
  20.8 0.3 multiply_cosine_fusion
  21.1 0.1 subtract_convert_fusion.1
  21.3 0.3 subtract_convert_fusion
  21.5 0.1 pad_maximum_fusion.1
  21.7 21.6 %broadcast_select_fusion = (bf16[128,64,2,256]{3,2,1,0:T(2,128)(2,1)}, bf16[128,64,2,256]{3,2,1,0:T(2,128)(2,1)S(1)}) fusion(bf16[128,64,2,256]{3,2,1,0:T(2,128)(2,1)} %param.19, pred[128,64]{1,0:T(8,128)(4,1)S(1)} %get-tuple-element.12, bf16[128,2,256]{2,1,0:T(2,128)(2,1)S(1)} %convert_element_type.44, bf16[128,64,2,256]{3,2,1,0:T(2,128)(2,1)} %param.18, ...), kind=kLoop, calls=%fused_computation | loop fusion | flops 8388608 | bytes 33824768 | tf_op jit(solution)/shard_map/jit(_where)/select_n | solution.py:46
  43.3 0.0 copy-start.1
  43.3 2.5 %fusion.36 = (f32[128,2,2]{2,1,0:T(2,128)S(1)}, f32[128,2,2,64]{3,2,1,0:T(2,128)S(1)}) fusion(bf16[128,64,2,256]{3,2,1,0:T(2,128)(2,1)S(1)} %get-tuple-element.10, bf16[128,2,2,128]{3,2,1,0:T(2,128)(2,1)S(1)} %get-tuple-element.6, bf16[128,2,2,128]{3,2,1,0:T(2,128)(2,1)S(1)} %get-tuple-element.5, pred[128,64]{1,0:T(8,128)(4,1)S(1)} %get-tuple-element.11), kind=kOutput, calls=%fused_computation.50 | convolution fusion | flops 17432064 | bytes 8792064 | tf_op jit(solution)/shard_map/bgrd,btgd->bgrt/dot_general | solution.py:47
  45.9 0.8 copy-done.1
  46.7 14.5 %pmax.7 = f32[128,2,2]{2,1,0:T(2,128)S(1)} all-reduce(f32[128,2,2]{2,1,0:T(2,128)S(1)} %get-tuple-element.15), channel_id=1, replica_groups=mesh['dp'=2,'tp'=4,'sp'=4] {'sp'}, use_global_device_ids=true, to_apply=%region_2.3 | all-reduce | flops 512 | bytes 4096 | tf_op jit(solution)/shard_map/pmax | solution.py:55
  61.2 0.8 fusion.28
  62.0 0.1 multiply_bitcast_fusion
  62.2 1.7 copy.25
  63.8 4.7 %fusion.8 = f32[128,2,2,256]{3,2,1,0:T(2,128)S(1)} fusion(bf16[128,64,2,256]{3,2,1,0:T(2,128)(2,1)} %get-tuple-element.9, f32[128,2,2]{2,1,0:T(2,128)S(1)} %get-tuple-element.4, f32[128,2,2,64]{3,2,1,0:T(2,128)S(1)} %get-tuple-element.16, pred[128,64]{1,0:T(8,128)(4,1)S(1)} %get-tuple-element.11, f32[128,2,2]{2,1,0:T(2,128)S(1)} %get-tuple-element.15), kind=kOutput, calls=%fused_computation.15 | convolution fusion | flops 17006592 | bytes 9056256 | tf_op jit(solution)/shard_map/bgrt,btgd->bgrd/dot_general | solution.py:54
  68.5 1.3 pad_maximum_fusion
  69.8 0.0 all-reduce.3.cloned.1.call-update
  69.8 0.2 all-reduce.5.cloned.1.call-start
  70.0 35.1 %all-reduce.3.cloned.1.call-done = f32[128,2,2,257]{3,2,1,0:T(2,128)} async-done(((f32[128,2,2,257]{3,2,1,0:T(2,128)}), f32[128,2,2,257]{3,2,1,0:T(2,128)}) %all-reduce.3.cloned.1.call-update) | async-done | bytes 526352 | tf_op jit(solution)/shard_map/psum | solution.py:58
  105.2 1.0 slice.29
  106.1 1.7 copy.30
  107.8 1.4 fusion.23
  109.2 0.2 convert_element_type.46
  109.4 0.0 copy-start.2
  109.4 5.7 %fusion.37 = f32[128,3840]{1,0:T(8,128)} fusion(bf16[128,1024]{1,0:T(8,128)(2,1)S(1)} %convert_element_type.46, bf16[1024,3840]{1,0:T(8,128)(2,1)} %param.16), kind=kOutput, calls=%fused_computation.51 | convolution fusion | flops 1006632960 | bytes 10092544 | tf_op jit(solution)/shard_map/dot_general | solution.py:60
  115.1 0.0 all-reduce.5.cloned.1.call-update
  115.1 0.0 copy-done.2
  115.1 81.5 %all-reduce.5.cloned.1.call-done = f32[128,3840]{1,0:T(8,128)} async-done(((f32[128,3840]{1,0:T(8,128)}), f32[128,3840]{1,0:T(8,128)}) %all-reduce.5.cloned.1.call-update) | async-done | bytes 1966096 | tf_op jit(solution)/shard_map/psum | solution.py:61
  196.6 1.8 multiply_reduce_fusion
  198.4 2.9 %fusion.7 = bf16[128,3840]{1,0:T(8,128)(2,1)} fusion(bf16[128,3840]{1,0:T(8,128)(2,1)S(1)} %copy-done, f32[128,3840]{1,0:T(8,128)} %all-reduce.5.cloned.1.call-done, f32[3840]{0:T(1024)S(1)} %broadcast_add_fusion, f32[128]{0:T(128)S(1)} %add_rsqrt_fusion), kind=kLoop, calls=%fused_computation.12 | loop fusion | flops 2457600 | bytes 3948032 | tf_op jit(solution)/shard_map/convert_element_type | solution.py:62
  (7 shorter events, 0.1 us)
Async XLA Ops:
  7.2 5.7 %copy-start = (bf16[128,3840]{1,0:T(8,128)(2,1)S(1)}, bf16[128,3840]{1,0:T(8,128)(2,1)}, u32[]{:S(2)}) copy-start(bf16[128,3840]{1,0:T(8,128)(2,1)} %param.10) | copy-start | bytes 2949124
  7.2 5.7 %copy-start.3 = (s32[128]{0:T(128)S(1)}, s32[128]{0:T(128)}, u32[]{:S(2)}) copy-start(s32[128]{0:T(128)} %param.11) | copy-start | bytes 1540
  7.2 98.0 %all-reduce.3.cloned.1.call-start = ((), (), s32[]{:S(2)}) async-start(), calls=%async_computation | async-start | bytes 1572864 | tf_op jit(solution)/shard_map/psum | solution.py:58
  43.3 3.4 %copy-start.1 = (bf16[128,64,2,256]{3,2,1,0:T(2,128)(2,1)}, bf16[128,64,2,256]{3,2,1,0:T(2,128)(2,1)S(1)}, u32[]{:S(2)}) copy-start(bf16[128,64,2,256]{3,2,1,0:T(2,128)(2,1)S(1)} %get-tuple-element.10) | copy-start | bytes 25165828
  69.8 126.8 %all-reduce.5.cloned.1.call-start = ((), (), s32[]{:S(2)}) async-start(), calls=%async_computation.1 | async-start | bytes 3932160 | tf_op jit(solution)/shard_map/psum | solution.py:61
  109.4 5.8 %copy-start.2 = (f32[3840]{0:T(1024)S(1)}, f32[3840]{0:T(1024)}, u32[]{:S(2)}) copy-start(f32[3840]{0:T(1024)} %param.17) | copy-start | bytes 46084
Sparse Core Ops, SparseCore 0:
  69.9 35.2 all-reduce.2
  115.2 81.3 all-reduce.4
where the time goes:
time: 209 us; the launch traced here: 208 us
  waiting for transfers between devices  117 us (56%)
  other arithmetic  33.1 us (16%)
  matrix products  23.4 us (11%)
  blocking collectives  14.5 us (7%)
  between operations  14.3 us (7%)
  local copies, waits for them, and re-layouts  5.97 us (3%)
    psum x1, waiting for transfers between devices, local_step(): proj_sum = lax.psum(proj_part, 'tp')  81.5 us
    psum x1, waiting for transfers between devices, local_step(): merged = lax.psum(packed, 'sp')  35.1 us
    select_n x1, other arithmetic, local_step(): v_out = jnp.where(slot_hit, v_new[:, None], v_cache)  21.6 us
    pmax x1, blocking collectives, local_step(): global_max = lax.pmax(block_max, 'sp')  14.5 us
    dot_general x1, matrix products, local_step(): jnp.dot(attn_out.astype(jnp.bfloat16), w_o, preferred_element_type=jnp.fl...  5.72 us
    dot_general x1, matrix products, local_step(): jnp.einsum('bgrt,btgd->bgrd', exp_w.astype(jnp.bfloat16), v_out, preferre...  4.65 us
    dot_general x1, matrix products, local_step(): q_proj = jnp.dot(normed, w_q, preferred_element_type=jnp.float32)  4.46 us
  transfers between devices with their start and end apart: 2, of which 2 were waited for; matrix products, arithmetic and copies ran while one was open for 0% of the time, Pallas kernels for 0%

commit v1 on v0

v1 whole, which is shorter than its diff:
```python
import functools

import jax
import jax.numpy as jnp
from jax import lax
from jax.experimental import pallas as pl
from jax.experimental.pallas import tpu as pltpu
from jax.sharding import PartitionSpec as P

SOFT_CAP = 50.0
ROPE_BASE = 10000.0
NORM_EPS = 1e-6

ROWS = 128
DM = 3840
HD = 256
TB = 64
RP = 136
LANES = 128
BCH = 16
NCH = ROWS // BCH
SHIFT = 20.0
CW = 256
NC = DM // CW
OWN = 32
MESH = pl.DeviceIdType.MESH


def rope_tables(positions):
    half = HD // 2
    inv_freq = ROPE_BASE ** (-2.0 * jnp.arange(half, dtype=jnp.float32) / (2 * half))
    ang = positions.astype(jnp.float32)[:, None] * inv_freq[None, :]
    return jnp.cos(ang), jnp.sin(ang)


def attn_kernel(pos_ref, x_h, cos_ref, sin_ref, wpre_ref, wq_h, wk_h, wv_h, kc_h, vc_h,
                o_ref, ko_h, vo_h,
                x_buf, a_buf, w_buf, kbuf, vbuf, qs, ks, vs,
                x_sem, w_sem, ki_sem, vi_sem, kw_sem, vw_sem):
    sp = lax.axis_index('sp')
    tbase = sp * TB

    def w_copy(i):
        if i < 2:
            src = wk_h.at[:, pl.ds(i * HD, HD)]
        elif i < 4:
            src = wv_h.at[:, pl.ds((i - 2) * HD, HD)]
        else:
            src = wq_h.at[:, pl.ds((i - 4) * HD, HD)]
        return pltpu.make_async_copy(src, w_buf.at[i], w_sem.at[i])

    def k_in(i):
        return pltpu.make_async_copy(kc_h.at[pl.ds(i * BCH, BCH)], kbuf.at[pl.ds(i * BCH, BCH)], ki_sem.at[i])

    def v_in(i):
        return pltpu.make_async_copy(vc_h.at[pl.ds(i * BCH, BCH)], vbuf.at[pl.ds(i * BCH, BCH)], vi_sem.at[i])

    def k_out(i):
        return pltpu.make_async_copy(kbuf.at[pl.ds(i * BCH, BCH)], ko_h.at[pl.ds(i * BCH, BCH)], kw_sem.at[i])

    def v_out(i):
        return pltpu.make_async_copy(vbuf.at[pl.ds(i * BCH, BCH)], vo_h.at[pl.ds(i * BCH, BCH)], vw_sem.at[i])

    x_copy = pltpu.make_async_copy(x_h, x_buf, x_sem)
    x_copy.start()
    ahead = 5
    for i in range(ahead):
        w_copy(i).start()
    x_copy.wait()

    gain = 1.0 + wpre_ref[...]

    def norm_rows(i, carry):
        r = pl.multiple_of(i * 16, 16)
        xb = x_buf[pl.ds(r, 16), :].astype(jnp.float32)
        ms = jnp.mean(xb * xb, axis=-1, keepdims=True)
        a_buf[pl.ds(r, 16), :] = (xb * lax.rsqrt(ms + NORM_EPS) * gain).astype(jnp.bfloat16)
        return carry

    lax.fori_loop(0, ROWS // 16, norm_rows, 0)

    for i in range(8):
        w_copy(i).wait()
        if i + ahead < 8:
            w_copy(i + ahead).start()
        else:
            c = i + ahead - 8
            k_in(c).start()
            v_in(c).start()
        y = jnp.dot(a_buf[...], w_buf[i], preferred_element_type=jnp.float32)
        lo, hi = y[:, :LANES], y[:, LANES:]
        if 2 <= i < 4:
            h = i - 2
            for rep in range(2):
                vs[pl.ds((rep * 4 + h) * RP, ROWS), :] = lo
                vs[pl.ds((rep * 4 + 2 + h) * RP, ROWS), :] = hi
        else:
            cos_t, sin_t = cos_ref[...], sin_ref[...]
            rlo = lo * cos_t - hi * sin_t
            rhi = hi * cos_t + lo * sin_t
            if i < 2:
                for rep in range(2):
                    ks[pl.ds((rep * 4 + i) * RP, ROWS), :] = rlo
                    ks[pl.ds((rep * 4 + 2 + i) * RP, ROWS), :] = rhi
            else:
                qs[pl.ds((i - 4) * RP, ROWS), :] = rlo
                qs[pl.ds((4 + i - 4) * RP, ROWS), :] = rhi
    for c in range(ahead, NCH):
        k_in(c).start()
        v_in(c).start()

    lane = lax.broadcasted_iota(jnp.int32, (8, LANES), 1)
    row = lax.broadcasted_iota(jnp.int32, (8, LANES), 0)
    row_c = row // 4
    row_h = (row // 2) % 2
    match = (((lane // 2) % 2) == row_c) & ((lane % 2) == row_h)
    match_f = jnp.where(match, 1.0, 0.0).astype(jnp.float32)
    first = row_c == 0
    t_half = [jnp.where(match, lane // 4 + 32 * hf, 1 << 20) for hf in range(2)]
    quad = lax.broadcasted_iota(jnp.int32, (16, LANES), 0) // 4
    zero = jnp.zeros((8, LANES), jnp.float32)

    def chunk(i, l_acc):
        k_in(i).wait()
        v_in(i).wait()
        tls = []
        for u in range(BCH):
            b = i * BCH + u
            tl = pos_ref[b] - tbase
            tls.append(tl)
            hit = jnp.logical_and(tl >= 0, tl < TB)
            tc = jnp.clip(tl, 0, TB - 1)
            tile = tc // 4
            tgt = jnp.where(hit, tc - tile * 4, -1)
            sel = quad == tgt
            off = pl.multiple_of(tile * 16, 16)
            kn = ks[pl.ds(b, 8, stride=RP), :]
            vn = vs[pl.ds(b, 8, stride=RP), :]
            kt = kbuf[b, pl.ds(off, 16), :].astype(jnp.float32)
            vt = vbuf[b, pl.ds(off, 16), :].astype(jnp.float32)
            kbuf[b, pl.ds(off, 16), :] = jnp.where(sel, jnp.concatenate([kn, kn], 0), kt).astype(jnp.bfloat16)
            vbuf[b, pl.ds(off, 16), :] = jnp.where(sel, jnp.concatenate([vn, vn], 0), vt).astype(jnp.bfloat16)
        scores = []
        for u in range(0, BCH, 2):
            b = i * BCH + u
            q0 = qs[pl.ds(b, 8, stride=RP), :]
            q1 = qs[pl.ds(b + 1, 8, stride=RP), :]
            lhs = jnp.concatenate([jnp.concatenate([q0, zero], 1), jnp.concatenate([zero, q1], 1)], 0).astype(jnp.bfloat16)
            kk = jnp.concatenate([kbuf[b], kbuf[b + 1]], 1)
            scores.append(lax.dot_general(lhs, kk, (((1,), (1,)), ((), ())), preferred_element_type=jnp.float32))
        weights = []
        for u in range(0, BCH, 2):
            pair = []
            for w in range(2):
                part = scores[u // 2][8 * w:8 * w + 8]
                es = []
                for hf in range(2):
                    a = part[:, hf * LANES:(hf + 1) * LANES] * match_f
                    e = pltpu.roll(a, 4, 0)
                    f = jnp.where(first, pltpu.roll(e, LANES - 2, 1), pltpu.roll(e, 2, 1))
                    s = SOFT_CAP * jnp.tanh((a + f) * (HD ** -0.5 / SOFT_CAP))
                    es.append(jnp.where(t_half[hf] <= tls[u + w], jnp.exp(s - SHIFT), 0.0))
                tot = jnp.sum(es[0] + es[1], axis=1, keepdims=True)
                inv = jnp.where(tot > 0.0, 1.0 / tot, 0.0)
                pair.append(jnp.concatenate([es[0] * inv, es[1] * inv], 1))
                l_acc = jnp.where(lane == i * BCH + u + w, tot, l_acc)
            weights.append(jnp.concatenate(pair, 0).astype(jnp.bfloat16))
        for u in range(0, BCH, 2):
            b = i * BCH + u
            vv = jnp.concatenate([vbuf[b], vbuf[b + 1]], 1)
            o = jnp.dot(weights[u // 2], vv, preferred_element_type=jnp.float32)
            o_ref[pl.ds(b, 8, stride=RP), :] = o[0:8, 0:LANES]
            o_ref[pl.ds(b + 1, 8, stride=RP), :] = o[8:16, LANES:]
        k_out(i).start()
        v_out(i).start()
        return l_acc

    l_acc = lax.fori_loop(0, NCH, chunk, zero)
    l_full = jnp.concatenate([l_acc, jnp.zeros((ROWS - 8, LANES), jnp.float32)], 0)
    o_ref[pl.ds(8 * RP, ROWS), :] = l_full.T
    for i in range(NCH):
        k_out(i).wait()
        v_out(i).wait()


def comm_kernel(x_ref, wpost_ref, o_ref, wo_h, out_ref,
                wo_buf, r1, m1, r2, lhs, p_buf, rr, rl, sr, sl, s_all,
                w_sem, r1_send, r1_recv, r2_send, r2_recv,
                right_send, right_recv, left_send, left_recv,
                part_send, part_recv, y_send, y_recv, f_send, f_recv):
    z = lax.axis_index('tp')
    sp = lax.axis_index('sp')
    core = sp % 2
    yy = sp // 2
    partner = sp + 1 - 2 * core
    ypeer = (sp + 2) % 4
    diag = 3 - sp

    def wo_copy(k):
        return pltpu.make_async_copy(wo_h.at[:, pl.ds(pl.multiple_of(k * CW, CW), CW)], wo_buf.at[k], w_sem.at[k])

    for k in range(NC):
        wo_copy(k).start()

    @pl.when(z == 0)
    def _():
        rr[...] = jnp.zeros_like(rr)

    @pl.when(z == 3)
    def _():
        rl[...] = jnp.zeros_like(rl)

    bar = pltpu.get_barrier_semaphore()
    pl.semaphore_signal(bar, inc=1, device_id={'sp': partner}, device_id_type=MESH)
    pl.semaphore_signal(bar, inc=1, device_id={'sp': ypeer}, device_id_type=MESH)

    @pl.when(z > 0)
    def _():
        pl.semaphore_signal(bar, inc=1, device_id={'tp': z - 1}, device_id_type=MESH)

    @pl.when(z < 3)
    def _():
        pl.semaphore_signal(bar, inc=1, device_id={'tp': z + 1}, device_id_type=MESH)

    pl.semaphore_wait(bar, 3 + (z * (3 - z)) // 2)

    def to_partner(slot):
        ychip = (1 - yy) if slot == 0 else yy
        r0 = pl.multiple_of(ychip * 64 + (1 - core) * OWN, OWN)
        return pltpu.make_async_remote_copy(
            src_ref=o_ref.at[:, pl.ds(r0, OWN), :], dst_ref=r1.at[slot],
            send_sem=r1_send.at[slot], recv_sem=r1_recv.at[slot], device_id={'sp': partner}, device_id_type=MESH)

    to_partner(0).start()
    to_partner(1).start()

    def merge(load_a, load_b, write):
        la, lb = load_a(8), load_b(8)
        tot = la + lb
        inv = jnp.where(tot > 0.0, 1.0 / tot, 0.0)
        fa, fb = la * inv, lb * inv
        for j in range(8):
            write(j, load_a(j) * fa[:, j:j + 1] + load_b(j) * fb[:, j:j + 1])
        write(8, tot)

    def own_rows(ychip):
        r0 = pl.multiple_of(ychip * 64 + core * OWN, OWN)
        return lambda j: o_ref[j, pl.ds(r0, OWN), :]

    def put_m1(j, val):
        m1[j] = val

    to_partner(0).wait()
    merge(own_rows(1 - yy), lambda j: r1[0, j], put_m1)
    y_merge = pltpu.make_async_remote_copy(
        src_ref=m1, dst_ref=r2, send_sem=r2_send, recv_sem=r2_recv, device_id={'sp': ypeer}, device_id_type=MESH)
    y_merge.start()
    to_partner(1).wait()

    def put_r1(j, val):
        r1[1, j] = val

    merge(own_rows(yy), lambda j: r1[1, j], put_r1)
    y_merge.wait()

    def put_lhs(j, val):
        if j < 8:
            c, hq = j // 4, j % 4
            lhs[:, (hq * 2 + c) * LANES:(hq * 2 + c + 1) * LANES] = val.astype(jnp.bfloat16)

    merge(lambda j: r1[1, j], lambda j: r2[j], put_lhs)

    def right_copy(k):
        return pltpu.make_async_remote_copy(
            src_ref=sr.at[k], dst_ref=rr.at[k], send_sem=right_send.at[k], recv_sem=right_recv.at[k],
            device_id={'tp': z + 1}, device_id_type=MESH)

    def left_copy(k):
        return pltpu.make_async_remote_copy(
            src_ref=sl.at[k], dst_ref=rl.at[k], send_sem=left_send.at[k], recv_sem=left_recv.at[k],
            device_id={'tp': z - 1}, device_id_type=MESH)

    def part_copy(k):
        return pltpu.make_async_remote_copy(
            src_ref=s_all.at[sp, k], dst_ref=s_all.at[sp, k], send_sem=part_send.at[k], recv_sem=part_recv.at[k],
            device_id={'sp': partner}, device_id_type=MESH)

    def y_copy(k):
        return pltpu.make_async_remote_copy(
            src_ref=s_all.at[sp, k], dst_ref=s_all.at[sp, k], send_sem=y_send.at[k], recv_sem=y_recv.at[k],
            device_id={'sp': ypeer}, device_id_type=MESH)

    def fwd_copy(k):
        return pltpu.make_async_remote_copy(
            src_ref=s_all.at[ypeer, k], dst_ref=s_all.at[ypeer, k], send_sem=f_send.at[k], recv_sem=f_recv.at[k],
            device_id={'sp': partner}, device_id_type=MESH)

    hop = 3
    lag_r = hop * z
    lag_l = hop * (3 - z)
    lag_s = hop * (3 - (z * (3 - z)) // 2)

    def tick(i, carry):
        @pl.when(i < NC)
        def _():
            wo_copy(i).wait()
            p_buf[i] = jnp.dot(lhs[...], wo_buf[i], preferred_element_type=jnp.float32)

        kr = i - lag_r

        @pl.when(jnp.logical_and(kr >= 0, kr < NC))
        def _():
            @pl.when(z > 0)
            def _():
                right_copy(kr).wait_recv()

            @pl.when(z < 3)
            def _():
                sr[kr] = p_buf[kr] + rr[kr]
                right_copy(kr).start()

        kl = i - lag_l

        @pl.when(jnp.logical_and(kl >= 0, kl < NC))
        def _():
            @pl.when(z < 3)
            def _():
                left_copy(kl).wait_recv()

            @pl.when(z > 0)
            def _():
                sl[kl] = p_buf[kl] + rl[kl]
                left_copy(kl).start()

        k_s = i - lag_s

        @pl.when(jnp.logical_and(k_s >= 0, k_s < NC))
        def _():
            s_all[sp, k_s] = p_buf[k_s] + rr[k_s] + rl[k_s]
            y_copy(k_s).start()
            part_copy(k_s).start()

        k_y = i - lag_s - hop

        @pl.when(jnp.logical_and(k_y >= 0, k_y < NC))
        def _():
            y_copy(k_y).wait_recv()
            fwd_copy(k_y).start()

        return carry

    lax.fori_loop(0, NC + 4 * hop, tick, 0)

    def drain(k, carry):
        part_copy(k).wait()
        y_copy(k).wait_send()
        fwd_copy(k).wait()

        @pl.when(z < 3)
        def _():
            right_copy(k).wait_send()

        @pl.when(z > 0)
        def _():
            left_copy(k).wait_send()

        return carry

    lax.fori_loop(0, NC, drain, 0)

    def finish(i, carry):
        g = i // 2
        r = pl.multiple_of((i % 2) * 16, 16)
        parts = [s_all[g, k, pl.ds(r, 16), :] for k in range(NC)]
        sq = parts[0] * parts[0]
        for k in range(1, NC):
            sq = sq + parts[k] * parts[k]
        ms = jnp.sum(sq, axis=-1, keepdims=True) * (1.0 / DM)
        rs = lax.rsqrt(ms + NORM_EPS)
        r16 = pl.multiple_of(i * 16, 16)
        for k in range(NC):
            cs = slice(k * CW, (k + 1) * CW)
            val = s_all[g, k, pl.ds(r, 16), :] * rs * (1.0 + wpost_ref[:, cs])
            out_ref[pl.ds(r16, 16), cs] = (x_ref[pl.ds(r16, 16), cs].astype(jnp.float32) + val).astype(jnp.bfloat16)
        return carry

    lax.fori_loop(0, ROWS // 16, finish, 0)


def solution(mesh):
    cache_spec = P('dp', 'sp', 'tp', None)
    hbm = pl.BlockSpec(memory_space=pltpu.HBM)
    vmem = pl.BlockSpec(memory_space=pltpu.VMEM)
    smem = pl.BlockSpec(memory_space=pltpu.SMEM)

    def in_hbm(arr):
        return pltpu.with_memory_space_constraint(arr, pltpu.HBM)

    def to_rows(c):
        b, t, h, d = c.shape
        return c.reshape(b, t, h, 2, LANES).transpose(0, 1, 3, 2, 4).reshape(b, t * 2 * h, LANES)

    def from_rows(r):
        return r.reshape(ROWS, TB, 2, 2, LANES).transpose(0, 1, 3, 2, 4).reshape(ROWS, TB, 2, HD)

    def local_step(x_in, cur_pos, w_pre, w_q, w_k, w_v, w_o, w_post, k_cache, v_cache):
        cos_t, sin_t = rope_tables(cur_pos)
        kr, vr = to_rows(k_cache), to_rows(v_cache)
        f32, bf16 = jnp.float32, jnp.bfloat16
        o_part, k_new, v_new = pl.pallas_call(
            attn_kernel,
            out_shape=(jax.ShapeDtypeStruct((9 * RP, LANES), f32),
                       jax.ShapeDtypeStruct(kr.shape, bf16), jax.ShapeDtypeStruct(vr.shape, bf16)),
            in_specs=[smem, hbm, vmem, vmem, vmem, hbm, hbm, hbm, hbm, hbm],
            out_specs=(vmem, hbm, hbm),
            scratch_shapes=[
                pltpu.VMEM((ROWS, DM), bf16), pltpu.VMEM((ROWS, DM), bf16), pltpu.VMEM((8, DM, HD), bf16),
                pltpu.VMEM(kr.shape, bf16), pltpu.VMEM(vr.shape, bf16),
                pltpu.VMEM((8 * RP, LANES), f32), pltpu.VMEM((8 * RP, LANES), f32), pltpu.VMEM((8 * RP, LANES), f32),
                pltpu.SemaphoreType.DMA, pltpu.SemaphoreType.DMA((8,)),
                pltpu.SemaphoreType.DMA((NCH,)), pltpu.SemaphoreType.DMA((NCH,)),
                pltpu.SemaphoreType.DMA((NCH,)), pltpu.SemaphoreType.DMA((NCH,)),
            ],
            compiler_params=pltpu.CompilerParams(vmem_limit_bytes=56 << 20),
            name='attend',
        )(cur_pos, in_hbm(x_in), cos_t, sin_t, w_pre.reshape(1, DM), in_hbm(w_q), in_hbm(w_k), in_hbm(w_v),
          in_hbm(kr), in_hbm(vr))
        dma = pltpu.SemaphoreType.DMA
        big = pltpu.VMEM((NC, OWN, CW), f32)
        x_out = pl.pallas_call(
            comm_kernel,
            out_shape=jax.ShapeDtypeStruct((ROWS, DM), bf16),
            in_specs=[vmem, vmem, vmem, hbm],
            out_specs=vmem,
            scratch_shapes=[
                pltpu.VMEM((NC, 1024, CW), bf16), pltpu.VMEM((2, 9, OWN, LANES), f32), pltpu.VMEM((9, OWN, LANES), f32),
                pltpu.VMEM((9, OWN, LANES), f32), pltpu.VMEM((OWN, 1024), bf16),
                big, big, big, big, big, pltpu.VMEM((4, NC, OWN, CW), f32),
                dma((NC,)), dma((2,)), dma((2,)), dma, dma,
                dma((NC,)), dma((NC,)), dma((NC,)), dma((NC,)),
                dma((NC,)), dma((NC,)), dma((NC,)), dma((NC,)), dma((NC,)), dma((NC,)),
            ],
            compiler_params=pltpu.CompilerParams(vmem_limit_bytes=40 << 20, collective_id=0, has_side_effects=True),
            name='combine',
        )(x_in, w_post.reshape(1, DM), o_part.reshape(9, RP, LANES), in_hbm(w_o))
        return x_out, from_rows(k_new), from_rows(v_new)

    return jax.shard_map(local_step, mesh=mesh,
                         in_specs=(P('dp', None), P('dp'), P(None), P(None, 'tp'), P(None, 'tp'), P(None, 'tp'), P('tp', None), P(None), cache_spec, cache_spec),
                         out_specs=(P('dp', None), cache_spec, cache_spec), check_vma=False)
```

time: 209 us -> 66.9 us (0.32)
  waiting for transfers between devices: 117 us -> 0 us
  Pallas kernels: 0 us -> 60.2 us
  other arithmetic: 33.1 us -> 1.63 us
  matrix products: 23.4 us -> 0 us
  blocking collectives: 14.5 us -> 0 us
  between operations: 14.3 us -> 0.67 us
    psum x2 -> x0, waiting for transfers between devices: 117 us -> none  [the longest x1 81.5 us: local_step(): proj_sum = lax.psum(proj_part, 'tp')]
    pallas_call x0 -> x2, Pallas kernels: none -> 60.2 us  [the longest x1 40.1 us: local_step(): pl.pallas_call(comm_kernel, out_shape=jax.ShapeDtypeStruct((ROWS, DM), bf...]
    dot_general x6 -> x0, matrix products: 23.4 us -> none  [the longest x1 5.72 us: local_step(): jnp.dot(attn_out.astype(jnp.bfloat16), w_o, preferred_element_type=jnp.fl...]
    select_n x1 -> x0, other arithmetic: 21.6 us -> none  [local_step(): v_out = jnp.where(slot_hit, v_new[:, None], v_cache)]
    pmax x1 -> x0, blocking collectives: 14.5 us -> none  [local_step(): global_max = lax.pmax(block_max, 'sp')]
    reduce_sum x3 -> x0, other arithmetic: 4.05 us -> none  [the longest x2 3.24 us: rms_scale(): mean_sq = jnp.mean(tensor * tensor, axis=-1, keepdims=True)]
    convert_element_type x3 -> x1, other arithmetic: 4.24 us -> 0.66 us  [rope_tables(): ang = positions.astype(jnp.float32)[:, None] * inv_freq[None, :]]
  transfers between devices with their start and end apart: 2 -> 0, of which waited for: 2 -> 0; matrix products, arithmetic and copies ran while one was open for 0% -> 0% of each run, Pallas kernels for 0% -> 0%
where the time goes in v1:
time: 66.9 us; the launch traced here: 66.5 us
  Pallas kernels  60.2 us (90%)
  local copies, waits for them, and re-layouts  4.08 us (6%)
  other arithmetic  1.63 us (2%)
  between operations  0.67 us (1%)
    pallas_call x1, Pallas kernels, local_step(): pl.pallas_call(comm_kernel, out_shape=jax.ShapeDtypeStruct((ROWS, DM), bf...  40.1 us
    pallas_call x1, Pallas kernels, local_step(): pl.pallas_call(attn_kernel, out_shape=(jax.ShapeDtypeStruct((9 * RP, LANE...  20 us
    unnamed x5, local copies, waits for them, and re-layouts  2.02 us

profile of v1, /device:TPU:0, one launch (start us, length us, event | category | flops | bytes accessed | tf_op | source)
XLA Modules:
  0.0 66.5 jit_solution(5445117621458332288)
XLA Ops:
  0.6 0.7 convert_element_type.3
  1.3 1.3 %reshape.46.wpre_ref = f32[1,3840]{1,0:T(1,128)} reshape(f32[3840]{0:T(1024)} %param.12) | data formatting | bytes 30720 | tf_op jit(solution)/shard_map/reshape | solution.py:426
  2.6 0.7 %reshape.45.wpost_ref = f32[1,3840]{1,0:T(1,128)S(1)} reshape(f32[3840]{0:T(1024)} %param.17) | data formatting | bytes 30720 | tf_op jit(solution)/shard_map/reshape | solution.py:445
  3.4 1.0 %multiply_sine_fusion = (f32[128,128]{1,0:T(8,128)}, f32[128,128]{1,0:T(8,128)}) fusion(f32[128]{0:T(128)S(1)} %multiply_power_fusion, f32[128]{0:T(128)S(1)} %convert_element_type.3), kind=kLoop, calls=%fused_computation | loop fusion | flops 16384 | bytes 132096 | tf_op jit(solution)/shard_map/sin | solution.py:33
  4.3 0.0 copy-start
  4.3 20.0 %attend.1 = (f32[1224,128]{1,0:T(8,128)}, bf16[128,256,128]{2,1,0:T(8,128)(2,1)}, bf16[128,256,128]{2,1,0:T(8,128)(2,1)}) custom-call(s32[128]{0:T(128)} %pos_ref.1, bf16[128,3840]{1,0:T(8,128)(2,1)} %x_ref.1, f32[128,128]{1,0:T(8,128)} %get-tuple-element.10.cos_ref, f32[128,128]{1,0:T(8,128)} %get-tuple-element.9.sin_ref, f32[1,3840]{1,0:T(1,128)} %reshape.46.wpre_ref, ...), custom_call_target="tpu_custom_call" | custom-call | tf_op jit(solution)/shard_map/attend/pallas_call | solution.py:410
  24.4 0.0 copy-done
  24.4 0.0 copy-start.1
  24.4 1.1 %copy-done.1 = f32[1224,128]{1,0:T(8,128)S(1)} copy-done((f32[1224,128]{1,0:T(8,128)S(1)}, f32[1224,128]{1,0:T(8,128)}, u32[]{:S(2)}) %copy-start.1) | copy-done | bytes 626712
  25.5 40.1 %combine.1 = bf16[128,3840]{1,0:T(8,128)(2,1)S(1)} custom-call(bf16[128,3840]{1,0:T(8,128)(2,1)S(1)} %copy-done, f32[1,3840]{1,0:T(1,128)S(1)} %reshape.45.wpost_ref, f32[9,136,128]{2,1,0:T(8,128)S(1)} %bitcast.21, bf16[1024,3840]{1,0:T(8,128)(2,1)} %wo_h.1), custom_call_target="tpu_custom_call" | custom-call | tf_op jit(solution)/shard_map/combine/pallas_call | solution.py:430
  65.6 0.9 %copy.18 = bf16[128,3840]{1,0:T(8,128)(2,1)} copy(bf16[128,3840]{1,0:T(8,128)(2,1)S(1)} %combine.1) | data formatting | bytes 1966080
  (1 shorter events, 0.0 us)
Async XLA Ops:
  4.3 20.1 %copy-start = (bf16[128,3840]{1,0:T(8,128)(2,1)S(1)}, bf16[128,3840]{1,0:T(8,128)(2,1)}, u32[]{:S(2)}) copy-start(bf16[128,3840]{1,0:T(8,128)(2,1)} %x_ref.1) | copy-start | bytes 2949124
  24.4 1.1 %copy-start.1 = (f32[1224,128]{1,0:T(8,128)S(1)}, f32[1224,128]{1,0:T(8,128)}, u32[]{:S(2)}) copy-start(f32[1224,128]{1,0:T(8,128)} %get-tuple-element.6) | copy-start | bytes 1880068

commit v2 on v1

--- a/solution.py
+++ b/solution.py
@@ -26,17 +26,11 @@
 MESH = pl.DeviceIdType.MESH
 
 
-def rope_tables(positions):
-    half = HD // 2
-    inv_freq = ROPE_BASE ** (-2.0 * jnp.arange(half, dtype=jnp.float32) / (2 * half))
-    ang = positions.astype(jnp.float32)[:, None] * inv_freq[None, :]
-    return jnp.cos(ang), jnp.sin(ang)
-
-
-def attn_kernel(pos_ref, x_h, cos_ref, sin_ref, wpre_ref, wq_h, wk_h, wv_h, kc_h, vc_h,
+def attn_kernel(pos_h, posv_h, freq_h, x_h, wpre_h, wq_h, wk_h, wv_h, kc_h, vc_h,
                 o_ref, ko_h, vo_h,
+                pos_ref, posv, freq, wpre_ref, cos_ref, sin_ref,
                 x_buf, a_buf, w_buf, kbuf, vbuf, qs, ks, vs,
-                x_sem, w_sem, ki_sem, vi_sem, kw_sem, vw_sem):
+                x_sem, s_sem, w_sem, ki_sem, vi_sem, kw_sem, vw_sem):
     sp = lax.axis_index('sp')
     tbase = sp * TB
 
@@ -63,12 +57,23 @@
 
     x_copy = pltpu.make_async_copy(x_h, x_buf, x_sem)
     x_copy.start()
+    small = [pltpu.make_async_copy(a, b, s_sem.at[i]) for i, (a, b) in enumerate(
+        ((wpre_h, wpre_ref), (posv_h, posv), (freq_h, freq), (pos_h, pos_ref)))]
+    for c in small:
+        c.start()
     ahead = 5
     for i in range(ahead):
         w_copy(i).start()
+    for c in small[1:]:
+        c.wait()
+    pos_col = jnp.broadcast_to(posv[...].astype(jnp.float32), (ROWS, LANES)).T
+    ang = pos_col * freq[...]
+    cos_ref[...] = jnp.cos(ang)
+    sin_ref[...] = jnp.sin(ang)
+    small[0].wait()
     x_copy.wait()
 
-    gain = 1.0 + wpre_ref[...]
+    gain = 1.0 + jnp.concatenate([wpre_ref[k:k + 1, :] for k in range(DM // LANES)], 1)
 
     def norm_rows(i, carry):
         r = pl.multiple_of(i * 16, 16)
@@ -183,8 +188,8 @@
         v_out(i).wait()
 
 
-def comm_kernel(x_ref, wpost_ref, o_ref, wo_h, out_ref,
-                wo_buf, r1, m1, r2, lhs, p_buf, rr, rl, sr, sl, s_all,
+def comm_kernel(o_ref, wo_h, s_all,
+                wo_buf, r1, m1, r2, lhs, p_buf, rr, rl, sr, sl,
                 w_sem, r1_send, r1_recv, r2_send, r2_recv,
                 right_send, right_recv, left_send, left_recv,
                 part_send, part_recv, y_send, y_recv, f_send, f_recv):
@@ -368,30 +373,37 @@
 
     lax.fori_loop(0, NC, drain, 0)
 
-    def finish(i, carry):
-        g = i // 2
-        r = pl.multiple_of((i % 2) * 16, 16)
-        parts = [s_all[g, k, pl.ds(r, 16), :] for k in range(NC)]
+
+def finish_kernel(s_all, x_ref, wpost_ref, out_h, out_buf, sem):
+    blk = 16
+
+    def out_copy(i):
+        rows = pl.ds(i * blk, blk)
+        return pltpu.make_async_copy(out_buf.at[rows], out_h.at[rows], sem.at[i])
+
+    for i in range(ROWS // blk):
+        g, r = (i * blk) // OWN, (i * blk) % OWN
+        parts = [s_all[g, k, r:r + blk, :] for k in range(NC)]
         sq = parts[0] * parts[0]
         for k in range(1, NC):
             sq = sq + parts[k] * parts[k]
-        ms = jnp.sum(sq, axis=-1, keepdims=True) * (1.0 / DM)
-        rs = lax.rsqrt(ms + NORM_EPS)
-        r16 = pl.multiple_of(i * 16, 16)
+        rs = lax.rsqrt(jnp.sum(sq, axis=-1, keepdims=True) * (1.0 / DM) + NORM_EPS)
         for k in range(NC):
-            cs = slice(k * CW, (k + 1) * CW)
-            val = s_all[g, k, pl.ds(r, 16), :] * rs * (1.0 + wpost_ref[:, cs])
-            out_ref[pl.ds(r16, 16), cs] = (x_ref[pl.ds(r16, 16), cs].astype(jnp.float32) + val).astype(jnp.bfloat16)
-        return carry
-
-    lax.fori_loop(0, ROWS // 16, finish, 0)
+            for hf in range(CW // LANES):
+                col = k * CW + hf * LANES
+                gain = 1.0 + wpost_ref[col // LANES:col // LANES + 1, :]
+                val = s_all[g, k, r:r + blk, hf * LANES:(hf + 1) * LANES] * rs * gain
+                cs = slice(col, col + LANES)
+                out_buf[i * blk:(i + 1) * blk, cs] = (x_ref[i * blk:(i + 1) * blk, cs].astype(jnp.float32) + val).astype(jnp.bfloat16)
+        out_copy(i).start()
+    for i in range(ROWS // blk):
+        out_copy(i).wait()
 
 
 def solution(mesh):
     cache_spec = P('dp', 'sp', 'tp', None)
     hbm = pl.BlockSpec(memory_space=pltpu.HBM)
     vmem = pl.BlockSpec(memory_space=pltpu.VMEM)
-    smem = pl.BlockSpec(memory_space=pltpu.SMEM)
 
     def in_hbm(arr):
         return pltpu.with_memory_space_constraint(arr, pltpu.HBM)
@@ -404,45 +416,57 @@
         return r.reshape(ROWS, TB, 2, 2, LANES).transpose(0, 1, 3, 2, 4).reshape(ROWS, TB, 2, HD)
 
     def local_step(x_in, cur_pos, w_pre, w_q, w_k, w_v, w_o, w_post, k_cache, v_cache):
-        cos_t, sin_t = rope_tables(cur_pos)
+        half = HD // 2
+        inv_freq = ROPE_BASE ** (-2.0 * jnp.arange(half, dtype=jnp.float32) / (2 * half))
         kr, vr = to_rows(k_cache), to_rows(v_cache)
         f32, bf16 = jnp.float32, jnp.bfloat16
         o_part, k_new, v_new = pl.pallas_call(
             attn_kernel,
-            out_shape=(jax.ShapeDtypeStruct((9 * RP, LANES), f32),
+            out_shape=(pltpu.VMEM((9 * RP, LANES), f32),
                        jax.ShapeDtypeStruct(kr.shape, bf16), jax.ShapeDtypeStruct(vr.shape, bf16)),
-            in_specs=[smem, hbm, vmem, vmem, vmem, hbm, hbm, hbm, hbm, hbm],
+            in_specs=[hbm] * 10,
             out_specs=(vmem, hbm, hbm),
             scratch_shapes=[
+                pltpu.SMEM((ROWS,), jnp.int32), pltpu.VMEM((1, ROWS), jnp.int32), pltpu.VMEM((1, LANES), f32),
+                pltpu.VMEM((DM // LANES, LANES), f32), pltpu.VMEM((ROWS, LANES), f32), pltpu.VMEM((ROWS, LANES), f32),
                 pltpu.VMEM((ROWS, DM), bf16), pltpu.VMEM((ROWS, DM), bf16), pltpu.VMEM((8, DM, HD), bf16),
                 pltpu.VMEM(kr.shape, bf16), pltpu.VMEM(vr.shape, bf16),
                 pltpu.VMEM((8 * RP, LANES), f32), pltpu.VMEM((8 * RP, LANES), f32), pltpu.VMEM((8 * RP, LANES), f32),
-                pltpu.SemaphoreType.DMA, pltpu.SemaphoreType.DMA((8,)),
+                pltpu.SemaphoreType.DMA, pltpu.SemaphoreType.DMA((4,)), pltpu.SemaphoreType.DMA((8,)),
                 pltpu.SemaphoreType.DMA((NCH,)), pltpu.SemaphoreType.DMA((NCH,)),
                 pltpu.SemaphoreType.DMA((NCH,)), pltpu.SemaphoreType.DMA((NCH,)),
             ],
             compiler_params=pltpu.CompilerParams(vmem_limit_bytes=56 << 20),
             name='attend',
-        )(cur_pos, in_hbm(x_in), cos_t, sin_t, w_pre.reshape(1, DM), in_hbm(w_q), in_hbm(w_k), in_hbm(w_v),
-          in_hbm(kr), in_hbm(vr))
+        )(in_hbm(cur_pos), in_hbm(cur_pos.reshape(1, ROWS)), in_hbm(inv_freq.reshape(1, LANES)), in_hbm(x_in),
+          in_hbm(w_pre.reshape(DM // LANES, LANES)), in_hbm(w_q), in_hbm(w_k), in_hbm(w_v), in_hbm(kr), in_hbm(vr))
         dma = pltpu.SemaphoreType.DMA
         big = pltpu.VMEM((NC, OWN, CW), f32)
-        x_out = pl.pallas_call(
+        sums = pl.pallas_call(
             comm_kernel,
-            out_shape=jax.ShapeDtypeStruct((ROWS, DM), bf16),
-            in_specs=[vmem, vmem, vmem, hbm],
+            out_shape=pltpu.VMEM((4, NC, OWN, CW), f32),
+            in_specs=[vmem, hbm],
             out_specs=vmem,
             scratch_shapes=[
                 pltpu.VMEM((NC, 1024, CW), bf16), pltpu.VMEM((2, 9, OWN, LANES), f32), pltpu.VMEM((9, OWN, LANES), f32),
                 pltpu.VMEM((9, OWN, LANES), f32), pltpu.VMEM((OWN, 1024), bf16),
-                big, big, big, big, big, pltpu.VMEM((4, NC, OWN, CW), f32),
+                big, big, big, big, big,
                 dma((NC,)), dma((2,)), dma((2,)), dma, dma,
                 dma((NC,)), dma((NC,)), dma((NC,)), dma((NC,)),
                 dma((NC,)), dma((NC,)), dma((NC,)), dma((NC,)), dma((NC,)), dma((NC,)),
             ],
             compiler_params=pltpu.CompilerParams(vmem_limit_bytes=40 << 20, collective_id=0, has_side_effects=True),
             name='combine',
-        )(x_in, w_post.reshape(1, DM), o_part.reshape(9, RP, LANES), in_hbm(w_o))
+        )(pltpu.with_memory_space_constraint(o_part.reshape(9, RP, LANES), pltpu.VMEM), in_hbm(w_o))
+        x_out = pl.pallas_call(
+            finish_kernel,
+            out_shape=jax.ShapeDtypeStruct((ROWS, DM), bf16),
+            in_specs=[vmem, vmem, vmem],
+            out_specs=hbm,
+            scratch_shapes=[pltpu.VMEM((ROWS, DM), bf16), dma((ROWS // 16,))],
+            compiler_params=pltpu.CompilerParams(vmem_limit_bytes=16 << 20),
+            name='finish',
+        )(pltpu.with_memory_space_constraint(sums, pltpu.VMEM), x_in, w_post.reshape(DM // LANES, LANES))
         return x_out, from_rows(k_new), from_rows(v_new)
 
     return jax.shard_map(local_step, mesh=mesh,

time: 66.9 us -> 59.7 us (0.89)
  local copies, waits for them, and re-layouts: 4.08 us -> 0.01 us
  Pallas kernels: 60.2 us -> 58.4 us
  other arithmetic: 1.63 us -> 0.53 us
    reshape x2 -> x0, local copies, waits for them, and re-layouts: 2.06 us -> none  [the longest x1 1.33 us: local_step(): w_pre.reshape(1, DM)]
    unnamed x5 -> x4, local copies, waits for them, and re-layouts: 2.02 us -> 0.01 us
    pallas_call x2 -> x3, Pallas kernels: 60.2 us -> 58.4 us  [the longest x1 39 us: local_step(): pl.pallas_call(comm_kernel, out_shape=pltpu.VMEM((4, NC, OWN, CW), f32),...]
    sin x1 -> x0, other arithmetic: 0.96 us -> none  [rope_tables(): return (jnp.cos(ang), jnp.sin(ang))]
where the time goes in v2:
time: 59.7 us; the launch traced here: 59.6 us
  Pallas kernels  58.4 us (98%)
  between operations  0.68 us (1%)
    pallas_call x1, Pallas kernels, local_step(): pl.pallas_call(comm_kernel, out_shape=pltpu.VMEM((4, NC, OWN, CW), f32),...  39 us
    pallas_call x1, Pallas kernels, local_step(): pl.pallas_call(attn_kernel, out_shape=(pltpu.VMEM((9 * RP, LANES), f32),...  18.1 us
    pallas_call x1, Pallas kernels, local_step(): pl.pallas_call(finish_kernel, out_shape=jax.ShapeDtypeStruct((ROWS, DM),...  1.28 us

profile of v2, /device:TPU:0, one launch (start us, length us, event | category | flops | bytes accessed | tf_op | source)
XLA Modules:
  0.0 59.6 jit_solution(13471646467127581700)
XLA Ops:
  0.6 0.5 multiply_power_fusion.freq_h
  1.2 18.1 %attend.1 = (f32[1224,128]{1,0:T(8,128)S(1)}, bf16[128,256,128]{2,1,0:T(8,128)(2,1)}, bf16[128,256,128]{2,1,0:T(8,128)(2,1)}) custom-call(s32[128]{0:T(128)} %pos_h.1, s32[1,128]{1,0:T(1,128)} %bitcast.29, f32[1,128]{1,0:T(1,128)} %multiply_power_fusion.freq_h, bf16[128,3840]{1,0:T(8,128)(2,1)} %x_ref.1, f32[30,128]{1,0:T(8,128)} %bitcast.28, ...), custom_call_target="tpu_custom_call" | custom-call | tf_op jit(solution)/shard_map/attend/pallas_call | solution.py:423
  19.2 0.0 copy-start
  19.3 0.0 copy-start.1
  19.3 39.0 %combine.1.s_all = f32[4,15,32,256]{3,2,1,0:T(8,128)S(1)} custom-call(f32[9,136,128]{2,1,0:T(8,128)S(1)} %bitcast.24, bf16[1024,3840]{1,0:T(8,128)(2,1)} %wo_h.1), custom_call_target="tpu_custom_call" | custom-call | tf_op jit(solution)/shard_map/combine/pallas_call | solution.py:445
  58.3 0.0 copy-done
  58.3 0.0 copy-done.1
  58.3 1.3 %finish.1 = bf16[128,3840]{1,0:T(8,128)(2,1)} custom-call(f32[4,15,32,256]{3,2,1,0:T(8,128)S(1)} %combine.1.s_all, bf16[128,3840]{1,0:T(8,128)(2,1)S(1)} %copy-done, f32[30,128]{1,0:T(8,128)S(1)} %bitcast.25), custom_call_target="tpu_custom_call" | custom-call | tf_op jit(solution)/shard_map/finish/pallas_call | solution.py:461
Async XLA Ops:
  19.2 39.1 %copy-start = (bf16[128,3840]{1,0:T(8,128)(2,1)S(1)}, bf16[128,3840]{1,0:T(8,128)(2,1)}, u32[]{:S(2)}) copy-start(bf16[128,3840]{1,0:T(8,128)(2,1)} %x_ref.1) | copy-start | bytes 2949124
  19.3 39.1 %copy-start.1 = (f32[3840]{0:T(1024)S(1)}, f32[3840]{0:T(1024)}, u32[]{:S(2)}) copy-start(f32[3840]{0:T(1024)} %param.17) | copy-start | bytes 46084

commit v3 on v2

--- a/solution.py
+++ b/solution.py
@@ -300,7 +300,7 @@
             src_ref=s_all.at[ypeer, k], dst_ref=s_all.at[ypeer, k], send_sem=f_send.at[k], recv_sem=f_recv.at[k],
             device_id={'sp': partner}, device_id_type=MESH)
 
-    hop = 3
+    hop = 6
     lag_r = hop * z
     lag_l = hop * (3 - z)
     lag_s = hop * (3 - (z * (3 - z)) // 2)

time: 59.7 us -> 55.8 us (0.935)
  Pallas kernels: 58.4 us -> 54.4 us
    pallas_call x1, Pallas kernels: 39 us -> 35 us  [local_step(): pl.pallas_call(comm_kernel, out_shape=pltpu.VMEM((4, NC, OWN, CW), f32),...]
where the time goes in v3:
time: 55.8 us; the launch traced here: 55.6 us
  Pallas kernels  54.4 us (97%)
  between operations  0.68 us (1%)
    pallas_call x1, Pallas kernels, local_step(): pl.pallas_call(comm_kernel, out_shape=pltpu.VMEM((4, NC, OWN, CW), f32),...  35 us
    pallas_call x1, Pallas kernels, local_step(): pl.pallas_call(attn_kernel, out_shape=(pltpu.VMEM((9 * RP, LANES), f32),...  18.1 us
    pallas_call x1, Pallas kernels, local_step(): pl.pallas_call(finish_kernel, out_shape=jax.ShapeDtypeStruct((ROWS, DM),...  1.28 us

profile of v3, /device:TPU:0, one launch (start us, length us, event | category | flops | bytes accessed | tf_op | source)
XLA Modules:
  0.0 55.6 jit_solution(7283107240867999859)
XLA Ops:
  0.6 0.5 multiply_power_fusion.freq_h
  1.2 18.1 %attend.1 = (f32[1224,128]{1,0:T(8,128)S(1)}, bf16[128,256,128]{2,1,0:T(8,128)(2,1)}, bf16[128,256,128]{2,1,0:T(8,128)(2,1)}) custom-call(s32[128]{0:T(128)} %pos_h.1, s32[1,128]{1,0:T(1,128)} %bitcast.29, f32[1,128]{1,0:T(1,128)} %multiply_power_fusion.freq_h, bf16[128,3840]{1,0:T(8,128)(2,1)} %x_ref.1, f32[30,128]{1,0:T(8,128)} %bitcast.28, ...), custom_call_target="tpu_custom_call" | custom-call | tf_op jit(solution)/shard_map/attend/pallas_call | solution.py:423
  19.2 0.0 copy-start
  19.3 0.0 copy-start.1
  19.3 35.0 %combine.1.s_all = f32[4,15,32,256]{3,2,1,0:T(8,128)S(1)} custom-call(f32[9,136,128]{2,1,0:T(8,128)S(1)} %bitcast.24, bf16[1024,3840]{1,0:T(8,128)(2,1)} %wo_h.1), custom_call_target="tpu_custom_call" | custom-call | tf_op jit(solution)/shard_map/combine/pallas_call | solution.py:445
  54.3 0.0 copy-done
  54.3 0.0 copy-done.1
  54.3 1.3 %finish.1 = bf16[128,3840]{1,0:T(8,128)(2,1)} custom-call(f32[4,15,32,256]{3,2,1,0:T(8,128)S(1)} %combine.1.s_all, bf16[128,3840]{1,0:T(8,128)(2,1)S(1)} %copy-done, f32[30,128]{1,0:T(8,128)S(1)} %bitcast.25), custom_call_target="tpu_custom_call" | custom-call | tf_op jit(solution)/shard_map/finish/pallas_call | solution.py:461
Async XLA Ops:
  19.2 35.1 %copy-start = (bf16[128,3840]{1,0:T(8,128)(2,1)S(1)}, bf16[128,3840]{1,0:T(8,128)(2,1)}, u32[]{:S(2)}) copy-start(bf16[128,3840]{1,0:T(8,128)(2,1)} %x_ref.1) | copy-start | bytes 2949124
  19.3 35.1 %copy-start.1 = (f32[3840]{0:T(1024)S(1)}, f32[3840]{0:T(1024)}, u32[]{:S(2)}) copy-start(f32[3840]{0:T(1024)} %param.17) | copy-start | bytes 46084

commit v4 on v3

v4 whole, which is shorter than its diff:
```python
import functools

import jax
import jax.numpy as jnp
from jax import lax
from jax.experimental import pallas as pl
from jax.experimental.pallas import tpu as pltpu
from jax.sharding import PartitionSpec as P

SOFT_CAP = 50.0
ROPE_BASE = 10000.0
NORM_EPS = 1e-6

ROWS = 128
DM = 3840
HD = 256
TB = 64
RP = 136
LANES = 128
BCH = 16
HALF = ROWS // 2
HP = 72
NCH = HALF // BCH
SHIFT = 20.0
CW = 256
NC = DM // CW
OWN = 32
MP = 40
MESH = pl.DeviceIdType.MESH


def attend_rows(row0, nchunk, pos_ref, kbuf, vbuf, qs, ks, vs, o_ref, before, after):
    tbase = lax.axis_index('sp') * TB
    lane = lax.broadcasted_iota(jnp.int32, (8, LANES), 1)
    row = lax.broadcasted_iota(jnp.int32, (8, LANES), 0)
    row_c = row // 4
    row_h = (row // 2) % 2
    match = (((lane // 2) % 2) == row_c) & ((lane % 2) == row_h)
    match_f = jnp.where(match, 1.0, 0.0).astype(jnp.float32)
    first = row_c == 0
    t_half = [jnp.where(match, lane // 4 + 32 * hf, 1 << 20) for hf in range(2)]
    quad = lax.broadcasted_iota(jnp.int32, (16, LANES), 0) // 4
    zero = jnp.zeros((8, LANES), jnp.float32)

    def chunk(i, l_acc):
        before(i)
        tls = []
        for u in range(BCH):
            lb = i * BCH + u
            b = row0 + lb
            tl = pos_ref[b] - tbase
            tls.append(tl)
            hit = jnp.logical_and(tl >= 0, tl < TB)
            tc = jnp.clip(tl, 0, TB - 1)
            tile = tc // 4
            tgt = jnp.where(hit, tc - tile * 4, -1)
            sel = quad == tgt
            off = pl.multiple_of(tile * 16, 16)
            kn = ks[pl.ds(b, 8, stride=RP), :]
            vn = vs[pl.ds(b, 8, stride=RP), :]
            kt = kbuf[lb, pl.ds(off, 16), :].astype(jnp.float32)
            vt = vbuf[lb, pl.ds(off, 16), :].astype(jnp.float32)
            kbuf[lb, pl.ds(off, 16), :] = jnp.where(sel, jnp.concatenate([kn, kn], 0), kt).astype(jnp.bfloat16)
            vbuf[lb, pl.ds(off, 16), :] = jnp.where(sel, jnp.concatenate([vn, vn], 0), vt).astype(jnp.bfloat16)
        scores = []
        for u in range(0, BCH, 2):
            lb = i * BCH + u
            q0 = qs[pl.ds(row0 + lb, 8, stride=RP), :]
            q1 = qs[pl.ds(row0 + lb + 1, 8, stride=RP), :]
            lhs = jnp.concatenate([jnp.concatenate([q0, zero], 1), jnp.concatenate([zero, q1], 1)], 0).astype(jnp.bfloat16)
            kk = jnp.concatenate([kbuf[lb], kbuf[lb + 1]], 1)
            scores.append(lax.dot_general(lhs, kk, (((1,), (1,)), ((), ())), preferred_element_type=jnp.float32))
        weights = []
        for u in range(0, BCH, 2):
            pair = []
            for w in range(2):
                part = scores[u // 2][8 * w:8 * w + 8]
                es = []
                for hf in range(2):
                    a = part[:, hf * LANES:(hf + 1) * LANES] * match_f
                    e = pltpu.roll(a, 4, 0)
                    f = jnp.where(first, pltpu.roll(e, LANES - 2, 1), pltpu.roll(e, 2, 1))
                    s = SOFT_CAP * jnp.tanh((a + f) * (HD ** -0.5 / SOFT_CAP))
                    es.append(jnp.where(t_half[hf] <= tls[u + w], jnp.exp(s - SHIFT), 0.0))
                tot = jnp.sum(es[0] + es[1], axis=1, keepdims=True)
                inv = jnp.where(tot > 0.0, 1.0 / tot, 0.0)
                pair.append(jnp.concatenate([es[0] * inv, es[1] * inv], 1))
                l_acc = jnp.where(lane == i * BCH + u + w, tot, l_acc)
            weights.append(jnp.concatenate(pair, 0).astype(jnp.bfloat16))
        for u in range(0, BCH, 2):
            lb = i * BCH + u
            vv = jnp.concatenate([vbuf[lb], vbuf[lb + 1]], 1)
            o = jnp.dot(weights[u // 2], vv, preferred_element_type=jnp.float32)
            o_ref[pl.ds(lb, 8, stride=HP), :] = o[0:8, 0:LANES]
            o_ref[pl.ds(lb + 1, 8, stride=HP), :] = o[8:16, LANES:]
        after(i)
        return l_acc

    l_acc = lax.fori_loop(0, nchunk, chunk, zero)
    o_ref[pl.ds(HALF, 8, stride=HP), :] = l_acc


def far_kernel(pos_h, posv_h, freq_h, x_h, wpre_h, wq_h, wk_h, wv_h, kc_h, vc_h,
               o_ref, kbuf, vbuf, qs, ks, vs,
               pos_ref, posv, freq, wpre_ref, cos_ref, sin_ref, x_buf, a_buf, w_buf,
               x_sem, s_sem, w_sem, ki_sem, vi_sem):
    row0 = (1 - lax.axis_index('sp') // 2) * HALF

    def w_copy(i):
        if i < 2:
            src = wk_h.at[:, pl.ds(i * HD, HD)]
        elif i < 4:
            src = wv_h.at[:, pl.ds((i - 2) * HD, HD)]
        else:
            src = wq_h.at[:, pl.ds((i - 4) * HD, HD)]
        return pltpu.make_async_copy(src, w_buf.at[i], w_sem.at[i])

    def k_in(i):
        return pltpu.make_async_copy(kc_h.at[pl.ds(row0 + i * BCH, BCH)], kbuf.at[pl.ds(i * BCH, BCH)], ki_sem.at[i])

    def v_in(i):
        return pltpu.make_async_copy(vc_h.at[pl.ds(row0 + i * BCH, BCH)], vbuf.at[pl.ds(i * BCH, BCH)], vi_sem.at[i])

    x_copy = pltpu.make_async_copy(x_h, x_buf, x_sem)
    x_copy.start()
    small = [pltpu.make_async_copy(a, b, s_sem.at[i]) for i, (a, b) in enumerate(
        ((wpre_h, wpre_ref), (posv_h, posv), (freq_h, freq), (pos_h, pos_ref)))]
    for c in small:
        c.start()
    ahead = 5
    for i in range(ahead):
        w_copy(i).start()
    for c in small[1:]:
        c.wait()
    pos_col = jnp.broadcast_to(posv[...].astype(jnp.float32), (ROWS, LANES)).T
    ang = pos_col * freq[...]
    cos_ref[...] = jnp.cos(ang)
    sin_ref[...] = jnp.sin(ang)
    small[0].wait()
    x_copy.wait()

    gain = 1.0 + jnp.concatenate([wpre_ref[k:k + 1, :] for k in range(DM // LANES)], 1)

    def norm_rows(i, carry):
        r = pl.multiple_of(i * 16, 16)
        xb = x_buf[pl.ds(r, 16), :].astype(jnp.float32)
        ms = jnp.mean(xb * xb, axis=-1, keepdims=True)
        a_buf[pl.ds(r, 16), :] = (xb * lax.rsqrt(ms + NORM_EPS) * gain).astype(jnp.bfloat16)
        return carry

    lax.fori_loop(0, ROWS // 16, norm_rows, 0)

    issued = 0
    for i in range(8):
        w_copy(i).wait()
        if i + ahead < 8:
            w_copy(i + ahead).start()
        elif issued < NCH:
            k_in(issued).start()
            v_in(issued).start()
            issued += 1
        y = jnp.dot(a_buf[...], w_buf[i], preferred_element_type=jnp.float32)
        lo, hi = y[:, :LANES], y[:, LANES:]
        if 2 <= i < 4:
            h = i - 2
            for rep in range(2):
                vs[pl.ds((rep * 4 + h) * RP, ROWS), :] = lo
                vs[pl.ds((rep * 4 + 2 + h) * RP, ROWS), :] = hi
        else:
            cos_t, sin_t = cos_ref[...], sin_ref[...]
            rlo = lo * cos_t - hi * sin_t
            rhi = hi * cos_t + lo * sin_t
            if i < 2:
                for rep in range(2):
                    ks[pl.ds((rep * 4 + i) * RP, ROWS), :] = rlo
                    ks[pl.ds((rep * 4 + 2 + i) * RP, ROWS), :] = rhi
            else:
                qs[pl.ds((i - 4) * RP, ROWS), :] = rlo
                qs[pl.ds((4 + i - 4) * RP, ROWS), :] = rhi
    for c in range(issued, NCH):
        k_in(c).start()
        v_in(c).start()

    def before(i):
        k_in(i).wait()
        v_in(i).wait()

    attend_rows(row0, NCH, pos_ref, kbuf, vbuf, qs, ks, vs, o_ref, before, lambda i: None)


def near_kernel(pos_h, qs, ks, vs, kfar, vfar, kc_h, vc_h,
                o_ref, ko_h, vo_h,
                pos_ref, kbuf, vbuf, p_sem, ki_sem, vi_sem, kw_sem, vw_sem, kf_sem, vf_sem):
    yy = lax.axis_index('sp') // 2
    row0 = yy * HALF
    far0 = (1 - yy) * HALF

    def k_in(i):
        return pltpu.make_async_copy(kc_h.at[pl.ds(row0 + i * BCH, BCH)], kbuf.at[pl.ds(i * BCH, BCH)], ki_sem.at[i])

    def v_in(i):
        return pltpu.make_async_copy(vc_h.at[pl.ds(row0 + i * BCH, BCH)], vbuf.at[pl.ds(i * BCH, BCH)], vi_sem.at[i])

    def k_out(i):
        return pltpu.make_async_copy(kbuf.at[pl.ds(i * BCH, BCH)], ko_h.at[pl.ds(row0 + i * BCH, BCH)], kw_sem.at[i])

    def v_out(i):
        return pltpu.make_async_copy(vbuf.at[pl.ds(i * BCH, BCH)], vo_h.at[pl.ds(row0 + i * BCH, BCH)], vw_sem.at[i])

    def kf_out(i):
        return pltpu.make_async_copy(kfar.at[pl.ds(i * BCH, BCH)], ko_h.at[pl.ds(far0 + i * BCH, BCH)], kf_sem.at[i])

    def vf_out(i):
        return pltpu.make_async_copy(vfar.at[pl.ds(i * BCH, BCH)], vo_h.at[pl.ds(far0 + i * BCH, BCH)], vf_sem.at[i])

    p_copy = pltpu.make_async_copy(pos_h, pos_ref, p_sem)
    p_copy.start()
    for i in range(NCH):
        k_in(i).start()
        v_in(i).start()
    for i in range(NCH):
        kf_out(i).start()
        vf_out(i).start()
    p_copy.wait()

    def before(i):
        k_in(i).wait()
        v_in(i).wait()

    def after(i):
        k_out(i).start()
        v_out(i).start()

    attend_rows(row0, NCH, pos_ref, kbuf, vbuf, qs, ks, vs, o_ref, before, after)
    for i in range(NCH):
        kf_out(i).wait()
        vf_out(i).wait()
        k_out(i).wait()
        v_out(i).wait()


def comm_kernel(o_own, o_got, wo_h, s_all,
                wo_buf, fac, m1, m2, r1, lhs, p_buf, rr, rl, sr, sl,
                w_sem, r1_send, r1_recv,
                right_send, right_recv, left_send, left_recv,
                part_send, part_recv, y_send, y_recv, f_send, f_recv):
    z = lax.axis_index('tp')
    sp = lax.axis_index('sp')
    core = sp % 2
    partner = sp + 1 - 2 * core
    ypeer = (sp + 2) % 4

    def wo_copy(k):
        return pltpu.make_async_copy(wo_h.at[:, pl.ds(pl.multiple_of(k * CW, CW), CW)], wo_buf.at[k], w_sem.at[k])

    for k in range(NC):
        wo_copy(k).start()

    @pl.when(z == 0)
    def _():
        rr[...] = jnp.zeros_like(rr)

    @pl.when(z == 3)
    def _():
        rl[...] = jnp.zeros_like(rl)

    bar = pltpu.get_barrier_semaphore()
    pl.semaphore_signal(bar, inc=1, device_id={'sp': partner}, device_id_type=MESH)
    pl.semaphore_signal(bar, inc=1, device_id={'sp': ypeer}, device_id_type=MESH)

    @pl.when(z > 0)
    def _():
        pl.semaphore_signal(bar, inc=1, device_id={'tp': z - 1}, device_id_type=MESH)

    @pl.when(z < 3)
    def _():
        pl.semaphore_signal(bar, inc=1, device_id={'tp': z + 1}, device_id_type=MESH)

    pl.semaphore_wait(bar, 3 + (z * (3 - z)) // 2)

    def shares(l_a, l_b, slot):
        tot = l_a + l_b
        inv = jnp.where(tot > 0.0, 1.0 / tot, 0.0)
        for w, l in enumerate((l_a, l_b)):
            fac[slot + w] = jnp.concatenate([l * inv, jnp.zeros((LANES - 8, LANES), jnp.float32)], 0).T
        return tot

    mine = pl.multiple_of(core * OWN, OWN)
    theirs = pl.multiple_of((1 - core) * OWN, OWN)
    tot = shares(o_own[pl.ds(HALF, 8, stride=HP), :], o_got[pl.ds(HALF, 8, stride=HP), :], 0)

    def merge_half(r0, dst, stride):
        fa, fb = fac[0, pl.ds(r0, OWN), :], fac[1, pl.ds(r0, OWN), :]
        for j in range(8):
            rows = pl.ds(pl.multiple_of(j * HP + r0, 8), OWN)
            dst[pl.ds(j * stride, OWN), :] = o_own[rows, :] * fa[:, j:j + 1] + o_got[rows, :] * fb[:, j:j + 1]

    merge_half(theirs, m1, MP)
    m1[pl.ds(OWN, 8, stride=MP), :] = tot
    pair = pltpu.make_async_remote_copy(
        src_ref=m1, dst_ref=r1, send_sem=r1_send, recv_sem=r1_recv, device_id={'sp': partner}, device_id_type=MESH)
    pair.start()
    merge_half(mine, m2, OWN)
    pair.wait()
    shares(tot, r1[pl.ds(OWN, 8, stride=MP), :], 2)
    fa, fb = fac[2, pl.ds(mine, OWN), :], fac[3, pl.ds(mine, OWN), :]
    for j in range(8):
        c, hq = j // 4, j % 4
        val = m2[j * OWN:(j + 1) * OWN, :] * fa[:, j:j + 1] + r1[j * MP:j * MP + OWN, :] * fb[:, j:j + 1]
        lhs[:, (hq * 2 + c) * LANES:(hq * 2 + c + 1) * LANES] = val.astype(jnp.bfloat16)

    def right_copy(k):
        return pltpu.make_async_remote_copy(
            src_ref=sr.at[k], dst_ref=rr.at[k], send_sem=right_send.at[k], recv_sem=right_recv.at[k],
            device_id={'tp': z + 1}, device_id_type=MESH)

    def left_copy(k):
        return pltpu.make_async_remote_copy(
            src_ref=sl.at[k], dst_ref=rl.at[k], send_sem=left_send.at[k], recv_sem=left_recv.at[k],
            device_id={'tp': z - 1}, device_id_type=MESH)

    def part_copy(k):
        return pltpu.make_async_remote_copy(
            src_ref=s_all.at[sp, k], dst_ref=s_all.at[sp, k], send_sem=part_send.at[k], recv_sem=part_recv.at[k],
            device_id={'sp': partner}, device_id_type=MESH)

    def y_copy(k):
        return pltpu.make_async_remote_copy(
            src_ref=s_all.at[sp, k], dst_ref=s_all.at[sp, k], send_sem=y_send.at[k], recv_sem=y_recv.at[k],
            device_id={'sp': ypeer}, device_id_type=MESH)

    def fwd_copy(k):
        return pltpu.make_async_remote_copy(
            src_ref=s_all.at[ypeer, k], dst_ref=s_all.at[ypeer, k], send_sem=f_send.at[k], recv_sem=f_recv.at[k],
            device_id={'sp': partner}, device_id_type=MESH)

    hop = 6
    lag_r = hop * z
    lag_l = hop * (3 - z)
    lag_s = hop * (3 - (z * (3 - z)) // 2)

    def tick(i, carry):
        @pl.when(i < NC)
        def _():
            wo_copy(i).wait()
            p_buf[i] = jnp.dot(lhs[...], wo_buf[i], preferred_element_type=jnp.float32)

        kr = i - lag_r

        @pl.when(jnp.logical_and(kr >= 0, kr < NC))
        def _():
            @pl.when(z > 0)
            def _():
                right_copy(kr).wait_recv()

            @pl.when(z < 3)
            def _():
                sr[kr] = p_buf[kr] + rr[kr]
                right_copy(kr).start()

        kl = i - lag_l

        @pl.when(jnp.logical_and(kl >= 0, kl < NC))
        def _():
            @pl.when(z < 3)
            def _():
                left_copy(kl).wait_recv()

            @pl.when(z > 0)
            def _():
                sl[kl] = p_buf[kl] + rl[kl]
                left_copy(kl).start()

        k_s = i - lag_s

        @pl.when(jnp.logical_and(k_s >= 0, k_s < NC))
        def _():
            s_all[sp, k_s] = p_buf[k_s] + rr[k_s] + rl[k_s]
            y_copy(k_s).start()
            part_copy(k_s).start()

        k_y = i - lag_s - hop

        @pl.when(jnp.logical_and(k_y >= 0, k_y < NC))
        def _():
            y_copy(k_y).wait_recv()
            fwd_copy(k_y).start()

        return carry

    lax.fori_loop(0, NC + 4 * hop, tick, 0)

    def drain(k, carry):
        part_copy(k).wait()
        y_copy(k).wait_send()
        fwd_copy(k).wait()

        @pl.when(z < 3)
        def _():
            right_copy(k).wait_send()

        @pl.when(z > 0)
        def _():
            left_copy(k).wait_send()

        return carry

    lax.fori_loop(0, NC, drain, 0)


def finish_kernel(s_all, x_ref, wpost_ref, out_h, out_buf, sem):
    blk = 16

    def out_copy(i):
        rows = pl.ds(i * blk, blk)
        return pltpu.make_async_copy(out_buf.at[rows], out_h.at[rows], sem.at[i])

    for i in range(ROWS // blk):
        g, r = (i * blk) // OWN, (i * blk) % OWN
        parts = [s_all[g, k, r:r + blk, :] for k in range(NC)]
        sq = parts[0] * parts[0]
        for k in range(1, NC):
            sq = sq + parts[k] * parts[k]
        rs = lax.rsqrt(jnp.sum(sq, axis=-1, keepdims=True) * (1.0 / DM) + NORM_EPS)
        for k in range(NC):
            for hf in range(CW // LANES):
                col = k * CW + hf * LANES
                gain = 1.0 + wpost_ref[col // LANES:col // LANES + 1, :]
                val = s_all[g, k, r:r + blk, hf * LANES:(hf + 1) * LANES] * rs * gain
                cs = slice(col, col + LANES)
                out_buf[i * blk:(i + 1) * blk, cs] = (x_ref[i * blk:(i + 1) * blk, cs].astype(jnp.float32) + val).astype(jnp.bfloat16)
        out_copy(i).start()
    for i in range(ROWS // blk):
        out_copy(i).wait()


def solution(mesh):
    cache_spec = P('dp', 'sp', 'tp', None)
    hbm = pl.BlockSpec(memory_space=pltpu.HBM)
    vmem = pl.BlockSpec(memory_space=pltpu.VMEM)

    def in_hbm(arr):
        return pltpu.with_memory_space_constraint(arr, pltpu.HBM)

    def in_vmem(arr):
        return pltpu.with_memory_space_constraint(arr, pltpu.VMEM)

    def to_rows(c):
        b, t, h, d = c.shape
        return c.reshape(b, t, h, 2, LANES).transpose(0, 1, 3, 2, 4).reshape(b, t * 2 * h, LANES)

    def from_rows(r):
        return r.reshape(ROWS, TB, 2, 2, LANES).transpose(0, 1, 3, 2, 4).reshape(ROWS, TB, 2, HD)

    def local_step(x_in, cur_pos, w_pre, w_q, w_k, w_v, w_o, w_post, k_cache, v_cache):
        half = HD // 2
        inv_freq = ROPE_BASE ** (-2.0 * jnp.arange(half, dtype=jnp.float32) / (2 * half))
        kr, vr = to_rows(k_cache), to_rows(v_cache)
        f32, bf16 = jnp.float32, jnp.bfloat16
        dma = pltpu.SemaphoreType.DMA
        half_shape = (HALF,) + kr.shape[1:]
        o_far, k_far, v_far, qs, ks, vs = pl.pallas_call(
            far_kernel,
            out_shape=(jax.ShapeDtypeStruct((8 * HP, LANES), f32),
                       pltpu.VMEM(half_shape, bf16), pltpu.VMEM(half_shape, bf16),
                       pltpu.VMEM((8 * RP, LANES), f32), pltpu.VMEM((8 * RP, LANES), f32), pltpu.VMEM((8 * RP, LANES), f32)),
            in_specs=[hbm] * 10,
            out_specs=(vmem,) * 6,
            scratch_shapes=[
                pltpu.SMEM((ROWS,), jnp.int32), pltpu.VMEM((1, ROWS), jnp.int32), pltpu.VMEM((1, LANES), f32),
                pltpu.VMEM((DM // LANES, LANES), f32), pltpu.VMEM((ROWS, LANES), f32), pltpu.VMEM((ROWS, LANES), f32),
                pltpu.VMEM((ROWS, DM), bf16), pltpu.VMEM((ROWS, DM), bf16), pltpu.VMEM((8, DM, HD), bf16),
                dma, dma((4,)), dma((8,)), dma((NCH,)), dma((NCH,)),
            ],
            compiler_params=pltpu.CompilerParams(vmem_limit_bytes=40 << 20),
            cost_estimate=pl.CostEstimate(flops=2 * 10 ** 9, bytes_accessed=25 * 10 ** 6, transcendentals=0),
            name='attend_far',
        )(in_hbm(cur_pos), in_hbm(cur_pos.reshape(1, ROWS)), in_hbm(inv_freq.reshape(1, LANES)), in_hbm(x_in),
          in_hbm(w_pre.reshape(DM // LANES, LANES)), in_hbm(w_q), in_hbm(w_k), in_hbm(w_v), in_hbm(kr), in_hbm(vr))
        o_got = lax.ppermute(o_far, 'sp', [(0, 2), (1, 3), (2, 0), (3, 1)])
        o_own, k_new, v_new = pl.pallas_call(
            near_kernel,
            out_shape=(pltpu.VMEM((8 * HP, LANES), f32),
                       jax.ShapeDtypeStruct(kr.shape, bf16), jax.ShapeDtypeStruct(vr.shape, bf16)),
            in_specs=[hbm, vmem, vmem, vmem, vmem, vmem, hbm, hbm],
            out_specs=(vmem, hbm, hbm),
            scratch_shapes=[
                pltpu.SMEM((ROWS,), jnp.int32), pltpu.VMEM(half_shape, bf16), pltpu.VMEM(half_shape, bf16),
                dma, dma((NCH,)), dma((NCH,)), dma((NCH,)), dma((NCH,)), dma((NCH,)), dma((NCH,)),
            ],
            compiler_params=pltpu.CompilerParams(vmem_limit_bytes=28 << 20),
            cost_estimate=pl.CostEstimate(flops=10 ** 10, bytes_accessed=25 * 10 ** 6, transcendentals=0),
            name='attend_near',
        )(in_hbm(cur_pos), in_vmem(qs), in_vmem(ks), in_vmem(vs), in_vmem(k_far), in_vmem(v_far), in_hbm(kr), in_hbm(vr))
        big = pltpu.VMEM((NC, OWN, CW), f32)
        sums = pl.pallas_call(
            comm_kernel,
            out_shape=pltpu.VMEM((4, NC, OWN, CW), f32),
            in_specs=[vmem, vmem, hbm],
            out_specs=vmem,
            scratch_shapes=[
                pltpu.VMEM((NC, 1024, CW), bf16), pltpu.VMEM((4, LANES, LANES), f32), pltpu.VMEM((8 * MP, LANES), f32),
                pltpu.VMEM((8 * OWN, LANES), f32), pltpu.VMEM((8 * MP, LANES), f32), pltpu.VMEM((OWN, 1024), bf16),
                big, big, big, big, big,
                dma((NC,)), dma, dma,
                dma((NC,)), dma((NC,)), dma((NC,)), dma((NC,)),
                dma((NC,)), dma((NC,)), dma((NC,)), dma((NC,)), dma((NC,)), dma((NC,)),
            ],
            compiler_params=pltpu.CompilerParams(vmem_limit_bytes=40 << 20, collective_id=0, has_side_effects=True),
            name='combine',
        )(in_vmem(o_own), o_got, in_hbm(w_o))
        x_out = pl.pallas_call(
            finish_kernel,
            out_shape=jax.ShapeDtypeStruct((ROWS, DM), bf16),
            in_specs=[vmem, vmem, vmem],
            out_specs=hbm,
            scratch_shapes=[pltpu.VMEM((ROWS, DM), bf16), dma((ROWS // 16,))],
            compiler_params=pltpu.CompilerParams(vmem_limit_bytes=16 << 20),
            name='finish',
        )(in_vmem(sums), x_in, w_post.reshape(DM // LANES, LANES))
        return x_out, from_rows(k_new), from_rows(v_new)

    return jax.shard_map(local_step, mesh=mesh,
                         in_specs=(P('dp', None), P('dp'), P(None), P(None, 'tp'), P(None, 'tp'), P(None, 'tp'), P('tp', None), P(None), cache_spec, cache_spec),
                         out_specs=(P('dp', None), cache_spec, cache_spec), check_vma=False)
```

time: 55.8 us -> 57.7 us (1.034)
  starting transfers between devices: 0 us -> 3.09 us
  Pallas kernels: 54.4 us -> 53.2 us
    pallas_call x1, Pallas kernels: 35 us -> 28.6 us  [local_step(): pl.pallas_call(comm_kernel, out_shape=pltpu.VMEM((4, NC, OWN, CW), f32),...]
    pallas_call x1 -> x2, Pallas kernels: 18.1 us -> 23.4 us  [the longest x1 13.6 us: local_step(): pl.pallas_call(far_kernel, out_shape=(jax.ShapeDtypeStruct((8 * HP, LANES...]
    ppermute x0 -> x1, starting transfers between devices: none -> 3.09 us  [local_step(): o_got = lax.ppermute(o_far, 'sp', [(0, 2), (1, 3), (2, 0), (3, 1)])]
  transfers between devices with their start and end apart: 0 -> 1, of which waited for: 0 -> 0; matrix products, arithmetic and copies ran while one was open for 0% -> 0% of each run, Pallas kernels for 0% -> 17%
where the time goes in v4:
time: 57.7 us; the launch traced here: 57.5 us
  Pallas kernels  53.2 us (92%)
  starting transfers between devices  3.09 us (5%)
  between operations  0.69 us (1%)
    pallas_call x1, Pallas kernels, local_step(): pl.pallas_call(comm_kernel, out_shape=pltpu.VMEM((4, NC, OWN, CW), f32),...  28.6 us
    pallas_call x1, Pallas kernels, local_step(): pl.pallas_call(far_kernel, out_shape=(jax.ShapeDtypeStruct((8 * HP, LANES...  13.6 us
    pallas_call x1, Pallas kernels, local_step(): pl.pallas_call(near_kernel, out_shape=(pltpu.VMEM((8 * HP, LANES), f32),...  9.82 us
    ppermute x1, starting transfers between devices, local_step(): o_got = lax.ppermute(o_far, 'sp', [(0, 2), (1, 3), (2, 0), (3, 1)])  3.09 us
    pallas_call x1, Pallas kernels, local_step(): pl.pallas_call(finish_kernel, out_shape=jax.ShapeDtypeStruct((ROWS, DM),...  1.24 us
  transfers between devices with their start and end apart: 1, of which 0 were waited for; matrix products, arithmetic and copies ran while one was open for 0% of the time, Pallas kernels for 17%

profile of v4, /device:TPU:0, one launch (start us, length us, event | category | flops | bytes accessed | tf_op | source)
XLA Modules:
  0.0 57.5 jit_solution(12135823430289962667)
XLA Ops:
  0.6 0.5 multiply_power_fusion.freq_h
  1.2 13.6 %attend_far.1 = (f32[576,128]{1,0:T(8,128)S(1)}, bf16[64,256,128]{2,1,0:T(8,128)(2,1)S(1)}, bf16[64,256,128]{2,1,0:T(8,128)(2,1)S(1)}, f32[1088,128]{1,0:T(8,128...) custom-call(s32[128]{0:T(128)} %pos_h.3, s32[1,128]{1,0:T(1,128)} %bitcast.29, ...), custom_call_target="tpu_custom_call" | custom-call | flops 2000000000 | bytes 25000000 | tf_op jit(solution)/shard_map/attend_far/pallas_call | solution.py:462
  14.7 3.1 %collective-permute-start = (f32[576,128]{1,0:T(8,128)S(1)}, f32[576,128]{1,0:T(8,128)S(1)}, u32[]{:S(2)}, u32[]{:S(2)}) collective-permute-start(f32[576,128]{1,0:T(8,128)S(1)} %get-tuple-element.18), channel_id=1, source_target_pairs={{0,2},{1,3},{2,0},{3,1},{4,6},{5,7},{6,4},{7,5},{8,10},{9,11},{10,... | collective-permute-start | bytes 884744 | tf_op jit(solution)/shard_map/ppermute | solution.py:480
  17.8 9.8 %attend_near.1 = (f32[576,128]{1,0:T(8,128)S(1)}, bf16[128,256,128]{2,1,0:T(8,128)(2,1)}, bf16[128,256,128]{2,1,0:T(8,128)(2,1)}) custom-call(s32[128]{0:T(128)} %pos_h.3, f32[1088,128]{1,0:T(8,128)S(1)} %get-tuple-element.12.qs, f32[1088,128]{1,0:T(8,128)S(1)} %get-tuple-element.13.ks, f32[1088,128]{1,0:T(8,128)S(1)} %get-tuple-element.14.vs, ...), custom_call_target="tpu_custom_call" | custom-call | flops 10000000000 | bytes 25000000 | tf_op jit(solution)/shard_map/attend_near/pallas_call | solution.py:481
  27.6 0.0 copy-start
  27.7 0.0 copy-start.1
  27.7 0.0 collective-permute-done.o_got
  27.7 28.6 %combine.1.s_all = f32[4,15,32,256]{3,2,1,0:T(8,128)S(1)} custom-call(f32[576,128]{1,0:T(8,128)S(1)} %get-tuple-element.17.o_own, f32[576,128]{1,0:T(8,128)S(1)} %collective-permute-done.o_got, bf16[1024,3840]{1,0:T(8,128)(2,1)} %wo_h.1), custom_call_target="tpu_custom_call" | custom-call | tf_op jit(solution)/shard_map/combine/pallas_call | solution.py:496
  56.2 0.0 copy-done
  56.3 0.0 copy-done.1
  56.3 1.2 %finish.1 = bf16[128,3840]{1,0:T(8,128)(2,1)} custom-call(f32[4,15,32,256]{3,2,1,0:T(8,128)S(1)} %combine.1.s_all, bf16[128,3840]{1,0:T(8,128)(2,1)S(1)} %copy-done, f32[30,128]{1,0:T(8,128)S(1)} %bitcast.23), custom_call_target="tpu_custom_call" | custom-call | tf_op jit(solution)/shard_map/finish/pallas_call | solution.py:512
Async XLA Ops:
  14.7 12.9 %collective-permute-start = (f32[576,128]{1,0:T(8,128)S(1)}, f32[576,128]{1,0:T(8,128)S(1)}, u32[]{:S(2)}, u32[]{:S(2)}) collective-permute-start(f32[576,128]{1,0:T(8,128)S(1)} %get-tuple-element.18), channel_id=1, source_target_pairs={{0,2},{1,3},{2,0},{3,1},{4,6},{5,7},{6,4},{7,5},{8,10},{9,11},{10,... | collective-permute-start | bytes 884744 | tf_op jit(solution)/shard_map/ppermute | solution.py:480
  27.6 28.6 %copy-start = (bf16[128,3840]{1,0:T(8,128)(2,1)S(1)}, bf16[128,3840]{1,0:T(8,128)(2,1)}, u32[]{:S(2)}) copy-start(bf16[128,3840]{1,0:T(8,128)(2,1)} %x_ref.1) | copy-start | bytes 2949124
  27.7 28.6 %copy-start.1 = (f32[3840]{0:T(1024)S(1)}, f32[3840]{0:T(1024)}, u32[]{:S(2)}) copy-start(f32[3840]{0:T(1024)} %param.17) | copy-start | bytes 46084

commit v5 on v4

--- a/solution.py
+++ b/solution.py
@@ -2,6 +2,7 @@
 
 import jax
 import jax.numpy as jnp
+import numpy as np
 from jax import lax
 from jax.experimental import pallas as pl
 from jax.experimental.pallas import tpu as pltpu
@@ -21,6 +22,8 @@
 HALF = ROWS // 2
 HP = 72
 NCH = HALF // BCH
+KC = 768
+NKC = DM // KC
 SHIFT = 20.0
 CW = 256
 NC = DM // CW
@@ -102,18 +105,19 @@
 
 def far_kernel(pos_h, posv_h, freq_h, x_h, wpre_h, wq_h, wk_h, wv_h, kc_h, vc_h,
                o_ref, kbuf, vbuf, qs, ks, vs,
-               pos_ref, posv, freq, wpre_ref, cos_ref, sin_ref, x_buf, a_buf, w_buf,
+               pos_ref, posv, freq, wpre_ref, cos_ref, sin_ref, x_buf, a_buf, wq_buf, wk_buf, wv_buf, acc,
                x_sem, s_sem, w_sem, ki_sem, vi_sem):
     row0 = (1 - lax.axis_index('sp') // 2) * HALF
 
-    def w_copy(i):
-        if i < 2:
-            src = wk_h.at[:, pl.ds(i * HD, HD)]
-        elif i < 4:
-            src = wv_h.at[:, pl.ds((i - 2) * HD, HD)]
-        else:
-            src = wq_h.at[:, pl.ds((i - 4) * HD, HD)]
-        return pltpu.make_async_copy(src, w_buf.at[i], w_sem.at[i])
+    def w_start(c):
+        rows = pl.ds(c * KC, KC)
+        for n, (src, dst) in enumerate(((wk_h, wk_buf), (wv_h, wv_buf), (wq_h, wq_buf))):
+            pltpu.make_async_copy(src.at[rows, :], dst.at[rows, :], w_sem.at[3 * c + n]).start()
+
+    def w_wait(c):
+        rows = pl.ds(c * KC, KC)
+        for n, (src, dst) in enumerate(((wk_h, wk_buf), (wv_h, wv_buf), (wq_h, wq_buf))):
+            pltpu.make_async_copy(src.at[rows, :], dst.at[rows, :], w_sem.at[3 * c + n]).wait()
 
     def k_in(i):
         return pltpu.make_async_copy(kc_h.at[pl.ds(row0 + i * BCH, BCH)], kbuf.at[pl.ds(i * BCH, BCH)], ki_sem.at[i])
@@ -121,23 +125,22 @@
     def v_in(i):
         return pltpu.make_async_copy(vc_h.at[pl.ds(row0 + i * BCH, BCH)], vbuf.at[pl.ds(i * BCH, BCH)], vi_sem.at[i])
 
-    x_copy = pltpu.make_async_copy(x_h, x_buf, x_sem)
-    x_copy.start()
     small = [pltpu.make_async_copy(a, b, s_sem.at[i]) for i, (a, b) in enumerate(
         ((wpre_h, wpre_ref), (posv_h, posv), (freq_h, freq), (pos_h, pos_ref)))]
     for c in small:
         c.start()
-    ahead = 5
-    for i in range(ahead):
-        w_copy(i).start()
-    for c in small[1:]:
+    x_copy = pltpu.make_async_copy(x_h, x_buf, x_sem)
+    x_copy.start()
+    w_start(0)
+    for c in small:
         c.wait()
+    w_start(1)
     pos_col = jnp.broadcast_to(posv[...].astype(jnp.float32), (ROWS, LANES)).T
     ang = pos_col * freq[...]
     cos_ref[...] = jnp.cos(ang)
     sin_ref[...] = jnp.sin(ang)
-    small[0].wait()
     x_copy.wait()
+    w_start(2)
 
     gain = 1.0 + jnp.concatenate([wpre_ref[k:k + 1, :] for k in range(DM // LANES)], 1)
 
@@ -150,36 +153,48 @@
 
     lax.fori_loop(0, ROWS // 16, norm_rows, 0)
 
-    issued = 0
-    for i in range(8):
-        w_copy(i).wait()
-        if i + ahead < 8:
-            w_copy(i + ahead).start()
-        elif issued < NCH:
-            k_in(issued).start()
-            v_in(issued).start()
-            issued += 1
-        y = jnp.dot(a_buf[...], w_buf[i], preferred_element_type=jnp.float32)
-        lo, hi = y[:, :LANES], y[:, LANES:]
-        if 2 <= i < 4:
-            h = i - 2
-            for rep in range(2):
-                vs[pl.ds((rep * 4 + h) * RP, ROWS), :] = lo
-                vs[pl.ds((rep * 4 + 2 + h) * RP, ROWS), :] = hi
+    for c in range(NKC):
+        w_wait(c)
+        if c + 3 < NKC:
+            w_start(c + 3)
         else:
-            cos_t, sin_t = cos_ref[...], sin_ref[...]
-            rlo = lo * cos_t - hi * sin_t
-            rhi = hi * cos_t + lo * sin_t
+            for n in range(2 * (c + 3 - NKC), min(NCH, 2 * (c + 4 - NKC))):
+                k_in(n).start()
+                v_in(n).start()
+        rows = slice(c * KC, (c + 1) * KC)
+        a_c = a_buf[:, rows]
+        for i in range(8):
             if i < 2:
+                w_c = wk_buf[rows, i * HD:(i + 1) * HD]
+            elif i < 4:
+                w_c = wv_buf[rows, (i - 2) * HD:(i - 1) * HD]
+            else:
+                w_c = wq_buf[rows, (i - 4) * HD:(i - 3) * HD]
+            y = jnp.dot(a_c, w_c, preferred_element_type=jnp.float32)
+            if c == 0:
+                acc[i] = y
+                continue
+            y = acc[i] + y
+            if c < NKC - 1:
+                acc[i] = y
+                continue
+            lo, hi = y[:, :LANES], y[:, LANES:]
+            if 2 <= i < 4:
+                h = i - 2
                 for rep in range(2):
-                    ks[pl.ds((rep * 4 + i) * RP, ROWS), :] = rlo
-                    ks[pl.ds((rep * 4 + 2 + i) * RP, ROWS), :] = rhi
+                    vs[pl.ds((rep * 4 + h) * RP, ROWS), :] = lo
+                    vs[pl.ds((rep * 4 + 2 + h) * RP, ROWS), :] = hi
             else:
-                qs[pl.ds((i - 4) * RP, ROWS), :] = rlo
-                qs[pl.ds((4 + i - 4) * RP, ROWS), :] = rhi
-    for c in range(issued, NCH):
-        k_in(c).start()
-        v_in(c).start()
+                cos_t, sin_t = cos_ref[...], sin_ref[...]
+                rlo = lo * cos_t - hi * sin_t
+                rhi = hi * cos_t + lo * sin_t
+                if i < 2:
+                    for rep in range(2):
+                        ks[pl.ds((rep * 4 + i) * RP, ROWS), :] = rlo
+                        ks[pl.ds((rep * 4 + 2 + i) * RP, ROWS), :] = rhi
+                else:
+                    qs[pl.ds((i - 4) * RP, ROWS), :] = rlo
+                    qs[pl.ds((4 + i - 4) * RP, ROWS), :] = rhi
 
     def before(i):
         k_in(i).wait()
@@ -218,14 +233,13 @@
     for i in range(NCH):
         k_in(i).start()
         v_in(i).start()
-    for i in range(NCH):
-        kf_out(i).start()
-        vf_out(i).start()
     p_copy.wait()
 
     def before(i):
         k_in(i).wait()
         v_in(i).wait()
+        kf_out(i).start()
+        vf_out(i).start()
 
     def after(i):
         k_out(i).start()
@@ -454,7 +468,7 @@
 
     def local_step(x_in, cur_pos, w_pre, w_q, w_k, w_v, w_o, w_post, k_cache, v_cache):
         half = HD // 2
-        inv_freq = ROPE_BASE ** (-2.0 * jnp.arange(half, dtype=jnp.float32) / (2 * half))
+        inv_freq = jnp.asarray((ROPE_BASE ** (-2.0 * np.arange(half) / (2 * half))).astype(np.float32))
         kr, vr = to_rows(k_cache), to_rows(v_cache)
         f32, bf16 = jnp.float32, jnp.bfloat16
         dma = pltpu.SemaphoreType.DMA
@@ -469,8 +483,9 @@
             scratch_shapes=[
                 pltpu.SMEM((ROWS,), jnp.int32), pltpu.VMEM((1, ROWS), jnp.int32), pltpu.VMEM((1, LANES), f32),
                 pltpu.VMEM((DM // LANES, LANES), f32), pltpu.VMEM((ROWS, LANES), f32), pltpu.VMEM((ROWS, LANES), f32),
-                pltpu.VMEM((ROWS, DM), bf16), pltpu.VMEM((ROWS, DM), bf16), pltpu.VMEM((8, DM, HD), bf16),
-                dma, dma((4,)), dma((8,)), dma((NCH,)), dma((NCH,)),
+                pltpu.VMEM((ROWS, DM), bf16), pltpu.VMEM((ROWS, DM), bf16),
+                pltpu.VMEM((DM, 1024), bf16), pltpu.VMEM((DM, 512), bf16), pltpu.VMEM((DM, 512), bf16), pltpu.VMEM((8, ROWS, HD), f32),
+                dma, dma((4,)), dma((3 * NKC,)), dma((NCH,)), dma((NCH,)),
             ],
             compiler_params=pltpu.CompilerParams(vmem_limit_bytes=40 << 20),
             cost_estimate=pl.CostEstimate(flops=2 * 10 ** 9, bytes_accessed=25 * 10 ** 6, transcendentals=0),

time: 57.7 us -> 52.3 us (0.906)
  Pallas kernels: 53.2 us -> 48.2 us
    pallas_call x1, Pallas kernels: 13.6 us -> 10.2 us  [local_step(): pl.pallas_call(far_kernel, out_shape=(jax.ShapeDtypeStruct((8 * HP, LANES...]
    pallas_call x1, Pallas kernels: 9.82 us -> 8.18 us  [local_step(): pl.pallas_call(near_kernel, out_shape=(pltpu.VMEM((8 * HP, LANES), f32),...]
  transfers between devices with their start and end apart: 1 -> 1, of which waited for: 0 -> 0; matrix products, arithmetic and copies ran while one was open for 0% -> 0% of each run, Pallas kernels for 17% -> 16%
where the time goes in v5:
time: 52.3 us; the launch traced here: 52 us
  Pallas kernels  48.2 us (92%)
  starting transfers between devices  3.09 us (6%)
  between operations  0.7 us (1%)
    pallas_call x1, Pallas kernels, local_step(): pl.pallas_call(comm_kernel, out_shape=pltpu.VMEM((4, NC, OWN, CW), f32),...  28.6 us
    pallas_call x1, Pallas kernels, local_step(): pl.pallas_call(far_kernel, out_shape=(jax.ShapeDtypeStruct((8 * HP, LANES...  10.2 us
    pallas_call x1, Pallas kernels, local_step(): pl.pallas_call(near_kernel, out_shape=(pltpu.VMEM((8 * HP, LANES), f32),...  8.18 us
    ppermute x1, starting transfers between devices, local_step(): o_got = lax.ppermute(o_far, 'sp', [(0, 2), (1, 3), (2, 0), (3, 1)])  3.09 us
    pallas_call x1, Pallas kernels, local_step(): pl.pallas_call(finish_kernel, out_shape=jax.ShapeDtypeStruct((ROWS, DM),...  1.24 us
  transfers between devices with their start and end apart: 1, of which 0 were waited for; matrix products, arithmetic and copies ran while one was open for 0% of the time, Pallas kernels for 16%

profile of v5, /device:TPU:0, one launch (start us, length us, event | category | flops | bytes accessed | tf_op | source)
XLA Modules:
  0.0 52.0 jit_solution(13111175832379471104)
XLA Ops:
  0.6 10.2 %attend_far.1 = (f32[576,128]{1,0:T(8,128)S(1)}, bf16[64,256,128]{2,1,0:T(8,128)(2,1)S(1)}, bf16[64,256,128]{2,1,0:T(8,128)(2,1)S(1)}, f32[1088,128]{1,0:T(8,128...) custom-call(s32[128]{0:T(128)} %pos_h.3, s32[1,128]{1,0:T(1,128)} %bitcast.29, f32[1,128]{1,0:T(1,128)} %constant.5.freq_h, ...), custom_call_target="tpu_custom_call" | custom-call | flops 2000000000 | bytes 25000000 | tf_op jit(solution)/shard_map/attend_far/pallas_call | solution.py:476
  10.9 3.1 %collective-permute-start = (f32[576,128]{1,0:T(8,128)S(1)}, f32[576,128]{1,0:T(8,128)S(1)}, u32[]{:S(2)}, u32[]{:S(2)}) collective-permute-start(f32[576,128]{1,0:T(8,128)S(1)} %get-tuple-element.18), channel_id=1, source_target_pairs={{0,2},{1,3},{2,0},{3,1},{4,6},{5,7},{6,4},{7,5},{8,10},{9,11},{10,... | collective-permute-start | bytes 884744 | tf_op jit(solution)/shard_map/ppermute | solution.py:495
  14.0 8.2 %attend_near.1 = (f32[576,128]{1,0:T(8,128)S(1)}, bf16[128,256,128]{2,1,0:T(8,128)(2,1)}, bf16[128,256,128]{2,1,0:T(8,128)(2,1)}) custom-call(s32[128]{0:T(128)} %pos_h.3, f32[1088,128]{1,0:T(8,128)S(1)} %get-tuple-element.12.qs, f32[1088,128]{1,0:T(8,128)S(1)} %get-tuple-element.13.ks, f32[1088,128]{1,0:T(8,128)S(1)} %get-tuple-element.14.vs, ...), custom_call_target="tpu_custom_call" | custom-call | flops 10000000000 | bytes 25000000 | tf_op jit(solution)/shard_map/attend_near/pallas_call | solution.py:496
  22.2 0.0 copy-start
  22.2 0.0 copy-start.1
  22.2 0.0 collective-permute-done.o_got
  22.2 28.6 %combine.1.s_all = f32[4,15,32,256]{3,2,1,0:T(8,128)S(1)} custom-call(f32[576,128]{1,0:T(8,128)S(1)} %get-tuple-element.17.o_own, f32[576,128]{1,0:T(8,128)S(1)} %collective-permute-done.o_got, bf16[1024,3840]{1,0:T(8,128)(2,1)} %wo_h.1), custom_call_target="tpu_custom_call" | custom-call | tf_op jit(solution)/shard_map/combine/pallas_call | solution.py:511
  50.8 0.0 copy-done
  50.8 0.0 copy-done.1
  50.8 1.2 %finish.1 = bf16[128,3840]{1,0:T(8,128)(2,1)} custom-call(f32[4,15,32,256]{3,2,1,0:T(8,128)S(1)} %combine.1.s_all, bf16[128,3840]{1,0:T(8,128)(2,1)S(1)} %copy-done, f32[30,128]{1,0:T(8,128)S(1)} %bitcast.23), custom_call_target="tpu_custom_call" | custom-call | tf_op jit(solution)/shard_map/finish/pallas_call | solution.py:527
Async XLA Ops:
  10.9 11.3 %collective-permute-start = (f32[576,128]{1,0:T(8,128)S(1)}, f32[576,128]{1,0:T(8,128)S(1)}, u32[]{:S(2)}, u32[]{:S(2)}) collective-permute-start(f32[576,128]{1,0:T(8,128)S(1)} %get-tuple-element.18), channel_id=1, source_target_pairs={{0,2},{1,3},{2,0},{3,1},{4,6},{5,7},{6,4},{7,5},{8,10},{9,11},{10,... | collective-permute-start | bytes 884744 | tf_op jit(solution)/shard_map/ppermute | solution.py:495
  22.2 28.6 %copy-start = (bf16[128,3840]{1,0:T(8,128)(2,1)S(1)}, bf16[128,3840]{1,0:T(8,128)(2,1)}, u32[]{:S(2)}) copy-start(bf16[128,3840]{1,0:T(8,128)(2,1)} %x_ref.1) | copy-start | bytes 2949124
  22.2 28.6 %copy-start.1 = (f32[3840]{0:T(1024)S(1)}, f32[3840]{0:T(1024)}, u32[]{:S(2)}) copy-start(f32[3840]{0:T(1024)} %param.18) | copy-start | bytes 46084

commit v6 on v5

--- a/solution.py
+++ b/solution.py
@@ -348,10 +348,11 @@
             src_ref=s_all.at[ypeer, k], dst_ref=s_all.at[ypeer, k], send_sem=f_send.at[k], recv_sem=f_recv.at[k],
             device_id={'sp': partner}, device_id_type=MESH)
 
-    hop = 6
-    lag_r = hop * z
-    lag_l = hop * (3 - z)
-    lag_s = hop * (3 - (z * (3 - z)) // 2)
+    hop = 9
+    late = core * NC
+    lag_r = late + hop * z
+    lag_l = late + hop * (3 - z)
+    lag_s = late + hop * (3 - (z * (3 - z)) // 2)
 
     def tick(i, carry):
         @pl.when(i < NC)
@@ -402,7 +403,7 @@
 
         return carry
 
-    lax.fori_loop(0, NC + 4 * hop, tick, 0)
+    lax.fori_loop(0, 2 * NC + 4 * hop, tick, 0)
 
     def drain(k, carry):
         part_copy(k).wait()

time: 52.3 us -> 53.6 us (1.025)
  Pallas kernels: 48.2 us -> 49.5 us
    pallas_call x1, Pallas kernels: 28.6 us -> 29.9 us  [local_step(): pl.pallas_call(comm_kernel, out_shape=pltpu.VMEM((4, NC, OWN, CW), f32),...]
  transfers between devices with their start and end apart: 1 -> 1, of which waited for: 0 -> 0; matrix products, arithmetic and copies ran while one was open for 0% -> 0% of each run, Pallas kernels for 16% -> 15%
where the time goes in v6:
time: 53.6 us; the launch traced here: 53.3 us
  Pallas kernels  49.5 us (92%)
  starting transfers between devices  3.09 us (6%)
  between operations  0.7 us (1%)
    pallas_call x1, Pallas kernels, local_step(): pl.pallas_call(comm_kernel, out_shape=pltpu.VMEM((4, NC, OWN, CW), f32),...  29.9 us
    pallas_call x1, Pallas kernels, local_step(): pl.pallas_call(far_kernel, out_shape=(jax.ShapeDtypeStruct((8 * HP, LANES...  10.2 us
    pallas_call x1, Pallas kernels, local_step(): pl.pallas_call(near_kernel, out_shape=(pltpu.VMEM((8 * HP, LANES), f32),...  8.18 us
    ppermute x1, starting transfers between devices, local_step(): o_got = lax.ppermute(o_far, 'sp', [(0, 2), (1, 3), (2, 0), (3, 1)])  3.09 us
    pallas_call x1, Pallas kernels, local_step(): pl.pallas_call(finish_kernel, out_shape=jax.ShapeDtypeStruct((ROWS, DM),...  1.24 us
  transfers between devices with their start and end apart: 1, of which 0 were waited for; matrix products, arithmetic and copies ran while one was open for 0% of the time, Pallas kernels for 15%

profile of v6, /device:TPU:0, one launch (start us, length us, event | category | flops | bytes accessed | tf_op | source)
XLA Modules:
  0.0 53.3 jit_solution(4728429101746574331)
XLA Ops:
  0.6 10.2 %attend_far.1 = (f32[576,128]{1,0:T(8,128)S(1)}, bf16[64,256,128]{2,1,0:T(8,128)(2,1)S(1)}, bf16[64,256,128]{2,1,0:T(8,128)(2,1)S(1)}, f32[1088,128]{1,0:T(8,128...) custom-call(s32[128]{0:T(128)} %pos_h.3, s32[1,128]{1,0:T(1,128)} %bitcast.29, f32[1,128]{1,0:T(1,128)} %constant.5.freq_h, ...), custom_call_target="tpu_custom_call" | custom-call | flops 2000000000 | bytes 25000000 | tf_op jit(solution)/shard_map/attend_far/pallas_call | solution.py:477
  10.9 3.1 %collective-permute-start = (f32[576,128]{1,0:T(8,128)S(1)}, f32[576,128]{1,0:T(8,128)S(1)}, u32[]{:S(2)}, u32[]{:S(2)}) collective-permute-start(f32[576,128]{1,0:T(8,128)S(1)} %get-tuple-element.18), channel_id=1, source_target_pairs={{0,2},{1,3},{2,0},{3,1},{4,6},{5,7},{6,4},{7,5},{8,10},{9,11},{10,... | collective-permute-start | bytes 884744 | tf_op jit(solution)/shard_map/ppermute | solution.py:496
  14.0 8.2 %attend_near.1 = (f32[576,128]{1,0:T(8,128)S(1)}, bf16[128,256,128]{2,1,0:T(8,128)(2,1)}, bf16[128,256,128]{2,1,0:T(8,128)(2,1)}) custom-call(s32[128]{0:T(128)} %pos_h.3, f32[1088,128]{1,0:T(8,128)S(1)} %get-tuple-element.12.qs, f32[1088,128]{1,0:T(8,128)S(1)} %get-tuple-element.13.ks, f32[1088,128]{1,0:T(8,128)S(1)} %get-tuple-element.14.vs, ...), custom_call_target="tpu_custom_call" | custom-call | flops 10000000000 | bytes 25000000 | tf_op jit(solution)/shard_map/attend_near/pallas_call | solution.py:497
  22.2 0.0 copy-start
  22.2 0.0 copy-start.1
  22.2 0.0 collective-permute-done.o_got
  22.2 29.9 %combine.1.s_all = f32[4,15,32,256]{3,2,1,0:T(8,128)S(1)} custom-call(f32[576,128]{1,0:T(8,128)S(1)} %get-tuple-element.17.o_own, f32[576,128]{1,0:T(8,128)S(1)} %collective-permute-done.o_got, bf16[1024,3840]{1,0:T(8,128)(2,1)} %wo_h.1), custom_call_target="tpu_custom_call" | custom-call | tf_op jit(solution)/shard_map/combine/pallas_call | solution.py:512
  52.1 0.0 copy-done
  52.1 0.0 copy-done.1
  52.1 1.2 %finish.1 = bf16[128,3840]{1,0:T(8,128)(2,1)} custom-call(f32[4,15,32,256]{3,2,1,0:T(8,128)S(1)} %combine.1.s_all, bf16[128,3840]{1,0:T(8,128)(2,1)S(1)} %copy-done, f32[30,128]{1,0:T(8,128)S(1)} %bitcast.23), custom_call_target="tpu_custom_call" | custom-call | tf_op jit(solution)/shard_map/finish/pallas_call | solution.py:528
Async XLA Ops:
  10.9 11.3 %collective-permute-start = (f32[576,128]{1,0:T(8,128)S(1)}, f32[576,128]{1,0:T(8,128)S(1)}, u32[]{:S(2)}, u32[]{:S(2)}) collective-permute-start(f32[576,128]{1,0:T(8,128)S(1)} %get-tuple-element.18), channel_id=1, source_target_pairs={{0,2},{1,3},{2,0},{3,1},{4,6},{5,7},{6,4},{7,5},{8,10},{9,11},{10,... | collective-permute-start | bytes 884744 | tf_op jit(solution)/shard_map/ppermute | solution.py:496
  22.2 29.9 %copy-start = (bf16[128,3840]{1,0:T(8,128)(2,1)S(1)}, bf16[128,3840]{1,0:T(8,128)(2,1)}, u32[]{:S(2)}) copy-start(bf16[128,3840]{1,0:T(8,128)(2,1)} %x_ref.1) | copy-start | bytes 2949124
  22.2 29.9 %copy-start.1 = (f32[3840]{0:T(1024)S(1)}, f32[3840]{0:T(1024)}, u32[]{:S(2)}) copy-start(f32[3840]{0:T(1024)} %param.18) | copy-start | bytes 46084

commit v7 on v5

--- a/solution.py
+++ b/solution.py
@@ -106,27 +106,27 @@
 def far_kernel(pos_h, posv_h, freq_h, x_h, wpre_h, wq_h, wk_h, wv_h, kc_h, vc_h,
                o_ref, kbuf, vbuf, qs, ks, vs,
                pos_ref, posv, freq, wpre_ref, cos_ref, sin_ref, x_buf, a_buf, wq_buf, wk_buf, wv_buf, acc,
-               x_sem, s_sem, w_sem, ki_sem, vi_sem):
+               x_sem, s_sem, w_sem, ki_sem):
     row0 = (1 - lax.axis_index('sp') // 2) * HALF
 
     def w_start(c):
         rows = pl.ds(c * KC, KC)
         for n, (src, dst) in enumerate(((wk_h, wk_buf), (wv_h, wv_buf), (wq_h, wq_buf))):
-            pltpu.make_async_copy(src.at[rows, :], dst.at[rows, :], w_sem.at[3 * c + n]).start()
+            pltpu.make_async_copy(src.at[rows, :], dst.at[rows, :], w_sem.at[c]).start()
 
     def w_wait(c):
         rows = pl.ds(c * KC, KC)
         for n, (src, dst) in enumerate(((wk_h, wk_buf), (wv_h, wv_buf), (wq_h, wq_buf))):
-            pltpu.make_async_copy(src.at[rows, :], dst.at[rows, :], w_sem.at[3 * c + n]).wait()
+            pltpu.make_async_copy(src.at[rows, :], dst.at[rows, :], w_sem.at[c]).wait()
 
     def k_in(i):
         return pltpu.make_async_copy(kc_h.at[pl.ds(row0 + i * BCH, BCH)], kbuf.at[pl.ds(i * BCH, BCH)], ki_sem.at[i])
 
     def v_in(i):
-        return pltpu.make_async_copy(vc_h.at[pl.ds(row0 + i * BCH, BCH)], vbuf.at[pl.ds(i * BCH, BCH)], vi_sem.at[i])
-
-    small = [pltpu.make_async_copy(a, b, s_sem.at[i]) for i, (a, b) in enumerate(
-        ((wpre_h, wpre_ref), (posv_h, posv), (freq_h, freq), (pos_h, pos_ref)))]
+        return pltpu.make_async_copy(vc_h.at[pl.ds(row0 + i * BCH, BCH)], vbuf.at[pl.ds(i * BCH, BCH)], ki_sem.at[i])
+
+    small = [pltpu.make_async_copy(a, b, s_sem) for a, b in (
+        (wpre_h, wpre_ref), (posv_h, posv), (freq_h, freq), (pos_h, pos_ref))]
     for c in small:
         c.start()
     x_copy = pltpu.make_async_copy(x_h, x_buf, x_sem)
@@ -205,7 +205,7 @@
 
 def near_kernel(pos_h, qs, ks, vs, kfar, vfar, kc_h, vc_h,
                 o_ref, ko_h, vo_h,
-                pos_ref, kbuf, vbuf, p_sem, ki_sem, vi_sem, kw_sem, vw_sem, kf_sem, vf_sem):
+                pos_ref, kbuf, vbuf, p_sem, ki_sem, w_sem):
     yy = lax.axis_index('sp') // 2
     row0 = yy * HALF
     far0 = (1 - yy) * HALF
@@ -214,19 +214,19 @@
         return pltpu.make_async_copy(kc_h.at[pl.ds(row0 + i * BCH, BCH)], kbuf.at[pl.ds(i * BCH, BCH)], ki_sem.at[i])
 
     def v_in(i):
-        return pltpu.make_async_copy(vc_h.at[pl.ds(row0 + i * BCH, BCH)], vbuf.at[pl.ds(i * BCH, BCH)], vi_sem.at[i])
+        return pltpu.make_async_copy(vc_h.at[pl.ds(row0 + i * BCH, BCH)], vbuf.at[pl.ds(i * BCH, BCH)], ki_sem.at[i])
 
     def k_out(i):
-        return pltpu.make_async_copy(kbuf.at[pl.ds(i * BCH, BCH)], ko_h.at[pl.ds(row0 + i * BCH, BCH)], kw_sem.at[i])
+        return pltpu.make_async_copy(kbuf.at[pl.ds(i * BCH, BCH)], ko_h.at[pl.ds(row0 + i * BCH, BCH)], w_sem)
 
     def v_out(i):
-        return pltpu.make_async_copy(vbuf.at[pl.ds(i * BCH, BCH)], vo_h.at[pl.ds(row0 + i * BCH, BCH)], vw_sem.at[i])
+        return pltpu.make_async_copy(vbuf.at[pl.ds(i * BCH, BCH)], vo_h.at[pl.ds(row0 + i * BCH, BCH)], w_sem)
 
     def kf_out(i):
-        return pltpu.make_async_copy(kfar.at[pl.ds(i * BCH, BCH)], ko_h.at[pl.ds(far0 + i * BCH, BCH)], kf_sem.at[i])
+        return pltpu.make_async_copy(kfar.at[pl.ds(i * BCH, BCH)], ko_h.at[pl.ds(far0 + i * BCH, BCH)], w_sem)
 
     def vf_out(i):
-        return pltpu.make_async_copy(vfar.at[pl.ds(i * BCH, BCH)], vo_h.at[pl.ds(far0 + i * BCH, BCH)], vf_sem.at[i])
+        return pltpu.make_async_copy(vfar.at[pl.ds(i * BCH, BCH)], vo_h.at[pl.ds(far0 + i * BCH, BCH)], w_sem)
 
     p_copy = pltpu.make_async_copy(pos_h, pos_ref, p_sem)
     p_copy.start()
@@ -325,28 +325,31 @@
 
     def right_copy(k):
         return pltpu.make_async_remote_copy(
-            src_ref=sr.at[k], dst_ref=rr.at[k], send_sem=right_send.at[k], recv_sem=right_recv.at[k],
+            src_ref=sr.at[k], dst_ref=rr.at[k], send_sem=right_send, recv_sem=right_recv.at[k],
             device_id={'tp': z + 1}, device_id_type=MESH)
 
     def left_copy(k):
         return pltpu.make_async_remote_copy(
-            src_ref=sl.at[k], dst_ref=rl.at[k], send_sem=left_send.at[k], recv_sem=left_recv.at[k],
+            src_ref=sl.at[k], dst_ref=rl.at[k], send_sem=left_send, recv_sem=left_recv.at[k],
             device_id={'tp': z - 1}, device_id_type=MESH)
 
     def part_copy(k):
         return pltpu.make_async_remote_copy(
-            src_ref=s_all.at[sp, k], dst_ref=s_all.at[sp, k], send_sem=part_send.at[k], recv_sem=part_recv.at[k],
+            src_ref=s_all.at[sp, k], dst_ref=s_all.at[sp, k], send_sem=part_send, recv_sem=part_recv,
             device_id={'sp': partner}, device_id_type=MESH)
 
     def y_copy(k):
         return pltpu.make_async_remote_copy(
-            src_ref=s_all.at[sp, k], dst_ref=s_all.at[sp, k], send_sem=y_send.at[k], recv_sem=y_recv.at[k],
+            src_ref=s_all.at[sp, k], dst_ref=s_all.at[sp, k], send_sem=y_send, recv_sem=y_recv.at[k],
             device_id={'sp': ypeer}, device_id_type=MESH)
 
     def fwd_copy(k):
         return pltpu.make_async_remote_copy(
-            src_ref=s_all.at[ypeer, k], dst_ref=s_all.at[ypeer, k], send_sem=f_send.at[k], recv_sem=f_recv.at[k],
+            src_ref=s_all.at[ypeer, k], dst_ref=s_all.at[ypeer, k], send_sem=f_send, recv_sem=f_recv,
             device_id={'sp': partner}, device_id_type=MESH)
+
+    def whole(ref, sem):
+        return pltpu.make_async_copy(ref, ref, sem)
 
     hop = 6
     lag_r = hop * z
@@ -404,22 +407,19 @@
 
     lax.fori_loop(0, NC + 4 * hop, tick, 0)
 
-    def drain(k, carry):
-        part_copy(k).wait()
-        y_copy(k).wait_send()
-        fwd_copy(k).wait()
-
-        @pl.when(z < 3)
-        def _():
-            right_copy(k).wait_send()
-
-        @pl.when(z > 0)
-        def _():
-            left_copy(k).wait_send()
-
-        return carry
-
-    lax.fori_loop(0, NC, drain, 0)
+    @pl.when(z < 3)
+    def _():
+        whole(sr, right_send).wait()
+
+    @pl.when(z > 0)
+    def _():
+        whole(sl, left_send).wait()
+
+    whole(s_all.at[sp], y_send).wait()
+    whole(s_all.at[sp], part_send).wait()
+    whole(s_all.at[ypeer], f_send).wait()
+    whole(s_all.at[partner], part_recv).wait()
+    whole(s_all.at[3 - sp], f_recv).wait()
 
 
 def finish_kernel(s_all, x_ref, wpost_ref, out_h, out_buf, sem):
@@ -427,7 +427,7 @@
 
     def out_copy(i):
         rows = pl.ds(i * blk, blk)
-        return pltpu.make_async_copy(out_buf.at[rows], out_h.at[rows], sem.at[i])
+        return pltpu.make_async_copy(out_buf.at[rows], out_h.at[rows], sem)
 
     for i in range(ROWS // blk):
         g, r = (i * blk) // OWN, (i * blk) % OWN
@@ -485,7 +485,7 @@
                 pltpu.VMEM((DM // LANES, LANES), f32), pltpu.VMEM((ROWS, LANES), f32), pltpu.VMEM((ROWS, LANES), f32),
                 pltpu.VMEM((ROWS, DM), bf16), pltpu.VMEM((ROWS, DM), bf16),
                 pltpu.VMEM((DM, 1024), bf16), pltpu.VMEM((DM, 512), bf16), pltpu.VMEM((DM, 512), bf16), pltpu.VMEM((8, ROWS, HD), f32),
-                dma, dma((4,)), dma((3 * NKC,)), dma((NCH,)), dma((NCH,)),
+                dma, dma, dma((NKC,)), dma((NCH,)),
             ],
             compiler_params=pltpu.CompilerParams(vmem_limit_bytes=40 << 20),
             cost_estimate=pl.CostEstimate(flops=2 * 10 ** 9, bytes_accessed=25 * 10 ** 6, transcendentals=0),
@@ -501,7 +501,7 @@
             out_specs=(vmem, hbm, hbm),
             scratch_shapes=[
                 pltpu.SMEM((ROWS,), jnp.int32), pltpu.VMEM(half_shape, bf16), pltpu.VMEM(half_shape, bf16),
-                dma, dma((NCH,)), dma((NCH,)), dma((NCH,)), dma((NCH,)), dma((NCH,)), dma((NCH,)),
+                dma, dma((NCH,)), dma,
             ],
             compiler_params=pltpu.CompilerParams(vmem_limit_bytes=28 << 20),
             cost_estimate=pl.CostEstimate(flops=10 ** 10, bytes_accessed=25 * 10 ** 6, transcendentals=0),
@@ -518,8 +518,8 @@
                 pltpu.VMEM((8 * OWN, LANES), f32), pltpu.VMEM((8 * MP, LANES), f32), pltpu.VMEM((OWN, 1024), bf16),
                 big, big, big, big, big,
                 dma((NC,)), dma, dma,
-                dma((NC,)), dma((NC,)), dma((NC,)), dma((NC,)),
-                dma((NC,)), dma((NC,)), dma((NC,)), dma((NC,)), dma((NC,)), dma((NC,)),
+                dma, dma((NC,)), dma, dma((NC,)),
+                dma, dma, dma, dma((NC,)), dma, dma,
             ],
             compiler_params=pltpu.CompilerParams(vmem_limit_bytes=40 << 20, collective_id=0, has_side_effects=True),
             name='combine',
@@ -529,7 +529,7 @@
             out_shape=jax.ShapeDtypeStruct((ROWS, DM), bf16),
             in_specs=[vmem, vmem, vmem],
             out_specs=hbm,
-            scratch_shapes=[pltpu.VMEM((ROWS, DM), bf16), dma((ROWS // 16,))],
+            scratch_shapes=[pltpu.VMEM((ROWS, DM), bf16), dma],
             compiler_params=pltpu.CompilerParams(vmem_limit_bytes=16 << 20),
             name='finish',
         )(in_vmem(sums), x_in, w_post.reshape(DM // LANES, LANES))

time: 52.3 us -> 50.9 us (0.973)
  Pallas kernels: 48.2 us -> 47 us
    pallas_call x1, Pallas kernels: 28.6 us -> 27.7 us  [local_step(): pl.pallas_call(comm_kernel, out_shape=pltpu.VMEM((4, NC, OWN, CW), f32),...]
where the time goes in v7:
time: 50.9 us; the launch traced here: 50.8 us
  Pallas kernels  47 us (92%)
  starting transfers between devices  3.09 us (6%)
  between operations  0.7 us (1%)
    pallas_call x1, Pallas kernels, local_step(): pl.pallas_call(comm_kernel, out_shape=pltpu.VMEM((4, NC, OWN, CW), f32),...  27.7 us
    pallas_call x1, Pallas kernels, local_step(): pl.pallas_call(far_kernel, out_shape=(jax.ShapeDtypeStruct((8 * HP, LANES...  10.1 us
    pallas_call x1, Pallas kernels, local_step(): pl.pallas_call(near_kernel, out_shape=(pltpu.VMEM((8 * HP, LANES), f32),...  8.01 us
    ppermute x1, starting transfers between devices, local_step(): o_got = lax.ppermute(o_far, 'sp', [(0, 2), (1, 3), (2, 0), (3, 1)])  3.09 us
    pallas_call x1, Pallas kernels, local_step(): pl.pallas_call(finish_kernel, out_shape=jax.ShapeDtypeStruct((ROWS, DM),...  1.18 us
  transfers between devices with their start and end apart: 1, of which 0 were waited for; matrix products, arithmetic and copies ran while one was open for 0% of the time, Pallas kernels for 16%

profile of v7, /device:TPU:0, one launch (start us, length us, event | category | flops | bytes accessed | tf_op | source)
XLA Modules:
  0.0 50.8 jit_solution(17300173669877697378)
XLA Ops:
  0.6 10.1 %attend_far.1 = (f32[576,128]{1,0:T(8,128)S(1)}, bf16[64,256,128]{2,1,0:T(8,128)(2,1)S(1)}, bf16[64,256,128]{2,1,0:T(8,128)(2,1)S(1)}, f32[1088,128]{1,0:T(8,128...) custom-call(s32[128]{0:T(128)} %pos_h.3, s32[1,128]{1,0:T(1,128)} %bitcast.29, f32[1,128]{1,0:T(1,128)} %constant.5.freq_h, ...), custom_call_target="tpu_custom_call" | custom-call | flops 2000000000 | bytes 25000000 | tf_op jit(solution)/shard_map/attend_far/pallas_call | solution.py:476
  10.7 3.1 %collective-permute-start = (f32[576,128]{1,0:T(8,128)S(1)}, f32[576,128]{1,0:T(8,128)S(1)}, u32[]{:S(2)}, u32[]{:S(2)}) collective-permute-start(f32[576,128]{1,0:T(8,128)S(1)} %get-tuple-element.18), channel_id=1, source_target_pairs={{0,2},{1,3},{2,0},{3,1},{4,6},{5,7},{6,4},{7,5},{8,10},{9,11},{10,... | collective-permute-start | bytes 884744 | tf_op jit(solution)/shard_map/ppermute | solution.py:495
  13.8 8.0 %attend_near.1 = (f32[576,128]{1,0:T(8,128)S(1)}, bf16[128,256,128]{2,1,0:T(8,128)(2,1)}, bf16[128,256,128]{2,1,0:T(8,128)(2,1)}) custom-call(s32[128]{0:T(128)} %pos_h.3, f32[1088,128]{1,0:T(8,128)S(1)} %get-tuple-element.12.qs, f32[1088,128]{1,0:T(8,128)S(1)} %get-tuple-element.13.ks, f32[1088,128]{1,0:T(8,128)S(1)} %get-tuple-element.14.vs, ...), custom_call_target="tpu_custom_call" | custom-call | flops 10000000000 | bytes 25000000 | tf_op jit(solution)/shard_map/attend_near/pallas_call | solution.py:496
  21.8 0.0 copy-start
  21.8 0.0 copy-start.1
  21.9 0.0 collective-permute-done.o_got
  21.9 27.7 %combine.1.s_all = f32[4,15,32,256]{3,2,1,0:T(8,128)S(1)} custom-call(f32[576,128]{1,0:T(8,128)S(1)} %get-tuple-element.17.o_own, f32[576,128]{1,0:T(8,128)S(1)} %collective-permute-done.o_got, bf16[1024,3840]{1,0:T(8,128)(2,1)} %wo_h.1), custom_call_target="tpu_custom_call" | custom-call | tf_op jit(solution)/shard_map/combine/pallas_call | solution.py:511
  49.6 0.0 copy-done
  49.6 0.0 copy-done.1
  49.6 1.2 %finish.1 = bf16[128,3840]{1,0:T(8,128)(2,1)} custom-call(f32[4,15,32,256]{3,2,1,0:T(8,128)S(1)} %combine.1.s_all, bf16[128,3840]{1,0:T(8,128)(2,1)S(1)} %copy-done, f32[30,128]{1,0:T(8,128)S(1)} %bitcast.23), custom_call_target="tpu_custom_call" | custom-call | tf_op jit(solution)/shard_map/finish/pallas_call | solution.py:527
Async XLA Ops:
  10.7 11.1 %collective-permute-start = (f32[576,128]{1,0:T(8,128)S(1)}, f32[576,128]{1,0:T(8,128)S(1)}, u32[]{:S(2)}, u32[]{:S(2)}) collective-permute-start(f32[576,128]{1,0:T(8,128)S(1)} %get-tuple-element.18), channel_id=1, source_target_pairs={{0,2},{1,3},{2,0},{3,1},{4,6},{5,7},{6,4},{7,5},{8,10},{9,11},{10,... | collective-permute-start | bytes 884744 | tf_op jit(solution)/shard_map/ppermute | solution.py:495
  21.8 27.7 %copy-start = (bf16[128,3840]{1,0:T(8,128)(2,1)S(1)}, bf16[128,3840]{1,0:T(8,128)(2,1)}, u32[]{:S(2)}) copy-start(bf16[128,3840]{1,0:T(8,128)(2,1)} %x_ref.1) | copy-start | bytes 2949124
  21.8 27.7 %copy-start.1 = (f32[3840]{0:T(1024)S(1)}, f32[3840]{0:T(1024)}, u32[]{:S(2)}) copy-start(f32[3840]{0:T(1024)} %param.18) | copy-start | bytes 46084

commit v8 on v7

--- a/solution.py
+++ b/solution.py
@@ -25,7 +25,7 @@
 KC = 768
 NKC = DM // KC
 SHIFT = 20.0
-CW = 256
+CW = 384
 NC = DM // CW
 OWN = 32
 MP = 40
@@ -351,7 +351,7 @@
     def whole(ref, sem):
         return pltpu.make_async_copy(ref, ref, sem)
 
-    hop = 6
+    hop = 4
     lag_r = hop * z
     lag_l = hop * (3 - z)
     lag_s = hop * (3 - (z * (3 - z)) // 2)

time: 50.9 us -> 51.5 us (1.012)
    pallas_call x1, Pallas kernels: 27.7 us -> 28.2 us  [local_step(): pl.pallas_call(comm_kernel, out_shape=pltpu.VMEM((4, NC, OWN, CW), f32),...]
where the time goes in v8:
time: 51.5 us; the launch traced here: 51.3 us
  Pallas kernels  47.5 us (92%)
  starting transfers between devices  3.09 us (6%)
  between operations  0.7 us (1%)
    pallas_call x1, Pallas kernels, local_step(): pl.pallas_call(comm_kernel, out_shape=pltpu.VMEM((4, NC, OWN, CW), f32),...  28.2 us
    pallas_call x1, Pallas kernels, local_step(): pl.pallas_call(far_kernel, out_shape=(jax.ShapeDtypeStruct((8 * HP, LANES...  10.1 us
    pallas_call x1, Pallas kernels, local_step(): pl.pallas_call(near_kernel, out_shape=(pltpu.VMEM((8 * HP, LANES), f32),...  8.01 us
    ppermute x1, starting transfers between devices, local_step(): o_got = lax.ppermute(o_far, 'sp', [(0, 2), (1, 3), (2, 0), (3, 1)])  3.09 us
    pallas_call x1, Pallas kernels, local_step(): pl.pallas_call(finish_kernel, out_shape=jax.ShapeDtypeStruct((ROWS, DM),...  1.18 us
  transfers between devices with their start and end apart: 1, of which 0 were waited for; matrix products, arithmetic and copies ran while one was open for 0% of the time, Pallas kernels for 16%

profile of v8, /device:TPU:0, one launch (start us, length us, event | category | flops | bytes accessed | tf_op | source)
XLA Modules:
  0.0 51.3 jit_solution(5661208544115989294)
XLA Ops:
  0.6 10.1 %attend_far.1 = (f32[576,128]{1,0:T(8,128)S(1)}, bf16[64,256,128]{2,1,0:T(8,128)(2,1)S(1)}, bf16[64,256,128]{2,1,0:T(8,128)(2,1)S(1)}, f32[1088,128]{1,0:T(8,128...) custom-call(s32[128]{0:T(128)} %pos_h.3, s32[1,128]{1,0:T(1,128)} %bitcast.29, f32[1,128]{1,0:T(1,128)} %constant.5.freq_h, ...), custom_call_target="tpu_custom_call" | custom-call | flops 2000000000 | bytes 25000000 | tf_op jit(solution)/shard_map/attend_far/pallas_call | solution.py:476
  10.7 3.1 %collective-permute-start = (f32[576,128]{1,0:T(8,128)S(1)}, f32[576,128]{1,0:T(8,128)S(1)}, u32[]{:S(2)}, u32[]{:S(2)}) collective-permute-start(f32[576,128]{1,0:T(8,128)S(1)} %get-tuple-element.18), channel_id=1, source_target_pairs={{0,2},{1,3},{2,0},{3,1},{4,6},{5,7},{6,4},{7,5},{8,10},{9,11},{10,... | collective-permute-start | bytes 884744 | tf_op jit(solution)/shard_map/ppermute | solution.py:495
  13.8 8.0 %attend_near.1 = (f32[576,128]{1,0:T(8,128)S(1)}, bf16[128,256,128]{2,1,0:T(8,128)(2,1)}, bf16[128,256,128]{2,1,0:T(8,128)(2,1)}) custom-call(s32[128]{0:T(128)} %pos_h.3, f32[1088,128]{1,0:T(8,128)S(1)} %get-tuple-element.12.qs, f32[1088,128]{1,0:T(8,128)S(1)} %get-tuple-element.13.ks, f32[1088,128]{1,0:T(8,128)S(1)} %get-tuple-element.14.vs, ...), custom_call_target="tpu_custom_call" | custom-call | flops 10000000000 | bytes 25000000 | tf_op jit(solution)/shard_map/attend_near/pallas_call | solution.py:496
  21.8 0.0 copy-start
  21.8 0.0 copy-start.1
  21.9 0.0 collective-permute-done.o_got
  21.9 28.2 %combine.1.s_all = f32[4,10,32,384]{3,2,1,0:T(8,128)S(1)} custom-call(f32[576,128]{1,0:T(8,128)S(1)} %get-tuple-element.17.o_own, f32[576,128]{1,0:T(8,128)S(1)} %collective-permute-done.o_got, bf16[1024,3840]{1,0:T(8,128)(2,1)} %wo_h.1), custom_call_target="tpu_custom_call" | custom-call | tf_op jit(solution)/shard_map/combine/pallas_call | solution.py:511
  50.1 0.0 copy-done
  50.1 0.0 copy-done.1
  50.1 1.2 %finish.1 = bf16[128,3840]{1,0:T(8,128)(2,1)} custom-call(f32[4,10,32,384]{3,2,1,0:T(8,128)S(1)} %combine.1.s_all, bf16[128,3840]{1,0:T(8,128)(2,1)S(1)} %copy-done, f32[30,128]{1,0:T(8,128)S(1)} %bitcast.23), custom_call_target="tpu_custom_call" | custom-call | tf_op jit(solution)/shard_map/finish/pallas_call | solution.py:527
Async XLA Ops:
  10.7 11.1 %collective-permute-start = (f32[576,128]{1,0:T(8,128)S(1)}, f32[576,128]{1,0:T(8,128)S(1)}, u32[]{:S(2)}, u32[]{:S(2)}) collective-permute-start(f32[576,128]{1,0:T(8,128)S(1)} %get-tuple-element.18), channel_id=1, source_target_pairs={{0,2},{1,3},{2,0},{3,1},{4,6},{5,7},{6,4},{7,5},{8,10},{9,11},{10,... | collective-permute-start | bytes 884744 | tf_op jit(solution)/shard_map/ppermute | solution.py:495
  21.8 28.3 %copy-start = (bf16[128,3840]{1,0:T(8,128)(2,1)S(1)}, bf16[128,3840]{1,0:T(8,128)(2,1)}, u32[]{:S(2)}) copy-start(bf16[128,3840]{1,0:T(8,128)(2,1)} %x_ref.1) | copy-start | bytes 2949124
  21.8 28.3 %copy-start.1 = (f32[3840]{0:T(1024)S(1)}, f32[3840]{0:T(1024)}, u32[]{:S(2)}) copy-start(f32[3840]{0:T(1024)} %param.18) | copy-start | bytes 46084

commit v9 on v7

--- a/solution.py
+++ b/solution.py
@@ -27,6 +27,7 @@
 SHIFT = 20.0
 CW = 256
 NC = DM // CW
+WG = 3
 OWN = 32
 MP = 40
 MESH = pl.DeviceIdType.MESH
@@ -265,9 +266,9 @@
     ypeer = (sp + 2) % 4
 
     def wo_copy(k):
-        return pltpu.make_async_copy(wo_h.at[:, pl.ds(pl.multiple_of(k * CW, CW), CW)], wo_buf.at[k], w_sem.at[k])
-
-    for k in range(NC):
+        return pltpu.make_async_copy(wo_h.at[:, pl.ds(pl.multiple_of(k * WG * CW, CW), WG * CW)], wo_buf.at[k], w_sem.at[k])
+
+    for k in range(NC // WG):
         wo_copy(k).start()
 
     @pl.when(z == 0)
@@ -351,7 +352,7 @@
     def whole(ref, sem):
         return pltpu.make_async_copy(ref, ref, sem)
 
-    hop = 6
+    hop = 5
     lag_r = hop * z
     lag_l = hop * (3 - z)
     lag_s = hop * (3 - (z * (3 - z)) // 2)
@@ -359,8 +360,14 @@
     def tick(i, carry):
         @pl.when(i < NC)
         def _():
-            wo_copy(i).wait()
-            p_buf[i] = jnp.dot(lhs[...], wo_buf[i], preferred_element_type=jnp.float32)
+            group, place = i // WG, i % WG
+
+            @pl.when(place == 0)
+            def _():
+                wo_copy(group).wait()
+
+            w_c = wo_buf[group, :, pl.ds(pl.multiple_of(place * CW, CW), CW)]
+            p_buf[i] = jnp.dot(lhs[...], w_c, preferred_element_type=jnp.float32)
 
         kr = i - lag_r
 
@@ -514,10 +521,10 @@
             in_specs=[vmem, vmem, hbm],
             out_specs=vmem,
             scratch_shapes=[
-                pltpu.VMEM((NC, 1024, CW), bf16), pltpu.VMEM((4, LANES, LANES), f32), pltpu.VMEM((8 * MP, LANES), f32),
+                pltpu.VMEM((NC // WG, 1024, WG * CW), bf16), pltpu.VMEM((4, LANES, LANES), f32), pltpu.VMEM((8 * MP, LANES), f32),
                 pltpu.VMEM((8 * OWN, LANES), f32), pltpu.VMEM((8 * MP, LANES), f32), pltpu.VMEM((OWN, 1024), bf16),
                 big, big, big, big, big,
-                dma((NC,)), dma, dma,
+                dma((NC // WG,)), dma, dma,
                 dma, dma((NC,)), dma, dma((NC,)),
                 dma, dma, dma, dma((NC,)), dma, dma,
             ],

time: 50.9 us -> 50.8 us (level)
  no operation moved by 1% of the time
where the time goes in v9:
time: 50.8 us; the launch traced here: 50.7 us
  Pallas kernels  46.9 us (92%)
  starting transfers between devices  3.09 us (6%)
  between operations  0.7 us (1%)
    pallas_call x1, Pallas kernels, local_step(): pl.pallas_call(comm_kernel, out_shape=pltpu.VMEM((4, NC, OWN, CW), f32),...  27.6 us
    pallas_call x1, Pallas kernels, local_step(): pl.pallas_call(far_kernel, out_shape=(jax.ShapeDtypeStruct((8 * HP, LANES...  10.1 us
    pallas_call x1, Pallas kernels, local_step(): pl.pallas_call(near_kernel, out_shape=(pltpu.VMEM((8 * HP, LANES), f32),...  8.01 us
    ppermute x1, starting transfers between devices, local_step(): o_got = lax.ppermute(o_far, 'sp', [(0, 2), (1, 3), (2, 0), (3, 1)])  3.09 us
    pallas_call x1, Pallas kernels, local_step(): pl.pallas_call(finish_kernel, out_shape=jax.ShapeDtypeStruct((ROWS, DM),...  1.18 us
  transfers between devices with their start and end apart: 1, of which 0 were waited for; matrix products, arithmetic and copies ran while one was open for 0% of the time, Pallas kernels for 16%

profile of v9, /device:TPU:0, one launch (start us, length us, event | category | flops | bytes accessed | tf_op | source)
XLA Modules:
  0.0 50.7 jit_solution(5518625402032466622)
XLA Ops:
  0.6 10.1 %attend_far.1 = (f32[576,128]{1,0:T(8,128)S(1)}, bf16[64,256,128]{2,1,0:T(8,128)(2,1)S(1)}, bf16[64,256,128]{2,1,0:T(8,128)(2,1)S(1)}, f32[1088,128]{1,0:T(8,128...) custom-call(s32[128]{0:T(128)} %pos_h.3, s32[1,128]{1,0:T(1,128)} %bitcast.29, f32[1,128]{1,0:T(1,128)} %constant.5.freq_h, ...), custom_call_target="tpu_custom_call" | custom-call | flops 2000000000 | bytes 25000000 | tf_op jit(solution)/shard_map/attend_far/pallas_call | solution.py:483
  10.7 3.1 %collective-permute-start = (f32[576,128]{1,0:T(8,128)S(1)}, f32[576,128]{1,0:T(8,128)S(1)}, u32[]{:S(2)}, u32[]{:S(2)}) collective-permute-start(f32[576,128]{1,0:T(8,128)S(1)} %get-tuple-element.18), channel_id=1, source_target_pairs={{0,2},{1,3},{2,0},{3,1},{4,6},{5,7},{6,4},{7,5},{8,10},{9,11},{10,... | collective-permute-start | bytes 884744 | tf_op jit(solution)/shard_map/ppermute | solution.py:502
  13.8 8.0 %attend_near.1 = (f32[576,128]{1,0:T(8,128)S(1)}, bf16[128,256,128]{2,1,0:T(8,128)(2,1)}, bf16[128,256,128]{2,1,0:T(8,128)(2,1)}) custom-call(s32[128]{0:T(128)} %pos_h.3, f32[1088,128]{1,0:T(8,128)S(1)} %get-tuple-element.12.qs, f32[1088,128]{1,0:T(8,128)S(1)} %get-tuple-element.13.ks, f32[1088,128]{1,0:T(8,128)S(1)} %get-tuple-element.14.vs, ...), custom_call_target="tpu_custom_call" | custom-call | flops 10000000000 | bytes 25000000 | tf_op jit(solution)/shard_map/attend_near/pallas_call | solution.py:503
  21.8 0.0 copy-start
  21.8 0.0 copy-start.1
  21.9 0.0 collective-permute-done.o_got
  21.9 27.6 %combine.1.s_all = f32[4,15,32,256]{3,2,1,0:T(8,128)S(1)} custom-call(f32[576,128]{1,0:T(8,128)S(1)} %get-tuple-element.17.o_own, f32[576,128]{1,0:T(8,128)S(1)} %collective-permute-done.o_got, bf16[1024,3840]{1,0:T(8,128)(2,1)} %wo_h.1), custom_call_target="tpu_custom_call" | custom-call | tf_op jit(solution)/shard_map/combine/pallas_call | solution.py:518
  49.5 0.0 copy-done
  49.5 0.0 copy-done.1
  49.5 1.2 %finish.1 = bf16[128,3840]{1,0:T(8,128)(2,1)} custom-call(f32[4,15,32,256]{3,2,1,0:T(8,128)S(1)} %combine.1.s_all, bf16[128,3840]{1,0:T(8,128)(2,1)S(1)} %copy-done, f32[30,128]{1,0:T(8,128)S(1)} %bitcast.23), custom_call_target="tpu_custom_call" | custom-call | tf_op jit(solution)/shard_map/finish/pallas_call | solution.py:534
Async XLA Ops:
  10.7 11.1 %collective-permute-start = (f32[576,128]{1,0:T(8,128)S(1)}, f32[576,128]{1,0:T(8,128)S(1)}, u32[]{:S(2)}, u32[]{:S(2)}) collective-permute-start(f32[576,128]{1,0:T(8,128)S(1)} %get-tuple-element.18), channel_id=1, source_target_pairs={{0,2},{1,3},{2,0},{3,1},{4,6},{5,7},{6,4},{7,5},{8,10},{9,11},{10,... | collective-permute-start | bytes 884744 | tf_op jit(solution)/shard_map/ppermute | solution.py:502
  21.8 27.6 %copy-start = (bf16[128,3840]{1,0:T(8,128)(2,1)S(1)}, bf16[128,3840]{1,0:T(8,128)(2,1)}, u32[]{:S(2)}) copy-start(bf16[128,3840]{1,0:T(8,128)(2,1)} %x_ref.1) | copy-start | bytes 2949124
  21.8 27.6 %copy-start.1 = (f32[3840]{0:T(1024)S(1)}, f32[3840]{0:T(1024)}, u32[]{:S(2)}) copy-start(f32[3840]{0:T(1024)} %param.18) | copy-start | bytes 46084

commit v10 on v9

--- a/solution.py
+++ b/solution.py
@@ -20,7 +20,7 @@
 LANES = 128
 BCH = 16
 HALF = ROWS // 2
-HP = 72
+HROWS = 8 * HALF + 8
 NCH = HALF // BCH
 KC = 768
 NKC = DM // KC
@@ -29,7 +29,7 @@
 NC = DM // CW
 WG = 3
 OWN = 32
-MP = 40
+MROWS = 8 * OWN + 8
 MESH = pl.DeviceIdType.MESH
 
 
@@ -95,13 +95,13 @@
             lb = i * BCH + u
             vv = jnp.concatenate([vbuf[lb], vbuf[lb + 1]], 1)
             o = jnp.dot(weights[u // 2], vv, preferred_element_type=jnp.float32)
-            o_ref[pl.ds(lb, 8, stride=HP), :] = o[0:8, 0:LANES]
-            o_ref[pl.ds(lb + 1, 8, stride=HP), :] = o[8:16, LANES:]
+            o_ref[pl.ds(lb, 8, stride=HALF), :] = o[0:8, 0:LANES]
+            o_ref[pl.ds(lb + 1, 8, stride=HALF), :] = o[8:16, LANES:]
         after(i)
         return l_acc
 
     l_acc = lax.fori_loop(0, nchunk, chunk, zero)
-    o_ref[pl.ds(HALF, 8, stride=HP), :] = l_acc
+    o_ref[pl.ds(8 * HALF, 8), :] = l_acc
 
 
 def far_kernel(pos_h, posv_h, freq_h, x_h, wpre_h, wq_h, wk_h, wv_h, kc_h, vc_h,
@@ -158,8 +158,8 @@
         w_wait(c)
         if c + 3 < NKC:
             w_start(c + 3)
-        else:
-            for n in range(2 * (c + 3 - NKC), min(NCH, 2 * (c + 4 - NKC))):
+        if c >= NKC - 2:
+            for n in range(2 * (c + 2 - NKC), 2 * (c + 3 - NKC)):
                 k_in(n).start()
                 v_in(n).start()
         rows = slice(c * KC, (c + 1) * KC)
@@ -302,26 +302,26 @@
 
     mine = pl.multiple_of(core * OWN, OWN)
     theirs = pl.multiple_of((1 - core) * OWN, OWN)
-    tot = shares(o_own[pl.ds(HALF, 8, stride=HP), :], o_got[pl.ds(HALF, 8, stride=HP), :], 0)
-
-    def merge_half(r0, dst, stride):
+    tot = shares(o_own[pl.ds(8 * HALF, 8), :], o_got[pl.ds(8 * HALF, 8), :], 0)
+
+    def merge_half(r0, dst):
         fa, fb = fac[0, pl.ds(r0, OWN), :], fac[1, pl.ds(r0, OWN), :]
         for j in range(8):
-            rows = pl.ds(pl.multiple_of(j * HP + r0, 8), OWN)
-            dst[pl.ds(j * stride, OWN), :] = o_own[rows, :] * fa[:, j:j + 1] + o_got[rows, :] * fb[:, j:j + 1]
-
-    merge_half(theirs, m1, MP)
-    m1[pl.ds(OWN, 8, stride=MP), :] = tot
+            rows = pl.ds(pl.multiple_of(j * HALF + r0, 8), OWN)
+            dst[pl.ds(j * OWN, OWN), :] = o_own[rows, :] * fa[:, j:j + 1] + o_got[rows, :] * fb[:, j:j + 1]
+
+    merge_half(theirs, m1)
+    m1[pl.ds(8 * OWN, 8), :] = tot
     pair = pltpu.make_async_remote_copy(
         src_ref=m1, dst_ref=r1, send_sem=r1_send, recv_sem=r1_recv, device_id={'sp': partner}, device_id_type=MESH)
     pair.start()
-    merge_half(mine, m2, OWN)
+    merge_half(mine, m2)
     pair.wait()
-    shares(tot, r1[pl.ds(OWN, 8, stride=MP), :], 2)
+    shares(tot, r1[pl.ds(8 * OWN, 8), :], 2)
     fa, fb = fac[2, pl.ds(mine, OWN), :], fac[3, pl.ds(mine, OWN), :]
     for j in range(8):
         c, hq = j // 4, j % 4
-        val = m2[j * OWN:(j + 1) * OWN, :] * fa[:, j:j + 1] + r1[j * MP:j * MP + OWN, :] * fb[:, j:j + 1]
+        val = m2[j * OWN:(j + 1) * OWN, :] * fa[:, j:j + 1] + r1[j * OWN:(j + 1) * OWN, :] * fb[:, j:j + 1]
         lhs[:, (hq * 2 + c) * LANES:(hq * 2 + c + 1) * LANES] = val.astype(jnp.bfloat16)
 
     def right_copy(k):
@@ -482,7 +482,7 @@
         half_shape = (HALF,) + kr.shape[1:]
         o_far, k_far, v_far, qs, ks, vs = pl.pallas_call(
             far_kernel,
-            out_shape=(jax.ShapeDtypeStruct((8 * HP, LANES), f32),
+            out_shape=(jax.ShapeDtypeStruct((HROWS, LANES), f32),
                        pltpu.VMEM(half_shape, bf16), pltpu.VMEM(half_shape, bf16),
                        pltpu.VMEM((8 * RP, LANES), f32), pltpu.VMEM((8 * RP, LANES), f32), pltpu.VMEM((8 * RP, LANES), f32)),
             in_specs=[hbm] * 10,
@@ -502,7 +502,7 @@
         o_got = lax.ppermute(o_far, 'sp', [(0, 2), (1, 3), (2, 0), (3, 1)])
         o_own, k_new, v_new = pl.pallas_call(
             near_kernel,
-            out_shape=(pltpu.VMEM((8 * HP, LANES), f32),
+            out_shape=(pltpu.VMEM((HROWS, LANES), f32),
                        jax.ShapeDtypeStruct(kr.shape, bf16), jax.ShapeDtypeStruct(vr.shape, bf16)),
             in_specs=[hbm, vmem, vmem, vmem, vmem, vmem, hbm, hbm],
             out_specs=(vmem, hbm, hbm),
@@ -521,8 +521,8 @@
             in_specs=[vmem, vmem, hbm],
             out_specs=vmem,
             scratch_shapes=[
-                pltpu.VMEM((NC // WG, 1024, WG * CW), bf16), pltpu.VMEM((4, LANES, LANES), f32), pltpu.VMEM((8 * MP, LANES), f32),
-                pltpu.VMEM((8 * OWN, LANES), f32), pltpu.VMEM((8 * MP, LANES), f32), pltpu.VMEM((OWN, 1024), bf16),
+                pltpu.VMEM((NC // WG, 1024, WG * CW), bf16), pltpu.VMEM((4, LANES, LANES), f32), pltpu.VMEM((MROWS, LANES), f32),
+                pltpu.VMEM((8 * OWN, LANES), f32), pltpu.VMEM((MROWS, LANES), f32), pltpu.VMEM((OWN, 1024), bf16),
                 big, big, big, big, big,
                 dma((NC // WG,)), dma, dma,
                 dma, dma((NC,)), dma, dma((NC,)),

time: 50.8 us -> 51.1 us (level)
  no operation moved by 1% of the time
where the time goes in v10:
time: 51.1 us; the launch traced here: 51 us
  Pallas kernels  47.2 us (92%)
  starting transfers between devices  3.09 us (6%)
  between operations  0.7 us (1%)
    pallas_call x1, Pallas kernels, local_step(): pl.pallas_call(comm_kernel, out_shape=pltpu.VMEM((4, NC, OWN, CW), f32),...  27.5 us
    pallas_call x1, Pallas kernels, local_step(): pl.pallas_call(far_kernel, out_shape=(jax.ShapeDtypeStruct((HROWS, LANES)...  10.4 us
    pallas_call x1, Pallas kernels, local_step(): pl.pallas_call(near_kernel, out_shape=(pltpu.VMEM((HROWS, LANES), f32), j...  8.01 us
    ppermute x1, starting transfers between devices, local_step(): o_got = lax.ppermute(o_far, 'sp', [(0, 2), (1, 3), (2, 0), (3, 1)])  3.09 us
    pallas_call x1, Pallas kernels, local_step(): pl.pallas_call(finish_kernel, out_shape=jax.ShapeDtypeStruct((ROWS, DM),...  1.21 us
  transfers between devices with their start and end apart: 1, of which 0 were waited for; matrix products, arithmetic and copies ran while one was open for 0% of the time, Pallas kernels for 16%

profile of v10, /device:TPU:0, one launch (start us, length us, event | category | flops | bytes accessed | tf_op | source)
XLA Modules:
  0.0 51.0 jit_solution(7092060234573432540)
XLA Ops:
  0.6 10.4 %attend_far.1 = (f32[520,128]{1,0:T(8,128)S(1)}, bf16[64,256,128]{2,1,0:T(8,128)(2,1)S(1)}, bf16[64,256,128]{2,1,0:T(8,128)(2,1)S(1)}, f32[1088,128]{1,0:T(8,128...) custom-call(s32[128]{0:T(128)} %pos_h.3, s32[1,128]{1,0:T(1,128)} %bitcast.29, f32[1,128]{1,0:T(1,128)} %constant.5.freq_h, ...), custom_call_target="tpu_custom_call" | custom-call | flops 2000000000 | bytes 25000000 | tf_op jit(solution)/shard_map/attend_far/pallas_call | solution.py:483
  11.0 3.1 %collective-permute-start = (f32[520,128]{1,0:T(8,128)S(1)}, f32[520,128]{1,0:T(8,128)S(1)}, u32[]{:S(2)}, u32[]{:S(2)}) collective-permute-start(f32[520,128]{1,0:T(8,128)S(1)} %get-tuple-element.18), channel_id=1, source_target_pairs={{0,2},{1,3},{2,0},{3,1},{4,6},{5,7},{6,4},{7,5},{8,10},{9,11},{10,... | collective-permute-start | bytes 798728 | tf_op jit(solution)/shard_map/ppermute | solution.py:502
  14.1 8.0 %attend_near.1 = (f32[520,128]{1,0:T(8,128)S(1)}, bf16[128,256,128]{2,1,0:T(8,128)(2,1)}, bf16[128,256,128]{2,1,0:T(8,128)(2,1)}) custom-call(s32[128]{0:T(128)} %pos_h.3, f32[1088,128]{1,0:T(8,128)S(1)} %get-tuple-element.12.qs, f32[1088,128]{1,0:T(8,128)S(1)} %get-tuple-element.13.ks, f32[1088,128]{1,0:T(8,128)S(1)} %get-tuple-element.14.vs, ...), custom_call_target="tpu_custom_call" | custom-call | flops 10000000000 | bytes 25000000 | tf_op jit(solution)/shard_map/attend_near/pallas_call | solution.py:503
  22.2 0.0 copy-start
  22.2 0.0 copy-start.1
  22.2 0.0 collective-permute-done.o_got
  22.2 27.5 %combine.1.s_all = f32[4,15,32,256]{3,2,1,0:T(8,128)S(1)} custom-call(f32[520,128]{1,0:T(8,128)S(1)} %get-tuple-element.17.o_own, f32[520,128]{1,0:T(8,128)S(1)} %collective-permute-done.o_got, bf16[1024,3840]{1,0:T(8,128)(2,1)} %wo_h.1), custom_call_target="tpu_custom_call" | custom-call | tf_op jit(solution)/shard_map/combine/pallas_call | solution.py:518
  49.7 0.0 copy-done
  49.8 0.0 copy-done.1
  49.8 1.2 %finish.1 = bf16[128,3840]{1,0:T(8,128)(2,1)} custom-call(f32[4,15,32,256]{3,2,1,0:T(8,128)S(1)} %combine.1.s_all, bf16[128,3840]{1,0:T(8,128)(2,1)S(1)} %copy-done, f32[30,128]{1,0:T(8,128)S(1)} %bitcast.23), custom_call_target="tpu_custom_call" | custom-call | tf_op jit(solution)/shard_map/finish/pallas_call | solution.py:534
Async XLA Ops:
  11.0 11.1 %collective-permute-start = (f32[520,128]{1,0:T(8,128)S(1)}, f32[520,128]{1,0:T(8,128)S(1)}, u32[]{:S(2)}, u32[]{:S(2)}) collective-permute-start(f32[520,128]{1,0:T(8,128)S(1)} %get-tuple-element.18), channel_id=1, source_target_pairs={{0,2},{1,3},{2,0},{3,1},{4,6},{5,7},{6,4},{7,5},{8,10},{9,11},{10,... | collective-permute-start | bytes 798728 | tf_op jit(solution)/shard_map/ppermute | solution.py:502
  22.2 27.6 %copy-start = (bf16[128,3840]{1,0:T(8,128)(2,1)S(1)}, bf16[128,3840]{1,0:T(8,128)(2,1)}, u32[]{:S(2)}) copy-start(bf16[128,3840]{1,0:T(8,128)(2,1)} %x_ref.1) | copy-start | bytes 2949124
  22.2 27.6 %copy-start.1 = (f32[3840]{0:T(1024)S(1)}, f32[3840]{0:T(1024)}, u32[]{:S(2)}) copy-start(f32[3840]{0:T(1024)} %param.18) | copy-start | bytes 46084

commit v11 on v10

--- a/solution.py
+++ b/solution.py
@@ -132,16 +132,18 @@
         c.start()
     x_copy = pltpu.make_async_copy(x_h, x_buf, x_sem)
     x_copy.start()
-    w_start(0)
+    for c in range(NKC):
+        w_start(c)
+    for n in range(NCH):
+        k_in(n).start()
+        v_in(n).start()
     for c in small:
         c.wait()
-    w_start(1)
     pos_col = jnp.broadcast_to(posv[...].astype(jnp.float32), (ROWS, LANES)).T
     ang = pos_col * freq[...]
     cos_ref[...] = jnp.cos(ang)
     sin_ref[...] = jnp.sin(ang)
     x_copy.wait()
-    w_start(2)
 
     gain = 1.0 + jnp.concatenate([wpre_ref[k:k + 1, :] for k in range(DM // LANES)], 1)
 
@@ -156,12 +158,6 @@
 
     for c in range(NKC):
         w_wait(c)
-        if c + 3 < NKC:
-            w_start(c + 3)
-        if c >= NKC - 2:
-            for n in range(2 * (c + 2 - NKC), 2 * (c + 3 - NKC)):
-                k_in(n).start()
-                v_in(n).start()
         rows = slice(c * KC, (c + 1) * KC)
         a_c = a_buf[:, rows]
         for i in range(8):

time: 51.1 us -> 56 us (1.096)
  Pallas kernels: 47.2 us -> 52.1 us
    pallas_call x1, Pallas kernels: 10.4 us -> 15.3 us  [local_step(): pl.pallas_call(far_kernel, out_shape=(jax.ShapeDtypeStruct((HROWS, LANES)...]
  transfers between devices with their start and end apart: 1 -> 1, of which waited for: 0 -> 0; matrix products, arithmetic and copies ran while one was open for 0% -> 0% of each run, Pallas kernels for 16% -> 14%
where the time goes in v11:
time: 56 us; the launch traced here: 55.9 us
  Pallas kernels  52.1 us (93%)
  starting transfers between devices  3.08 us (6%)
  between operations  0.7 us (1%)
    pallas_call x1, Pallas kernels, local_step(): pl.pallas_call(comm_kernel, out_shape=pltpu.VMEM((4, NC, OWN, CW), f32),...  27.6 us
    pallas_call x1, Pallas kernels, local_step(): pl.pallas_call(far_kernel, out_shape=(jax.ShapeDtypeStruct((HROWS, LANES)...  15.3 us
    pallas_call x1, Pallas kernels, local_step(): pl.pallas_call(near_kernel, out_shape=(pltpu.VMEM((HROWS, LANES), f32), j...  8.01 us
    ppermute x1, starting transfers between devices, local_step(): o_got = lax.ppermute(o_far, 'sp', [(0, 2), (1, 3), (2, 0), (3, 1)])  3.08 us
    pallas_call x1, Pallas kernels, local_step(): pl.pallas_call(finish_kernel, out_shape=jax.ShapeDtypeStruct((ROWS, DM),...  1.21 us
  transfers between devices with their start and end apart: 1, of which 0 were waited for; matrix products, arithmetic and copies ran while one was open for 0% of the time, Pallas kernels for 14%

profile of v11, /device:TPU:0, one launch (start us, length us, event | category | flops | bytes accessed | tf_op | source)
XLA Modules:
  0.0 55.9 jit_solution(556418106033483901)
XLA Ops:
  0.6 15.3 %attend_far.1 = (f32[520,128]{1,0:T(8,128)S(1)}, bf16[64,256,128]{2,1,0:T(8,128)(2,1)S(1)}, bf16[64,256,128]{2,1,0:T(8,128)(2,1)S(1)}, f32[1088,128]{1,0:T(8,128...) custom-call(s32[128]{0:T(128)} %pos_h.3, s32[1,128]{1,0:T(1,128)} %bitcast.29, f32[1,128]{1,0:T(1,128)} %constant.5.freq_h, ...), custom_call_target="tpu_custom_call" | custom-call | flops 2000000000 | bytes 25000000 | tf_op jit(solution)/shard_map/attend_far/pallas_call | solution.py:479
  16.0 3.1 %collective-permute-start = (f32[520,128]{1,0:T(8,128)S(1)}, f32[520,128]{1,0:T(8,128)S(1)}, u32[]{:S(2)}, u32[]{:S(2)}) collective-permute-start(f32[520,128]{1,0:T(8,128)S(1)} %get-tuple-element.18), channel_id=1, source_target_pairs={{0,2},{1,3},{2,0},{3,1},{4,6},{5,7},{6,4},{7,5},{8,10},{9,11},{10,... | collective-permute-start | bytes 798728 | tf_op jit(solution)/shard_map/ppermute | solution.py:498
  19.0 8.0 %attend_near.1 = (f32[520,128]{1,0:T(8,128)S(1)}, bf16[128,256,128]{2,1,0:T(8,128)(2,1)}, bf16[128,256,128]{2,1,0:T(8,128)(2,1)}) custom-call(s32[128]{0:T(128)} %pos_h.3, f32[1088,128]{1,0:T(8,128)S(1)} %get-tuple-element.12.qs, f32[1088,128]{1,0:T(8,128)S(1)} %get-tuple-element.13.ks, f32[1088,128]{1,0:T(8,128)S(1)} %get-tuple-element.14.vs, ...), custom_call_target="tpu_custom_call" | custom-call | flops 10000000000 | bytes 25000000 | tf_op jit(solution)/shard_map/attend_near/pallas_call | solution.py:499
  27.1 0.0 copy-start
  27.1 0.0 copy-start.1
  27.1 0.0 collective-permute-done.o_got
  27.1 27.6 %combine.1.s_all = f32[4,15,32,256]{3,2,1,0:T(8,128)S(1)} custom-call(f32[520,128]{1,0:T(8,128)S(1)} %get-tuple-element.17.o_own, f32[520,128]{1,0:T(8,128)S(1)} %collective-permute-done.o_got, bf16[1024,3840]{1,0:T(8,128)(2,1)} %wo_h.1), custom_call_target="tpu_custom_call" | custom-call | tf_op jit(solution)/shard_map/combine/pallas_call | solution.py:514
  54.6 0.0 copy-done
  54.7 0.0 copy-done.1
  54.7 1.2 %finish.1 = bf16[128,3840]{1,0:T(8,128)(2,1)} custom-call(f32[4,15,32,256]{3,2,1,0:T(8,128)S(1)} %combine.1.s_all, bf16[128,3840]{1,0:T(8,128)(2,1)S(1)} %copy-done, f32[30,128]{1,0:T(8,128)S(1)} %bitcast.23), custom_call_target="tpu_custom_call" | custom-call | tf_op jit(solution)/shard_map/finish/pallas_call | solution.py:530
Async XLA Ops:
  16.0 11.1 %collective-permute-start = (f32[520,128]{1,0:T(8,128)S(1)}, f32[520,128]{1,0:T(8,128)S(1)}, u32[]{:S(2)}, u32[]{:S(2)}) collective-permute-start(f32[520,128]{1,0:T(8,128)S(1)} %get-tuple-element.18), channel_id=1, source_target_pairs={{0,2},{1,3},{2,0},{3,1},{4,6},{5,7},{6,4},{7,5},{8,10},{9,11},{10,... | collective-permute-start | bytes 798728 | tf_op jit(solution)/shard_map/ppermute | solution.py:498
  27.1 27.6 %copy-start = (bf16[128,3840]{1,0:T(8,128)(2,1)S(1)}, bf16[128,3840]{1,0:T(8,128)(2,1)}, u32[]{:S(2)}) copy-start(bf16[128,3840]{1,0:T(8,128)(2,1)} %x_ref.1) | copy-start | bytes 2949124
  27.1 27.6 %copy-start.1 = (f32[3840]{0:T(1024)S(1)}, f32[3840]{0:T(1024)}, u32[]{:S(2)}) copy-start(f32[3840]{0:T(1024)} %param.18) | copy-start | bytes 46084

commit v12 on v11

--- a/solution.py
+++ b/solution.py
@@ -24,6 +24,9 @@
 NCH = HALF // BCH
 KC = 768
 NKC = DM // KC
+KP = 256
+NKP = DM // KP
+WIN = 5
 SHIFT = 20.0
 CW = 256
 NC = DM // CW
@@ -111,12 +114,12 @@
     row0 = (1 - lax.axis_index('sp') // 2) * HALF
 
     def w_start(c):
-        rows = pl.ds(c * KC, KC)
+        rows = pl.ds(c * KP, KP)
         for n, (src, dst) in enumerate(((wk_h, wk_buf), (wv_h, wv_buf), (wq_h, wq_buf))):
             pltpu.make_async_copy(src.at[rows, :], dst.at[rows, :], w_sem.at[c]).start()
 
     def w_wait(c):
-        rows = pl.ds(c * KC, KC)
+        rows = pl.ds(c * KP, KP)
         for n, (src, dst) in enumerate(((wk_h, wk_buf), (wv_h, wv_buf), (wq_h, wq_buf))):
             pltpu.make_async_copy(src.at[rows, :], dst.at[rows, :], w_sem.at[c]).wait()
 
@@ -132,13 +135,12 @@
         c.start()
     x_copy = pltpu.make_async_copy(x_h, x_buf, x_sem)
     x_copy.start()
-    for c in range(NKC):
+    for c in range(3):
         w_start(c)
-    for n in range(NCH):
-        k_in(n).start()
-        v_in(n).start()
     for c in small:
         c.wait()
+    for c in range(3, WIN):
+        w_start(c)
     pos_col = jnp.broadcast_to(posv[...].astype(jnp.float32), (ROWS, LANES)).T
     ang = pos_col * freq[...]
     cos_ref[...] = jnp.cos(ang)
@@ -157,7 +159,14 @@
     lax.fori_loop(0, ROWS // 16, norm_rows, 0)
 
     for c in range(NKC):
-        w_wait(c)
+        for p in range(c * (KC // KP), (c + 1) * (KC // KP)):
+            w_wait(p)
+            if p + WIN < NKP:
+                w_start(p + WIN)
+            elif (p + WIN - NKP) % 2 == 0:
+                n = (p + WIN - NKP) // 2
+                k_in(n).start()
+                v_in(n).start()
         rows = slice(c * KC, (c + 1) * KC)
         a_c = a_buf[:, rows]
         for i in range(8):
@@ -197,6 +206,11 @@
         k_in(i).wait()
         v_in(i).wait()
 
+        @pl.when(i == 0)
+        def _():
+            k_in(NCH - 1).start()
+            v_in(NCH - 1).start()
+
     attend_rows(row0, NCH, pos_ref, kbuf, vbuf, qs, ks, vs, o_ref, before, lambda i: None)
 
 
@@ -488,7 +502,7 @@
                 pltpu.VMEM((DM // LANES, LANES), f32), pltpu.VMEM((ROWS, LANES), f32), pltpu.VMEM((ROWS, LANES), f32),
                 pltpu.VMEM((ROWS, DM), bf16), pltpu.VMEM((ROWS, DM), bf16),
                 pltpu.VMEM((DM, 1024), bf16), pltpu.VMEM((DM, 512), bf16), pltpu.VMEM((DM, 512), bf16), pltpu.VMEM((8, ROWS, HD), f32),
-                dma, dma, dma((NKC,)), dma((NCH,)),
+                dma, dma, dma((NKP,)), dma((NCH,)),
             ],
             compiler_params=pltpu.CompilerParams(vmem_limit_bytes=40 << 20),
             cost_estimate=pl.CostEstimate(flops=2 * 10 ** 9, bytes_accessed=25 * 10 ** 6, transcendentals=0),

time: 56 us -> 52.4 us (0.936)
  Pallas kernels: 52.1 us -> 48.5 us
    pallas_call x1, Pallas kernels: 15.3 us -> 11.7 us  [local_step(): pl.pallas_call(far_kernel, out_shape=(jax.ShapeDtypeStruct((HROWS, LANES)...]
  transfers between devices with their start and end apart: 1 -> 1, of which waited for: 0 -> 0; matrix products, arithmetic and copies ran while one was open for 0% -> 0% of each run, Pallas kernels for 14% -> 15%
where the time goes in v12:
time: 52.4 us; the launch traced here: 52.3 us
  Pallas kernels  48.5 us (93%)
  starting transfers between devices  3.1 us (6%)
  between operations  0.7 us (1%)
    pallas_call x1, Pallas kernels, local_step(): pl.pallas_call(comm_kernel, out_shape=pltpu.VMEM((4, NC, OWN, CW), f32),...  27.5 us
    pallas_call x1, Pallas kernels, local_step(): pl.pallas_call(far_kernel, out_shape=(jax.ShapeDtypeStruct((HROWS, LANES)...  11.7 us
    pallas_call x1, Pallas kernels, local_step(): pl.pallas_call(near_kernel, out_shape=(pltpu.VMEM((HROWS, LANES), f32), j...  8.01 us
    ppermute x1, starting transfers between devices, local_step(): o_got = lax.ppermute(o_far, 'sp', [(0, 2), (1, 3), (2, 0), (3, 1)])  3.1 us
    pallas_call x1, Pallas kernels, local_step(): pl.pallas_call(finish_kernel, out_shape=jax.ShapeDtypeStruct((ROWS, DM),...  1.21 us
  transfers between devices with their start and end apart: 1, of which 0 were waited for; matrix products, arithmetic and copies ran while one was open for 0% of the time, Pallas kernels for 15%

profile of v12, /device:TPU:0, one launch (start us, length us, event | category | flops | bytes accessed | tf_op | source)
XLA Modules:
  0.0 52.3 jit_solution(3455411711006900124)
XLA Ops:
  0.6 11.7 %attend_far.1 = (f32[520,128]{1,0:T(8,128)S(1)}, bf16[64,256,128]{2,1,0:T(8,128)(2,1)S(1)}, bf16[64,256,128]{2,1,0:T(8,128)(2,1)S(1)}, f32[1088,128]{1,0:T(8,128...) custom-call(s32[128]{0:T(128)} %pos_h.3, s32[1,128]{1,0:T(1,128)} %bitcast.29, f32[1,128]{1,0:T(1,128)} %constant.5.freq_h, ...), custom_call_target="tpu_custom_call" | custom-call | flops 2000000000 | bytes 25000000 | tf_op jit(solution)/shard_map/attend_far/pallas_call | solution.py:493
  12.4 3.1 %collective-permute-start = (f32[520,128]{1,0:T(8,128)S(1)}, f32[520,128]{1,0:T(8,128)S(1)}, u32[]{:S(2)}, u32[]{:S(2)}) collective-permute-start(f32[520,128]{1,0:T(8,128)S(1)} %get-tuple-element.18), channel_id=1, source_target_pairs={{0,2},{1,3},{2,0},{3,1},{4,6},{5,7},{6,4},{7,5},{8,10},{9,11},{10,... | collective-permute-start | bytes 798728 | tf_op jit(solution)/shard_map/ppermute | solution.py:512
  15.5 8.0 %attend_near.1 = (f32[520,128]{1,0:T(8,128)S(1)}, bf16[128,256,128]{2,1,0:T(8,128)(2,1)}, bf16[128,256,128]{2,1,0:T(8,128)(2,1)}) custom-call(s32[128]{0:T(128)} %pos_h.3, f32[1088,128]{1,0:T(8,128)S(1)} %get-tuple-element.12.qs, f32[1088,128]{1,0:T(8,128)S(1)} %get-tuple-element.13.ks, f32[1088,128]{1,0:T(8,128)S(1)} %get-tuple-element.14.vs, ...), custom_call_target="tpu_custom_call" | custom-call | flops 10000000000 | bytes 25000000 | tf_op jit(solution)/shard_map/attend_near/pallas_call | solution.py:513
  23.5 0.0 copy-start
  23.5 0.0 copy-start.1
  23.5 0.0 collective-permute-done.o_got
  23.5 27.5 %combine.1.s_all = f32[4,15,32,256]{3,2,1,0:T(8,128)S(1)} custom-call(f32[520,128]{1,0:T(8,128)S(1)} %get-tuple-element.17.o_own, f32[520,128]{1,0:T(8,128)S(1)} %collective-permute-done.o_got, bf16[1024,3840]{1,0:T(8,128)(2,1)} %wo_h.1), custom_call_target="tpu_custom_call" | custom-call | tf_op jit(solution)/shard_map/combine/pallas_call | solution.py:528
  51.1 0.0 copy-done
  51.1 0.0 copy-done.1
  51.1 1.2 %finish.1 = bf16[128,3840]{1,0:T(8,128)(2,1)} custom-call(f32[4,15,32,256]{3,2,1,0:T(8,128)S(1)} %combine.1.s_all, bf16[128,3840]{1,0:T(8,128)(2,1)S(1)} %copy-done, f32[30,128]{1,0:T(8,128)S(1)} %bitcast.23), custom_call_target="tpu_custom_call" | custom-call | tf_op jit(solution)/shard_map/finish/pallas_call | solution.py:544
Async XLA Ops:
  12.4 11.1 %collective-permute-start = (f32[520,128]{1,0:T(8,128)S(1)}, f32[520,128]{1,0:T(8,128)S(1)}, u32[]{:S(2)}, u32[]{:S(2)}) collective-permute-start(f32[520,128]{1,0:T(8,128)S(1)} %get-tuple-element.18), channel_id=1, source_target_pairs={{0,2},{1,3},{2,0},{3,1},{4,6},{5,7},{6,4},{7,5},{8,10},{9,11},{10,... | collective-permute-start | bytes 798728 | tf_op jit(solution)/shard_map/ppermute | solution.py:512
  23.5 27.6 %copy-start = (bf16[128,3840]{1,0:T(8,128)(2,1)S(1)}, bf16[128,3840]{1,0:T(8,128)(2,1)}, u32[]{:S(2)}) copy-start(bf16[128,3840]{1,0:T(8,128)(2,1)} %x_ref.1) | copy-start | bytes 2949124
  23.5 27.6 %copy-start.1 = (f32[3840]{0:T(1024)S(1)}, f32[3840]{0:T(1024)}, u32[]{:S(2)}) copy-start(f32[3840]{0:T(1024)} %param.18) | copy-start | bytes 46084

commit v13 on v12

--- a/solution.py
+++ b/solution.py
@@ -26,7 +26,7 @@
 NKC = DM // KC
 KP = 256
 NKP = DM // KP
-WIN = 5
+WIN = 9
 SHIFT = 20.0
 CW = 256
 NC = DM // CW
@@ -163,7 +163,7 @@
             w_wait(p)
             if p + WIN < NKP:
                 w_start(p + WIN)
-            elif (p + WIN - NKP) % 2 == 0:
+            elif (p + WIN - NKP) % 2 == 0 and (p + WIN - NKP) // 2 < NCH:
                 n = (p + WIN - NKP) // 2
                 k_in(n).start()
                 v_in(n).start()
@@ -205,11 +205,6 @@
     def before(i):
         k_in(i).wait()
         v_in(i).wait()
-
-        @pl.when(i == 0)
-        def _():
-            k_in(NCH - 1).start()
-            v_in(NCH - 1).start()
 
     attend_rows(row0, NCH, pos_ref, kbuf, vbuf, qs, ks, vs, o_ref, before, lambda i: None)
 

time: 52.4 us -> 51.1 us (0.975)
  Pallas kernels: 48.5 us -> 47.1 us
    pallas_call x1, Pallas kernels: 11.7 us -> 10.4 us  [local_step(): pl.pallas_call(far_kernel, out_shape=(jax.ShapeDtypeStruct((HROWS, LANES)...]
  transfers between devices with their start and end apart: 1 -> 1, of which waited for: 0 -> 0; matrix products, arithmetic and copies ran while one was open for 0% -> 0% of each run, Pallas kernels for 15% -> 16%
where the time goes in v13:
time: 51.1 us; the launch traced here: 50.9 us
  Pallas kernels  47.1 us (92%)
  starting transfers between devices  3.09 us (6%)
  between operations  0.7 us (1%)
    pallas_call x1, Pallas kernels, local_step(): pl.pallas_call(comm_kernel, out_shape=pltpu.VMEM((4, NC, OWN, CW), f32),...  27.5 us
    pallas_call x1, Pallas kernels, local_step(): pl.pallas_call(far_kernel, out_shape=(jax.ShapeDtypeStruct((HROWS, LANES)...  10.4 us
    pallas_call x1, Pallas kernels, local_step(): pl.pallas_call(near_kernel, out_shape=(pltpu.VMEM((HROWS, LANES), f32), j...  8.01 us
    ppermute x1, starting transfers between devices, local_step(): o_got = lax.ppermute(o_far, 'sp', [(0, 2), (1, 3), (2, 0), (3, 1)])  3.09 us
    pallas_call x1, Pallas kernels, local_step(): pl.pallas_call(finish_kernel, out_shape=jax.ShapeDtypeStruct((ROWS, DM),...  1.21 us
  transfers between devices with their start and end apart: 1, of which 0 were waited for; matrix products, arithmetic and copies ran while one was open for 0% of the time, Pallas kernels for 16%

profile of v13, /device:TPU:0, one launch (start us, length us, event | category | flops | bytes accessed | tf_op | source)
XLA Modules:
  0.0 50.9 jit_solution(14531253479620079619)
XLA Ops:
  0.6 10.4 %attend_far.1 = (f32[520,128]{1,0:T(8,128)S(1)}, bf16[64,256,128]{2,1,0:T(8,128)(2,1)S(1)}, bf16[64,256,128]{2,1,0:T(8,128)(2,1)S(1)}, f32[1088,128]{1,0:T(8,128...) custom-call(s32[128]{0:T(128)} %pos_h.3, s32[1,128]{1,0:T(1,128)} %bitcast.29, f32[1,128]{1,0:T(1,128)} %constant.5.freq_h, ...), custom_call_target="tpu_custom_call" | custom-call | flops 2000000000 | bytes 25000000 | tf_op jit(solution)/shard_map/attend_far/pallas_call | solution.py:488
  11.0 3.1 %collective-permute-start = (f32[520,128]{1,0:T(8,128)S(1)}, f32[520,128]{1,0:T(8,128)S(1)}, u32[]{:S(2)}, u32[]{:S(2)}) collective-permute-start(f32[520,128]{1,0:T(8,128)S(1)} %get-tuple-element.18), channel_id=1, source_target_pairs={{0,2},{1,3},{2,0},{3,1},{4,6},{5,7},{6,4},{7,5},{8,10},{9,11},{10,... | collective-permute-start | bytes 798728 | tf_op jit(solution)/shard_map/ppermute | solution.py:507
  14.1 8.0 %attend_near.1 = (f32[520,128]{1,0:T(8,128)S(1)}, bf16[128,256,128]{2,1,0:T(8,128)(2,1)}, bf16[128,256,128]{2,1,0:T(8,128)(2,1)}) custom-call(s32[128]{0:T(128)} %pos_h.3, f32[1088,128]{1,0:T(8,128)S(1)} %get-tuple-element.12.qs, f32[1088,128]{1,0:T(8,128)S(1)} %get-tuple-element.13.ks, f32[1088,128]{1,0:T(8,128)S(1)} %get-tuple-element.14.vs, ...), custom_call_target="tpu_custom_call" | custom-call | flops 10000000000 | bytes 25000000 | tf_op jit(solution)/shard_map/attend_near/pallas_call | solution.py:508
  22.1 0.0 copy-start
  22.1 0.0 copy-start.1
  22.1 0.0 collective-permute-done.o_got
  22.2 27.5 %combine.1.s_all = f32[4,15,32,256]{3,2,1,0:T(8,128)S(1)} custom-call(f32[520,128]{1,0:T(8,128)S(1)} %get-tuple-element.17.o_own, f32[520,128]{1,0:T(8,128)S(1)} %collective-permute-done.o_got, bf16[1024,3840]{1,0:T(8,128)(2,1)} %wo_h.1), custom_call_target="tpu_custom_call" | custom-call | tf_op jit(solution)/shard_map/combine/pallas_call | solution.py:523
  49.7 0.0 copy-done
  49.7 0.0 copy-done.1
  49.7 1.2 %finish.1 = bf16[128,3840]{1,0:T(8,128)(2,1)} custom-call(f32[4,15,32,256]{3,2,1,0:T(8,128)S(1)} %combine.1.s_all, bf16[128,3840]{1,0:T(8,128)(2,1)S(1)} %copy-done, f32[30,128]{1,0:T(8,128)S(1)} %bitcast.23), custom_call_target="tpu_custom_call" | custom-call | tf_op jit(solution)/shard_map/finish/pallas_call | solution.py:539
Async XLA Ops:
  11.0 11.1 %collective-permute-start = (f32[520,128]{1,0:T(8,128)S(1)}, f32[520,128]{1,0:T(8,128)S(1)}, u32[]{:S(2)}, u32[]{:S(2)}) collective-permute-start(f32[520,128]{1,0:T(8,128)S(1)} %get-tuple-element.18), channel_id=1, source_target_pairs={{0,2},{1,3},{2,0},{3,1},{4,6},{5,7},{6,4},{7,5},{8,10},{9,11},{10,... | collective-permute-start | bytes 798728 | tf_op jit(solution)/shard_map/ppermute | solution.py:507
  22.1 27.6 %copy-start = (bf16[128,3840]{1,0:T(8,128)(2,1)S(1)}, bf16[128,3840]{1,0:T(8,128)(2,1)}, u32[]{:S(2)}) copy-start(bf16[128,3840]{1,0:T(8,128)(2,1)} %x_ref.1) | copy-start | bytes 2949124
  22.1 27.6 %copy-start.1 = (f32[3840]{0:T(1024)S(1)}, f32[3840]{0:T(1024)}, u32[]{:S(2)}) copy-start(f32[3840]{0:T(1024)} %param.18) | copy-start | bytes 46084

commit v14 on v10

--- a/solution.py
+++ b/solution.py
@@ -158,10 +158,9 @@
         w_wait(c)
         if c + 3 < NKC:
             w_start(c + 3)
-        if c >= NKC - 2:
-            for n in range(2 * (c + 2 - NKC), 2 * (c + 3 - NKC)):
-                k_in(n).start()
-                v_in(n).start()
+        for n in ((), (), (0,), (1,), (2, 3))[c]:
+            k_in(n).start()
+            v_in(n).start()
         rows = slice(c * KC, (c + 1) * KC)
         a_c = a_buf[:, rows]
         for i in range(8):
@@ -291,8 +290,6 @@
     def _():
         pl.semaphore_signal(bar, inc=1, device_id={'tp': z + 1}, device_id_type=MESH)
 
-    pl.semaphore_wait(bar, 3 + (z * (3 - z)) // 2)
-
     def shares(l_a, l_b, slot):
         tot = l_a + l_b
         inv = jnp.where(tot > 0.0, 1.0 / tot, 0.0)
@@ -312,10 +309,11 @@
 
     merge_half(theirs, m1)
     m1[pl.ds(8 * OWN, 8), :] = tot
+    merge_half(mine, m2)
     pair = pltpu.make_async_remote_copy(
         src_ref=m1, dst_ref=r1, send_sem=r1_send, recv_sem=r1_recv, device_id={'sp': partner}, device_id_type=MESH)
+    pl.semaphore_wait(bar, 3 + (z * (3 - z)) // 2)
     pair.start()
-    merge_half(mine, m2)
     pair.wait()
     shares(tot, r1[pl.ds(8 * OWN, 8), :], 2)
     fa, fb = fac[2, pl.ds(mine, OWN), :], fac[3, pl.ds(mine, OWN), :]

time: 51.1 us -> 50.5 us (0.988)
  Pallas kernels: 47.2 us -> 46.6 us
where the time goes in v14:
time: 50.5 us; the launch traced here: 50.4 us
  Pallas kernels  46.6 us (92%)
  starting transfers between devices  3.09 us (6%)
  between operations  0.7 us (1%)
    pallas_call x1, Pallas kernels, local_step(): pl.pallas_call(comm_kernel, out_shape=pltpu.VMEM((4, NC, OWN, CW), f32),...  27.2 us
    pallas_call x1, Pallas kernels, local_step(): pl.pallas_call(far_kernel, out_shape=(jax.ShapeDtypeStruct((HROWS, LANES)...  10.1 us
    pallas_call x1, Pallas kernels, local_step(): pl.pallas_call(near_kernel, out_shape=(pltpu.VMEM((HROWS, LANES), f32), j...  8.01 us
    ppermute x1, starting transfers between devices, local_step(): o_got = lax.ppermute(o_far, 'sp', [(0, 2), (1, 3), (2, 0), (3, 1)])  3.09 us
    pallas_call x1, Pallas kernels, local_step(): pl.pallas_call(finish_kernel, out_shape=jax.ShapeDtypeStruct((ROWS, DM),...  1.21 us
  transfers between devices with their start and end apart: 1, of which 0 were waited for; matrix products, arithmetic and copies ran while one was open for 0% of the time, Pallas kernels for 16%

profile of v14, /device:TPU:0, one launch (start us, length us, event | category | flops | bytes accessed | tf_op | source)
XLA Modules:
  0.0 50.4 jit_solution(6512793946501178510)
XLA Ops:
  0.6 10.1 %attend_far.1 = (f32[520,128]{1,0:T(8,128)S(1)}, bf16[64,256,128]{2,1,0:T(8,128)(2,1)S(1)}, bf16[64,256,128]{2,1,0:T(8,128)(2,1)S(1)}, f32[1088,128]{1,0:T(8,128...) custom-call(s32[128]{0:T(128)} %pos_h.3, s32[1,128]{1,0:T(1,128)} %bitcast.29, f32[1,128]{1,0:T(1,128)} %constant.5.freq_h, ...), custom_call_target="tpu_custom_call" | custom-call | flops 2000000000 | bytes 25000000 | tf_op jit(solution)/shard_map/attend_far/pallas_call | solution.py:481
  10.8 3.1 %collective-permute-start = (f32[520,128]{1,0:T(8,128)S(1)}, f32[520,128]{1,0:T(8,128)S(1)}, u32[]{:S(2)}, u32[]{:S(2)}) collective-permute-start(f32[520,128]{1,0:T(8,128)S(1)} %get-tuple-element.18), channel_id=1, source_target_pairs={{0,2},{1,3},{2,0},{3,1},{4,6},{5,7},{6,4},{7,5},{8,10},{9,11},{10,... | collective-permute-start | bytes 798728 | tf_op jit(solution)/shard_map/ppermute | solution.py:500
  13.9 8.0 %attend_near.1 = (f32[520,128]{1,0:T(8,128)S(1)}, bf16[128,256,128]{2,1,0:T(8,128)(2,1)}, bf16[128,256,128]{2,1,0:T(8,128)(2,1)}) custom-call(s32[128]{0:T(128)} %pos_h.3, f32[1088,128]{1,0:T(8,128)S(1)} %get-tuple-element.12.qs, f32[1088,128]{1,0:T(8,128)S(1)} %get-tuple-element.13.ks, f32[1088,128]{1,0:T(8,128)S(1)} %get-tuple-element.14.vs, ...), custom_call_target="tpu_custom_call" | custom-call | flops 10000000000 | bytes 25000000 | tf_op jit(solution)/shard_map/attend_near/pallas_call | solution.py:501
  21.9 0.0 copy-start
  21.9 0.0 copy-start.1
  21.9 0.0 collective-permute-done.o_got
  21.9 27.2 %combine.1.s_all = f32[4,15,32,256]{3,2,1,0:T(8,128)S(1)} custom-call(f32[520,128]{1,0:T(8,128)S(1)} %get-tuple-element.17.o_own, f32[520,128]{1,0:T(8,128)S(1)} %collective-permute-done.o_got, bf16[1024,3840]{1,0:T(8,128)(2,1)} %wo_h.1), custom_call_target="tpu_custom_call" | custom-call | tf_op jit(solution)/shard_map/combine/pallas_call | solution.py:516
  49.1 0.0 copy-done
  49.2 0.0 copy-done.1
  49.2 1.2 %finish.1 = bf16[128,3840]{1,0:T(8,128)(2,1)} custom-call(f32[4,15,32,256]{3,2,1,0:T(8,128)S(1)} %combine.1.s_all, bf16[128,3840]{1,0:T(8,128)(2,1)S(1)} %copy-done, f32[30,128]{1,0:T(8,128)S(1)} %bitcast.23), custom_call_target="tpu_custom_call" | custom-call | tf_op jit(solution)/shard_map/finish/pallas_call | solution.py:532
Async XLA Ops:
  10.8 11.1 %collective-permute-start = (f32[520,128]{1,0:T(8,128)S(1)}, f32[520,128]{1,0:T(8,128)S(1)}, u32[]{:S(2)}, u32[]{:S(2)}) collective-permute-start(f32[520,128]{1,0:T(8,128)S(1)} %get-tuple-element.18), channel_id=1, source_target_pairs={{0,2},{1,3},{2,0},{3,1},{4,6},{5,7},{6,4},{7,5},{8,10},{9,11},{10,... | collective-permute-start | bytes 798728 | tf_op jit(solution)/shard_map/ppermute | solution.py:500
  21.9 27.3 %copy-start = (bf16[128,3840]{1,0:T(8,128)(2,1)S(1)}, bf16[128,3840]{1,0:T(8,128)(2,1)}, u32[]{:S(2)}) copy-start(bf16[128,3840]{1,0:T(8,128)(2,1)} %x_ref.1) | copy-start | bytes 2949124
  21.9 27.3 %copy-start.1 = (f32[3840]{0:T(1024)S(1)}, f32[3840]{0:T(1024)}, u32[]{:S(2)}) copy-start(f32[3840]{0:T(1024)} %param.18) | copy-start | bytes 46084

commit v15 on v14

--- a/solution.py
+++ b/solution.py
@@ -367,10 +367,11 @@
             w_c = wo_buf[group, :, pl.ds(pl.multiple_of(place * CW, CW), CW)]
             p_buf[i] = jnp.dot(lhs[...], w_c, preferred_element_type=jnp.float32)
 
-        kr = i - lag_r
-
-        @pl.when(jnp.logical_and(kr >= 0, kr < NC))
-        def _():
+        kr, kl = i - lag_r, i - lag_l
+        r_live = jnp.logical_and(kr >= 0, kr < NC)
+        l_live = jnp.logical_and(kl >= 0, kl < NC)
+
+        def step_right():
             @pl.when(z > 0)
             def _():
                 right_copy(kr).wait_recv()
@@ -380,10 +381,7 @@
                 sr[kr] = p_buf[kr] + rr[kr]
                 right_copy(kr).start()
 
-        kl = i - lag_l
-
-        @pl.when(jnp.logical_and(kl >= 0, kl < NC))
-        def _():
+        def step_left():
             @pl.when(z < 3)
             def _():
                 left_copy(kl).wait_recv()
@@ -392,6 +390,10 @@
             def _():
                 sl[kl] = p_buf[kl] + rl[kl]
                 left_copy(kl).start()
+
+        pl.when(jnp.logical_and(l_live, z < 2))(step_left)
+        pl.when(r_live)(step_right)
+        pl.when(jnp.logical_and(l_live, z >= 2))(step_left)
 
         k_s = i - lag_s
 

time: 50.5 us -> 50.5 us (level)
  no operation moved by 1% of the time
where the time goes in v15:
time: 50.5 us; the launch traced here: 50.4 us
  Pallas kernels  46.6 us (92%)
  starting transfers between devices  3.09 us (6%)
  between operations  0.7 us (1%)
    pallas_call x1, Pallas kernels, local_step(): pl.pallas_call(comm_kernel, out_shape=pltpu.VMEM((4, NC, OWN, CW), f32),...  27.2 us
    pallas_call x1, Pallas kernels, local_step(): pl.pallas_call(far_kernel, out_shape=(jax.ShapeDtypeStruct((HROWS, LANES)...  10.1 us
    pallas_call x1, Pallas kernels, local_step(): pl.pallas_call(near_kernel, out_shape=(pltpu.VMEM((HROWS, LANES), f32), j...  8.01 us
    ppermute x1, starting transfers between devices, local_step(): o_got = lax.ppermute(o_far, 'sp', [(0, 2), (1, 3), (2, 0), (3, 1)])  3.09 us
    pallas_call x1, Pallas kernels, local_step(): pl.pallas_call(finish_kernel, out_shape=jax.ShapeDtypeStruct((ROWS, DM),...  1.21 us
  transfers between devices with their start and end apart: 1, of which 0 were waited for; matrix products, arithmetic and copies ran while one was open for 0% of the time, Pallas kernels for 16%

profile of v15, /device:TPU:0, one launch (start us, length us, event | category | flops | bytes accessed | tf_op | source)
XLA Modules:
  0.0 50.4 jit_solution(6296784942982654323)
XLA Ops:
  0.6 10.1 %attend_far.1 = (f32[520,128]{1,0:T(8,128)S(1)}, bf16[64,256,128]{2,1,0:T(8,128)(2,1)S(1)}, bf16[64,256,128]{2,1,0:T(8,128)(2,1)S(1)}, f32[1088,128]{1,0:T(8,128...) custom-call(s32[128]{0:T(128)} %pos_h.3, s32[1,128]{1,0:T(1,128)} %bitcast.29, f32[1,128]{1,0:T(1,128)} %constant.5.freq_h, ...), custom_call_target="tpu_custom_call" | custom-call | flops 2000000000 | bytes 25000000 | tf_op jit(solution)/shard_map/attend_far/pallas_call | solution.py:483
  10.8 3.1 %collective-permute-start = (f32[520,128]{1,0:T(8,128)S(1)}, f32[520,128]{1,0:T(8,128)S(1)}, u32[]{:S(2)}, u32[]{:S(2)}) collective-permute-start(f32[520,128]{1,0:T(8,128)S(1)} %get-tuple-element.18), channel_id=1, source_target_pairs={{0,2},{1,3},{2,0},{3,1},{4,6},{5,7},{6,4},{7,5},{8,10},{9,11},{10,... | collective-permute-start | bytes 798728 | tf_op jit(solution)/shard_map/ppermute | solution.py:502
  13.9 8.0 %attend_near.1 = (f32[520,128]{1,0:T(8,128)S(1)}, bf16[128,256,128]{2,1,0:T(8,128)(2,1)}, bf16[128,256,128]{2,1,0:T(8,128)(2,1)}) custom-call(s32[128]{0:T(128)} %pos_h.3, f32[1088,128]{1,0:T(8,128)S(1)} %get-tuple-element.12.qs, f32[1088,128]{1,0:T(8,128)S(1)} %get-tuple-element.13.ks, f32[1088,128]{1,0:T(8,128)S(1)} %get-tuple-element.14.vs, ...), custom_call_target="tpu_custom_call" | custom-call | flops 10000000000 | bytes 25000000 | tf_op jit(solution)/shard_map/attend_near/pallas_call | solution.py:503
  21.9 0.0 copy-start
  21.9 0.0 copy-start.1
  21.9 0.0 collective-permute-done.o_got
  21.9 27.2 %combine.1.s_all = f32[4,15,32,256]{3,2,1,0:T(8,128)S(1)} custom-call(f32[520,128]{1,0:T(8,128)S(1)} %get-tuple-element.17.o_own, f32[520,128]{1,0:T(8,128)S(1)} %collective-permute-done.o_got, bf16[1024,3840]{1,0:T(8,128)(2,1)} %wo_h.1), custom_call_target="tpu_custom_call" | custom-call | tf_op jit(solution)/shard_map/combine/pallas_call | solution.py:518
  49.1 0.0 copy-done
  49.2 0.0 copy-done.1
  49.2 1.2 %finish.1 = bf16[128,3840]{1,0:T(8,128)(2,1)} custom-call(f32[4,15,32,256]{3,2,1,0:T(8,128)S(1)} %combine.1.s_all, bf16[128,3840]{1,0:T(8,128)(2,1)S(1)} %copy-done, f32[30,128]{1,0:T(8,128)S(1)} %bitcast.23), custom_call_target="tpu_custom_call" | custom-call | tf_op jit(solution)/shard_map/finish/pallas_call | solution.py:534
Async XLA Ops:
  10.8 11.1 %collective-permute-start = (f32[520,128]{1,0:T(8,128)S(1)}, f32[520,128]{1,0:T(8,128)S(1)}, u32[]{:S(2)}, u32[]{:S(2)}) collective-permute-start(f32[520,128]{1,0:T(8,128)S(1)} %get-tuple-element.18), channel_id=1, source_target_pairs={{0,2},{1,3},{2,0},{3,1},{4,6},{5,7},{6,4},{7,5},{8,10},{9,11},{10,... | collective-permute-start | bytes 798728 | tf_op jit(solution)/shard_map/ppermute | solution.py:502
  21.9 27.3 %copy-start = (bf16[128,3840]{1,0:T(8,128)(2,1)S(1)}, bf16[128,3840]{1,0:T(8,128)(2,1)}, u32[]{:S(2)}) copy-start(bf16[128,3840]{1,0:T(8,128)(2,1)} %x_ref.1) | copy-start | bytes 2949124
  21.9 27.3 %copy-start.1 = (f32[3840]{0:T(1024)S(1)}, f32[3840]{0:T(1024)}, u32[]{:S(2)}) copy-start(f32[3840]{0:T(1024)} %param.18) | copy-start | bytes 46084

commit v16 on v15

--- a/solution.py
+++ b/solution.py
@@ -33,7 +33,7 @@
 MESH = pl.DeviceIdType.MESH
 
 
-def attend_rows(row0, nchunk, pos_ref, kbuf, vbuf, qs, ks, vs, o_ref, before, after):
+def attend_rows(row0, bch, pos_ref, kbuf, vbuf, qs, ks, vs, o_ref, before, after):
     tbase = lax.axis_index('sp') * TB
     lane = lax.broadcasted_iota(jnp.int32, (8, LANES), 1)
     row = lax.broadcasted_iota(jnp.int32, (8, LANES), 0)
@@ -49,8 +49,8 @@
     def chunk(i, l_acc):
         before(i)
         tls = []
-        for u in range(BCH):
-            lb = i * BCH + u
+        for u in range(bch):
+            lb = i * bch + u
             b = row0 + lb
             tl = pos_ref[b] - tbase
             tls.append(tl)
@@ -67,15 +67,15 @@
             kbuf[lb, pl.ds(off, 16), :] = jnp.where(sel, jnp.concatenate([kn, kn], 0), kt).astype(jnp.bfloat16)
             vbuf[lb, pl.ds(off, 16), :] = jnp.where(sel, jnp.concatenate([vn, vn], 0), vt).astype(jnp.bfloat16)
         scores = []
-        for u in range(0, BCH, 2):
-            lb = i * BCH + u
+        for u in range(0, bch, 2):
+            lb = i * bch + u
             q0 = qs[pl.ds(row0 + lb, 8, stride=RP), :]
             q1 = qs[pl.ds(row0 + lb + 1, 8, stride=RP), :]
             lhs = jnp.concatenate([jnp.concatenate([q0, zero], 1), jnp.concatenate([zero, q1], 1)], 0).astype(jnp.bfloat16)
             kk = jnp.concatenate([kbuf[lb], kbuf[lb + 1]], 1)
             scores.append(lax.dot_general(lhs, kk, (((1,), (1,)), ((), ())), preferred_element_type=jnp.float32))
         weights = []
-        for u in range(0, BCH, 2):
+        for u in range(0, bch, 2):
             pair = []
             for w in range(2):
                 part = scores[u // 2][8 * w:8 * w + 8]
@@ -89,10 +89,10 @@
                 tot = jnp.sum(es[0] + es[1], axis=1, keepdims=True)
                 inv = jnp.where(tot > 0.0, 1.0 / tot, 0.0)
                 pair.append(jnp.concatenate([es[0] * inv, es[1] * inv], 1))
-                l_acc = jnp.where(lane == i * BCH + u + w, tot, l_acc)
+                l_acc = jnp.where(lane == i * bch + u + w, tot, l_acc)
             weights.append(jnp.concatenate(pair, 0).astype(jnp.bfloat16))
-        for u in range(0, BCH, 2):
-            lb = i * BCH + u
+        for u in range(0, bch, 2):
+            lb = i * bch + u
             vv = jnp.concatenate([vbuf[lb], vbuf[lb + 1]], 1)
             o = jnp.dot(weights[u // 2], vv, preferred_element_type=jnp.float32)
             o_ref[pl.ds(lb, 8, stride=HALF), :] = o[0:8, 0:LANES]
@@ -100,7 +100,7 @@
         after(i)
         return l_acc
 
-    l_acc = lax.fori_loop(0, nchunk, chunk, zero)
+    l_acc = lax.fori_loop(0, HALF // bch, chunk, zero)
     o_ref[pl.ds(8 * HALF, 8), :] = l_acc
 
 
@@ -197,10 +197,11 @@
                     qs[pl.ds((4 + i - 4) * RP, ROWS), :] = rhi
 
     def before(i):
-        k_in(i).wait()
-        v_in(i).wait()
-
-    attend_rows(row0, NCH, pos_ref, kbuf, vbuf, qs, ks, vs, o_ref, before, lambda i: None)
+        for n in range(2):
+            k_in(2 * i + n).wait()
+            v_in(2 * i + n).wait()
+
+    attend_rows(row0, 2 * BCH, pos_ref, kbuf, vbuf, qs, ks, vs, o_ref, before, lambda i: None)
 
 
 def near_kernel(pos_h, qs, ks, vs, kfar, vfar, kc_h, vc_h,
@@ -245,7 +246,7 @@
         k_out(i).start()
         v_out(i).start()
 
-    attend_rows(row0, NCH, pos_ref, kbuf, vbuf, qs, ks, vs, o_ref, before, after)
+    attend_rows(row0, BCH, pos_ref, kbuf, vbuf, qs, ks, vs, o_ref, before, after)
     for i in range(NCH):
         kf_out(i).wait()
         vf_out(i).wait()

time: 50.5 us -> 50.3 us (level)
  no operation moved by 1% of the time
where the time goes in v16:
time: 50.3 us; the launch traced here: 50.1 us
  Pallas kernels  46.3 us (92%)
  starting transfers between devices  3.09 us (6%)
  between operations  0.7 us (1%)
    pallas_call x1, Pallas kernels, local_step(): pl.pallas_call(comm_kernel, out_shape=pltpu.VMEM((4, NC, OWN, CW), f32),...  27.2 us
    pallas_call x1, Pallas kernels, local_step(): pl.pallas_call(far_kernel, out_shape=(jax.ShapeDtypeStruct((HROWS, LANES)...  9.89 us
    pallas_call x1, Pallas kernels, local_step(): pl.pallas_call(near_kernel, out_shape=(pltpu.VMEM((HROWS, LANES), f32), j...  8.01 us
    ppermute x1, starting transfers between devices, local_step(): o_got = lax.ppermute(o_far, 'sp', [(0, 2), (1, 3), (2, 0), (3, 1)])  3.09 us
    pallas_call x1, Pallas kernels, local_step(): pl.pallas_call(finish_kernel, out_shape=jax.ShapeDtypeStruct((ROWS, DM),...  1.21 us
  transfers between devices with their start and end apart: 1, of which 0 were waited for; matrix products, arithmetic and copies ran while one was open for 0% of the time, Pallas kernels for 16%

profile of v16, /device:TPU:0, one launch (start us, length us, event | category | flops | bytes accessed | tf_op | source)
XLA Modules:
  0.0 50.1 jit_solution(4742278700932718120)
XLA Ops:
  0.6 9.9 %attend_far.1 = (f32[520,128]{1,0:T(8,128)S(1)}, bf16[64,256,128]{2,1,0:T(8,128)(2,1)S(1)}, bf16[64,256,128]{2,1,0:T(8,128)(2,1)S(1)}, f32[1088,128]{1,0:T(8,128...) custom-call(s32[128]{0:T(128)} %pos_h.3, s32[1,128]{1,0:T(1,128)} %bitcast.29, f32[1,128]{1,0:T(1,128)} %constant.5.freq_h, ...), custom_call_target="tpu_custom_call" | custom-call | flops 2000000000 | bytes 25000000 | tf_op jit(solution)/shard_map/attend_far/pallas_call | solution.py:484
  10.5 3.1 %collective-permute-start = (f32[520,128]{1,0:T(8,128)S(1)}, f32[520,128]{1,0:T(8,128)S(1)}, u32[]{:S(2)}, u32[]{:S(2)}) collective-permute-start(f32[520,128]{1,0:T(8,128)S(1)} %get-tuple-element.18), channel_id=1, source_target_pairs={{0,2},{1,3},{2,0},{3,1},{4,6},{5,7},{6,4},{7,5},{8,10},{9,11},{10,... | collective-permute-start | bytes 798728 | tf_op jit(solution)/shard_map/ppermute | solution.py:503
  13.6 8.0 %attend_near.1 = (f32[520,128]{1,0:T(8,128)S(1)}, bf16[128,256,128]{2,1,0:T(8,128)(2,1)}, bf16[128,256,128]{2,1,0:T(8,128)(2,1)}) custom-call(s32[128]{0:T(128)} %pos_h.3, f32[1088,128]{1,0:T(8,128)S(1)} %get-tuple-element.12.qs, f32[1088,128]{1,0:T(8,128)S(1)} %get-tuple-element.13.ks, f32[1088,128]{1,0:T(8,128)S(1)} %get-tuple-element.14.vs, ...), custom_call_target="tpu_custom_call" | custom-call | flops 10000000000 | bytes 25000000 | tf_op jit(solution)/shard_map/attend_near/pallas_call | solution.py:504
  21.6 0.0 copy-start
  21.6 0.0 copy-start.1
  21.7 0.0 collective-permute-done.o_got
  21.7 27.2 %combine.1.s_all = f32[4,15,32,256]{3,2,1,0:T(8,128)S(1)} custom-call(f32[520,128]{1,0:T(8,128)S(1)} %get-tuple-element.17.o_own, f32[520,128]{1,0:T(8,128)S(1)} %collective-permute-done.o_got, bf16[1024,3840]{1,0:T(8,128)(2,1)} %wo_h.1), custom_call_target="tpu_custom_call" | custom-call | tf_op jit(solution)/shard_map/combine/pallas_call | solution.py:519
  48.9 0.0 copy-done
  48.9 0.0 copy-done.1
  48.9 1.2 %finish.1 = bf16[128,3840]{1,0:T(8,128)(2,1)} custom-call(f32[4,15,32,256]{3,2,1,0:T(8,128)S(1)} %combine.1.s_all, bf16[128,3840]{1,0:T(8,128)(2,1)S(1)} %copy-done, f32[30,128]{1,0:T(8,128)S(1)} %bitcast.23), custom_call_target="tpu_custom_call" | custom-call | tf_op jit(solution)/shard_map/finish/pallas_call | solution.py:535
Async XLA Ops:
  10.5 11.1 %collective-permute-start = (f32[520,128]{1,0:T(8,128)S(1)}, f32[520,128]{1,0:T(8,128)S(1)}, u32[]{:S(2)}, u32[]{:S(2)}) collective-permute-start(f32[520,128]{1,0:T(8,128)S(1)} %get-tuple-element.18), channel_id=1, source_target_pairs={{0,2},{1,3},{2,0},{3,1},{4,6},{5,7},{6,4},{7,5},{8,10},{9,11},{10,... | collective-permute-start | bytes 798728 | tf_op jit(solution)/shard_map/ppermute | solution.py:503
  21.6 27.3 %copy-start = (bf16[128,3840]{1,0:T(8,128)(2,1)S(1)}, bf16[128,3840]{1,0:T(8,128)(2,1)}, u32[]{:S(2)}) copy-start(bf16[128,3840]{1,0:T(8,128)(2,1)} %x_ref.1) | copy-start | bytes 2949124
  21.6 27.3 %copy-start.1 = (f32[3840]{0:T(1024)S(1)}, f32[3840]{0:T(1024)}, u32[]{:S(2)}) copy-start(f32[3840]{0:T(1024)} %param.18) | copy-start | bytes 46084

commit v17 on v16

--- a/solution.py
+++ b/solution.py
@@ -258,12 +258,14 @@
                 wo_buf, fac, m1, m2, r1, lhs, p_buf, rr, rl, sr, sl,
                 w_sem, r1_send, r1_recv,
                 right_send, right_recv, left_send, left_recv,
-                part_send, part_recv, y_send, y_recv, f_send, f_recv):
+                part_send, part_recv, y_send, y_recv, f_send, f_recv, a_send):
     z = lax.axis_index('tp')
     sp = lax.axis_index('sp')
     core = sp % 2
     partner = sp + 1 - 2 * core
     ypeer = (sp + 2) % 4
+    middle = (z * (3 - z)) // 2
+    across = z + 1 - 2 * (z % 2)
 
     def wo_copy(k):
         return pltpu.make_async_copy(wo_h.at[:, pl.ds(pl.multiple_of(k * WG * CW, CW), WG * CW)], wo_buf.at[k], w_sem.at[k])
@@ -282,6 +284,7 @@
     bar = pltpu.get_barrier_semaphore()
     pl.semaphore_signal(bar, inc=1, device_id={'sp': partner}, device_id_type=MESH)
     pl.semaphore_signal(bar, inc=1, device_id={'sp': ypeer}, device_id_type=MESH)
+    pl.semaphore_signal(bar, inc=1, device_id={'sp': ypeer, 'tp': across}, device_id_type=MESH)
 
     @pl.when(z > 0)
     def _():
@@ -313,7 +316,7 @@
     merge_half(mine, m2)
     pair = pltpu.make_async_remote_copy(
         src_ref=m1, dst_ref=r1, send_sem=r1_send, recv_sem=r1_recv, device_id={'sp': partner}, device_id_type=MESH)
-    pl.semaphore_wait(bar, 3 + (z * (3 - z)) // 2)
+    pl.semaphore_wait(bar, 4 + middle)
     pair.start()
     pair.wait()
     shares(tot, r1[pl.ds(8 * OWN, 8), :], 2)
@@ -343,6 +346,12 @@
             src_ref=s_all.at[sp, k], dst_ref=s_all.at[sp, k], send_sem=y_send, recv_sem=y_recv.at[k],
             device_id={'sp': ypeer}, device_id_type=MESH)
 
+    def across_copy():
+        last = NC - 1
+        return pltpu.make_async_remote_copy(
+            src_ref=s_all.at[sp, last], dst_ref=s_all.at[sp, last], send_sem=a_send, recv_sem=y_recv.at[last],
+            device_id={'sp': ypeer, 'tp': across}, device_id_type=MESH)
+
     def fwd_copy(k):
         return pltpu.make_async_remote_copy(
             src_ref=s_all.at[ypeer, k], dst_ref=s_all.at[ypeer, k], send_sem=f_send, recv_sem=f_recv,
@@ -401,7 +410,15 @@
         @pl.when(jnp.logical_and(k_s >= 0, k_s < NC))
         def _():
             s_all[sp, k_s] = p_buf[k_s] + rr[k_s] + rl[k_s]
-            y_copy(k_s).start()
+
+            @pl.when(jnp.logical_or(k_s < NC - 1, middle == 1))
+            def _():
+                y_copy(k_s).start()
+
+            @pl.when(jnp.logical_and(k_s == NC - 1, middle == 1))
+            def _():
+                across_copy().start()
+
             part_copy(k_s).start()
 
         k_y = i - lag_s - hop
@@ -423,7 +440,15 @@
     def _():
         whole(sl, left_send).wait()
 
-    whole(s_all.at[sp], y_send).wait()
+    @pl.when(middle == 1)
+    def _():
+        whole(s_all.at[sp], y_send).wait()
+        whole(s_all.at[sp, NC - 1], a_send).wait()
+
+    @pl.when(middle == 0)
+    def _():
+        whole(s_all.at[sp, pl.ds(0, NC - 1)], y_send).wait()
+
     whole(s_all.at[sp], part_send).wait()
     whole(s_all.at[ypeer], f_send).wait()
     whole(s_all.at[partner], part_recv).wait()
@@ -527,7 +552,7 @@
                 big, big, big, big, big,
                 dma((NC // WG,)), dma, dma,
                 dma, dma((NC,)), dma, dma((NC,)),
-                dma, dma, dma, dma((NC,)), dma, dma,
+                dma, dma, dma, dma((NC,)), dma, dma, dma,
             ],
             compiler_params=pltpu.CompilerParams(vmem_limit_bytes=40 << 20, collective_id=0, has_side_effects=True),
             name='combine',

time: 50.3 us -> 50.2 us (level)
  no operation moved by 1% of the time
where the time goes in v17:
time: 50.2 us; the launch traced here: 50 us
  Pallas kernels  46.2 us (92%)
  starting transfers between devices  3.09 us (6%)
  between operations  0.7 us (1%)
    pallas_call x1, Pallas kernels, local_step(): pl.pallas_call(comm_kernel, out_shape=pltpu.VMEM((4, NC, OWN, CW), f32),...  27.1 us
    pallas_call x1, Pallas kernels, local_step(): pl.pallas_call(far_kernel, out_shape=(jax.ShapeDtypeStruct((HROWS, LANES)...  9.89 us
    pallas_call x1, Pallas kernels, local_step(): pl.pallas_call(near_kernel, out_shape=(pltpu.VMEM((HROWS, LANES), f32), j...  8.01 us
    ppermute x1, starting transfers between devices, local_step(): o_got = lax.ppermute(o_far, 'sp', [(0, 2), (1, 3), (2, 0), (3, 1)])  3.09 us
    pallas_call x1, Pallas kernels, local_step(): pl.pallas_call(finish_kernel, out_shape=jax.ShapeDtypeStruct((ROWS, DM),...  1.21 us
  transfers between devices with their start and end apart: 1, of which 0 were waited for; matrix products, arithmetic and copies ran while one was open for 0% of the time, Pallas kernels for 16%

profile of v17, /device:TPU:0, one launch (start us, length us, event | category | flops | bytes accessed | tf_op | source)
XLA Modules:
  0.0 50.0 jit_solution(10629160575791240514)
XLA Ops:
  0.6 9.9 %attend_far.1 = (f32[520,128]{1,0:T(8,128)S(1)}, bf16[64,256,128]{2,1,0:T(8,128)(2,1)S(1)}, bf16[64,256,128]{2,1,0:T(8,128)(2,1)S(1)}, f32[1088,128]{1,0:T(8,128...) custom-call(s32[128]{0:T(128)} %pos_h.3, s32[1,128]{1,0:T(1,128)} %bitcast.29, f32[1,128]{1,0:T(1,128)} %constant.5.freq_h, ...), custom_call_target="tpu_custom_call" | custom-call | flops 2000000000 | bytes 25000000 | tf_op jit(solution)/shard_map/attend_far/pallas_call | solution.py:509
  10.5 3.1 %collective-permute-start = (f32[520,128]{1,0:T(8,128)S(1)}, f32[520,128]{1,0:T(8,128)S(1)}, u32[]{:S(2)}, u32[]{:S(2)}) collective-permute-start(f32[520,128]{1,0:T(8,128)S(1)} %get-tuple-element.18), channel_id=1, source_target_pairs={{0,2},{1,3},{2,0},{3,1},{4,6},{5,7},{6,4},{7,5},{8,10},{9,11},{10,... | collective-permute-start | bytes 798728 | tf_op jit(solution)/shard_map/ppermute | solution.py:528
  13.6 8.0 %attend_near.1 = (f32[520,128]{1,0:T(8,128)S(1)}, bf16[128,256,128]{2,1,0:T(8,128)(2,1)}, bf16[128,256,128]{2,1,0:T(8,128)(2,1)}) custom-call(s32[128]{0:T(128)} %pos_h.3, f32[1088,128]{1,0:T(8,128)S(1)} %get-tuple-element.12.qs, f32[1088,128]{1,0:T(8,128)S(1)} %get-tuple-element.13.ks, f32[1088,128]{1,0:T(8,128)S(1)} %get-tuple-element.14.vs, ...), custom_call_target="tpu_custom_call" | custom-call | flops 10000000000 | bytes 25000000 | tf_op jit(solution)/shard_map/attend_near/pallas_call | solution.py:529
  21.6 0.0 copy-start
  21.6 0.0 copy-start.1
  21.7 0.0 collective-permute-done.o_got
  21.7 27.1 %combine.1.s_all = f32[4,15,32,256]{3,2,1,0:T(8,128)S(1)} custom-call(f32[520,128]{1,0:T(8,128)S(1)} %get-tuple-element.17.o_own, f32[520,128]{1,0:T(8,128)S(1)} %collective-permute-done.o_got, bf16[1024,3840]{1,0:T(8,128)(2,1)} %wo_h.1), custom_call_target="tpu_custom_call" | custom-call | tf_op jit(solution)/shard_map/combine/pallas_call | solution.py:544
  48.8 0.0 copy-done
  48.8 0.0 copy-done.1
  48.8 1.2 %finish.1 = bf16[128,3840]{1,0:T(8,128)(2,1)} custom-call(f32[4,15,32,256]{3,2,1,0:T(8,128)S(1)} %combine.1.s_all, bf16[128,3840]{1,0:T(8,128)(2,1)S(1)} %copy-done, f32[30,128]{1,0:T(8,128)S(1)} %bitcast.23), custom_call_target="tpu_custom_call" | custom-call | tf_op jit(solution)/shard_map/finish/pallas_call | solution.py:560
Async XLA Ops:
  10.5 11.1 %collective-permute-start = (f32[520,128]{1,0:T(8,128)S(1)}, f32[520,128]{1,0:T(8,128)S(1)}, u32[]{:S(2)}, u32[]{:S(2)}) collective-permute-start(f32[520,128]{1,0:T(8,128)S(1)} %get-tuple-element.18), channel_id=1, source_target_pairs={{0,2},{1,3},{2,0},{3,1},{4,6},{5,7},{6,4},{7,5},{8,10},{9,11},{10,... | collective-permute-start | bytes 798728 | tf_op jit(solution)/shard_map/ppermute | solution.py:528
  21.6 27.1 %copy-start = (bf16[128,3840]{1,0:T(8,128)(2,1)S(1)}, bf16[128,3840]{1,0:T(8,128)(2,1)}, u32[]{:S(2)}) copy-start(bf16[128,3840]{1,0:T(8,128)(2,1)} %x_ref.1) | copy-start | bytes 2949124
  21.6 27.1 %copy-start.1 = (f32[3840]{0:T(1024)S(1)}, f32[3840]{0:T(1024)}, u32[]{:S(2)}) copy-start(f32[3840]{0:T(1024)} %param.18) | copy-start | bytes 46084

commit v18 on v17

--- a/solution.py
+++ b/solution.py
@@ -28,6 +28,7 @@
 CW = 256
 NC = DM // CW
 WG = 3
+LASTS = 3
 OWN = 32
 MROWS = 8 * OWN + 8
 MESH = pl.DeviceIdType.MESH
@@ -346,10 +347,9 @@
             src_ref=s_all.at[sp, k], dst_ref=s_all.at[sp, k], send_sem=y_send, recv_sem=y_recv.at[k],
             device_id={'sp': ypeer}, device_id_type=MESH)
 
-    def across_copy():
-        last = NC - 1
+    def across_copy(k):
         return pltpu.make_async_remote_copy(
-            src_ref=s_all.at[sp, last], dst_ref=s_all.at[sp, last], send_sem=a_send, recv_sem=y_recv.at[last],
+            src_ref=s_all.at[sp, k], dst_ref=s_all.at[sp, k], send_sem=a_send, recv_sem=y_recv.at[k],
             device_id={'sp': ypeer, 'tp': across}, device_id_type=MESH)
 
     def fwd_copy(k):
@@ -411,13 +411,13 @@
         def _():
             s_all[sp, k_s] = p_buf[k_s] + rr[k_s] + rl[k_s]
 
-            @pl.when(jnp.logical_or(k_s < NC - 1, middle == 1))
+            @pl.when(jnp.logical_or(k_s < NC - LASTS, middle == 1))
             def _():
                 y_copy(k_s).start()
 
-            @pl.when(jnp.logical_and(k_s == NC - 1, middle == 1))
-            def _():
-                across_copy().start()
+            @pl.when(jnp.logical_and(k_s >= NC - LASTS, middle == 1))
+            def _():
+                across_copy(k_s).start()
 
             part_copy(k_s).start()
 
@@ -443,11 +443,11 @@
     @pl.when(middle == 1)
     def _():
         whole(s_all.at[sp], y_send).wait()
-        whole(s_all.at[sp, NC - 1], a_send).wait()
+        whole(s_all.at[sp, pl.ds(NC - LASTS, LASTS)], a_send).wait()
 
     @pl.when(middle == 0)
     def _():
-        whole(s_all.at[sp, pl.ds(0, NC - 1)], y_send).wait()
+        whole(s_all.at[sp, pl.ds(0, NC - LASTS)], y_send).wait()
 
     whole(s_all.at[sp], part_send).wait()
     whole(s_all.at[ypeer], f_send).wait()

time: 50.2 us -> 50 us (level)
  no operation moved by 1% of the time
where the time goes in v18:
time: 50 us; the launch traced here: 49.9 us
  Pallas kernels  46.1 us (92%)
  starting transfers between devices  3.09 us (6%)
  between operations  0.7 us (1%)
    pallas_call x1, Pallas kernels, local_step(): pl.pallas_call(comm_kernel, out_shape=pltpu.VMEM((4, NC, OWN, CW), f32),...  27 us
    pallas_call x1, Pallas kernels, local_step(): pl.pallas_call(far_kernel, out_shape=(jax.ShapeDtypeStruct((HROWS, LANES)...  9.89 us
    pallas_call x1, Pallas kernels, local_step(): pl.pallas_call(near_kernel, out_shape=(pltpu.VMEM((HROWS, LANES), f32), j...  8.01 us
    ppermute x1, starting transfers between devices, local_step(): o_got = lax.ppermute(o_far, 'sp', [(0, 2), (1, 3), (2, 0), (3, 1)])  3.09 us
    pallas_call x1, Pallas kernels, local_step(): pl.pallas_call(finish_kernel, out_shape=jax.ShapeDtypeStruct((ROWS, DM),...  1.21 us
  transfers between devices with their start and end apart: 1, of which 0 were waited for; matrix products, arithmetic and copies ran while one was open for 0% of the time, Pallas kernels for 16%

profile of v18, /device:TPU:0, one launch (start us, length us, event | category | flops | bytes accessed | tf_op | source)
XLA Modules:
  0.0 49.9 jit_solution(15380160147015619116)
XLA Ops:
  0.6 9.9 %attend_far.1 = (f32[520,128]{1,0:T(8,128)S(1)}, bf16[64,256,128]{2,1,0:T(8,128)(2,1)S(1)}, bf16[64,256,128]{2,1,0:T(8,128)(2,1)S(1)}, f32[1088,128]{1,0:T(8,128...) custom-call(s32[128]{0:T(128)} %pos_h.3, s32[1,128]{1,0:T(1,128)} %bitcast.29, f32[1,128]{1,0:T(1,128)} %constant.5.freq_h, ...), custom_call_target="tpu_custom_call" | custom-call | flops 2000000000 | bytes 25000000 | tf_op jit(solution)/shard_map/attend_far/pallas_call | solution.py:509
  10.5 3.1 %collective-permute-start = (f32[520,128]{1,0:T(8,128)S(1)}, f32[520,128]{1,0:T(8,128)S(1)}, u32[]{:S(2)}, u32[]{:S(2)}) collective-permute-start(f32[520,128]{1,0:T(8,128)S(1)} %get-tuple-element.18), channel_id=1, source_target_pairs={{0,2},{1,3},{2,0},{3,1},{4,6},{5,7},{6,4},{7,5},{8,10},{9,11},{10,... | collective-permute-start | bytes 798728 | tf_op jit(solution)/shard_map/ppermute | solution.py:528
  13.6 8.0 %attend_near.1 = (f32[520,128]{1,0:T(8,128)S(1)}, bf16[128,256,128]{2,1,0:T(8,128)(2,1)}, bf16[128,256,128]{2,1,0:T(8,128)(2,1)}) custom-call(s32[128]{0:T(128)} %pos_h.3, f32[1088,128]{1,0:T(8,128)S(1)} %get-tuple-element.12.qs, f32[1088,128]{1,0:T(8,128)S(1)} %get-tuple-element.13.ks, f32[1088,128]{1,0:T(8,128)S(1)} %get-tuple-element.14.vs, ...), custom_call_target="tpu_custom_call" | custom-call | flops 10000000000 | bytes 25000000 | tf_op jit(solution)/shard_map/attend_near/pallas_call | solution.py:529
  21.6 0.0 copy-start
  21.6 0.0 copy-start.1
  21.7 0.0 collective-permute-done.o_got
  21.7 27.0 %combine.1.s_all = f32[4,15,32,256]{3,2,1,0:T(8,128)S(1)} custom-call(f32[520,128]{1,0:T(8,128)S(1)} %get-tuple-element.17.o_own, f32[520,128]{1,0:T(8,128)S(1)} %collective-permute-done.o_got, bf16[1024,3840]{1,0:T(8,128)(2,1)} %wo_h.1), custom_call_target="tpu_custom_call" | custom-call | tf_op jit(solution)/shard_map/combine/pallas_call | solution.py:544
  48.6 0.0 copy-done
  48.6 0.0 copy-done.1
  48.7 1.2 %finish.1 = bf16[128,3840]{1,0:T(8,128)(2,1)} custom-call(f32[4,15,32,256]{3,2,1,0:T(8,128)S(1)} %combine.1.s_all, bf16[128,3840]{1,0:T(8,128)(2,1)S(1)} %copy-done, f32[30,128]{1,0:T(8,128)S(1)} %bitcast.23), custom_call_target="tpu_custom_call" | custom-call | tf_op jit(solution)/shard_map/finish/pallas_call | solution.py:560
Async XLA Ops:
  10.5 11.1 %collective-permute-start = (f32[520,128]{1,0:T(8,128)S(1)}, f32[520,128]{1,0:T(8,128)S(1)}, u32[]{:S(2)}, u32[]{:S(2)}) collective-permute-start(f32[520,128]{1,0:T(8,128)S(1)} %get-tuple-element.18), channel_id=1, source_target_pairs={{0,2},{1,3},{2,0},{3,1},{4,6},{5,7},{6,4},{7,5},{8,10},{9,11},{10,... | collective-permute-start | bytes 798728 | tf_op jit(solution)/shard_map/ppermute | solution.py:528
  21.6 27.0 %copy-start = (bf16[128,3840]{1,0:T(8,128)(2,1)S(1)}, bf16[128,3840]{1,0:T(8,128)(2,1)}, u32[]{:S(2)}) copy-start(bf16[128,3840]{1,0:T(8,128)(2,1)} %x_ref.1) | copy-start | bytes 2949124
  21.6 27.0 %copy-start.1 = (f32[3840]{0:T(1024)S(1)}, f32[3840]{0:T(1024)}, u32[]{:S(2)}) copy-start(f32[3840]{0:T(1024)} %param.18) | copy-start | bytes 46084

commit v19 on v18

--- a/solution.py
+++ b/solution.py
@@ -28,7 +28,7 @@
 CW = 256
 NC = DM // CW
 WG = 3
-LASTS = 3
+LASTS = 6
 OWN = 32
 MROWS = 8 * OWN + 8
 MESH = pl.DeviceIdType.MESH

time: 50 us -> 51.9 us (1.038)
  Pallas kernels: 46.1 us -> 47.9 us
    pallas_call x1, Pallas kernels: 27 us -> 28.8 us  [local_step(): pl.pallas_call(comm_kernel, out_shape=pltpu.VMEM((4, NC, OWN, CW), f32),...]
  transfers between devices with their start and end apart: 1 -> 1, of which waited for: 0 -> 0; matrix products, arithmetic and copies ran while one was open for 0% -> 0% of each run, Pallas kernels for 16% -> 15%
where the time goes in v19:
time: 51.9 us; the launch traced here: 51.7 us
  Pallas kernels  47.9 us (92%)
  starting transfers between devices  3.09 us (6%)
  between operations  0.7 us (1%)
    pallas_call x1, Pallas kernels, local_step(): pl.pallas_call(comm_kernel, out_shape=pltpu.VMEM((4, NC, OWN, CW), f32),...  28.8 us
    pallas_call x1, Pallas kernels, local_step(): pl.pallas_call(far_kernel, out_shape=(jax.ShapeDtypeStruct((HROWS, LANES)...  9.89 us
    pallas_call x1, Pallas kernels, local_step(): pl.pallas_call(near_kernel, out_shape=(pltpu.VMEM((HROWS, LANES), f32), j...  8.01 us
    ppermute x1, starting transfers between devices, local_step(): o_got = lax.ppermute(o_far, 'sp', [(0, 2), (1, 3), (2, 0), (3, 1)])  3.09 us
    pallas_call x1, Pallas kernels, local_step(): pl.pallas_call(finish_kernel, out_shape=jax.ShapeDtypeStruct((ROWS, DM),...  1.21 us
  transfers between devices with their start and end apart: 1, of which 0 were waited for; matrix products, arithmetic and copies ran while one was open for 0% of the time, Pallas kernels for 15%

profile of v19, /device:TPU:0, one launch (start us, length us, event | category | flops | bytes accessed | tf_op | source)
XLA Modules:
  0.0 51.7 jit_solution(10533335359612417078)
XLA Ops:
  0.6 9.9 %attend_far.1 = (f32[520,128]{1,0:T(8,128)S(1)}, bf16[64,256,128]{2,1,0:T(8,128)(2,1)S(1)}, bf16[64,256,128]{2,1,0:T(8,128)(2,1)S(1)}, f32[1088,128]{1,0:T(8,128...) custom-call(s32[128]{0:T(128)} %pos_h.3, s32[1,128]{1,0:T(1,128)} %bitcast.29, f32[1,128]{1,0:T(1,128)} %constant.5.freq_h, ...), custom_call_target="tpu_custom_call" | custom-call | flops 2000000000 | bytes 25000000 | tf_op jit(solution)/shard_map/attend_far/pallas_call | solution.py:509
  10.5 3.1 %collective-permute-start = (f32[520,128]{1,0:T(8,128)S(1)}, f32[520,128]{1,0:T(8,128)S(1)}, u32[]{:S(2)}, u32[]{:S(2)}) collective-permute-start(f32[520,128]{1,0:T(8,128)S(1)} %get-tuple-element.18), channel_id=1, source_target_pairs={{0,2},{1,3},{2,0},{3,1},{4,6},{5,7},{6,4},{7,5},{8,10},{9,11},{10,... | collective-permute-start | bytes 798728 | tf_op jit(solution)/shard_map/ppermute | solution.py:528
  13.6 8.0 %attend_near.1 = (f32[520,128]{1,0:T(8,128)S(1)}, bf16[128,256,128]{2,1,0:T(8,128)(2,1)}, bf16[128,256,128]{2,1,0:T(8,128)(2,1)}) custom-call(s32[128]{0:T(128)} %pos_h.3, f32[1088,128]{1,0:T(8,128)S(1)} %get-tuple-element.12.qs, f32[1088,128]{1,0:T(8,128)S(1)} %get-tuple-element.13.ks, f32[1088,128]{1,0:T(8,128)S(1)} %get-tuple-element.14.vs, ...), custom_call_target="tpu_custom_call" | custom-call | flops 10000000000 | bytes 25000000 | tf_op jit(solution)/shard_map/attend_near/pallas_call | solution.py:529
  21.6 0.0 copy-start
  21.6 0.0 copy-start.1
  21.7 0.0 collective-permute-done.o_got
  21.7 28.8 %combine.1.s_all = f32[4,15,32,256]{3,2,1,0:T(8,128)S(1)} custom-call(f32[520,128]{1,0:T(8,128)S(1)} %get-tuple-element.17.o_own, f32[520,128]{1,0:T(8,128)S(1)} %collective-permute-done.o_got, bf16[1024,3840]{1,0:T(8,128)(2,1)} %wo_h.1), custom_call_target="tpu_custom_call" | custom-call | tf_op jit(solution)/shard_map/combine/pallas_call | solution.py:544
  50.5 0.0 copy-done
  50.5 0.0 copy-done.1
  50.5 1.2 %finish.1 = bf16[128,3840]{1,0:T(8,128)(2,1)} custom-call(f32[4,15,32,256]{3,2,1,0:T(8,128)S(1)} %combine.1.s_all, bf16[128,3840]{1,0:T(8,128)(2,1)S(1)} %copy-done, f32[30,128]{1,0:T(8,128)S(1)} %bitcast.23), custom_call_target="tpu_custom_call" | custom-call | tf_op jit(solution)/shard_map/finish/pallas_call | solution.py:560
Async XLA Ops:
  10.5 11.1 %collective-permute-start = (f32[520,128]{1,0:T(8,128)S(1)}, f32[520,128]{1,0:T(8,128)S(1)}, u32[]{:S(2)}, u32[]{:S(2)}) collective-permute-start(f32[520,128]{1,0:T(8,128)S(1)} %get-tuple-element.18), channel_id=1, source_target_pairs={{0,2},{1,3},{2,0},{3,1},{4,6},{5,7},{6,4},{7,5},{8,10},{9,11},{10,... | collective-permute-start | bytes 798728 | tf_op jit(solution)/shard_map/ppermute | solution.py:528
  21.6 28.9 %copy-start = (bf16[128,3840]{1,0:T(8,128)(2,1)S(1)}, bf16[128,3840]{1,0:T(8,128)(2,1)}, u32[]{:S(2)}) copy-start(bf16[128,3840]{1,0:T(8,128)(2,1)} %x_ref.1) | copy-start | bytes 2949124
  21.6 28.9 %copy-start.1 = (f32[3840]{0:T(1024)S(1)}, f32[3840]{0:T(1024)}, u32[]{:S(2)}) copy-start(f32[3840]{0:T(1024)} %param.18) | copy-start | bytes 46084

commit v20 on v19

--- a/solution.py
+++ b/solution.py
@@ -28,7 +28,7 @@
 CW = 256
 NC = DM // CW
 WG = 3
-LASTS = 6
+LASTS = 2
 OWN = 32
 MROWS = 8 * OWN + 8
 MESH = pl.DeviceIdType.MESH

time: 51.9 us -> 50 us (0.963)
  Pallas kernels: 47.9 us -> 46 us
    pallas_call x1, Pallas kernels: 28.8 us -> 26.9 us  [local_step(): pl.pallas_call(comm_kernel, out_shape=pltpu.VMEM((4, NC, OWN, CW), f32),...]
  transfers between devices with their start and end apart: 1 -> 1, of which waited for: 0 -> 0; matrix products, arithmetic and copies ran while one was open for 0% -> 0% of each run, Pallas kernels for 15% -> 16%
where the time goes in v20:
time: 50 us; the launch traced here: 49.8 us
  Pallas kernels  46 us (92%)
  starting transfers between devices  3.09 us (6%)
  between operations  0.7 us (1%)
    pallas_call x1, Pallas kernels, local_step(): pl.pallas_call(comm_kernel, out_shape=pltpu.VMEM((4, NC, OWN, CW), f32),...  26.9 us
    pallas_call x1, Pallas kernels, local_step(): pl.pallas_call(far_kernel, out_shape=(jax.ShapeDtypeStruct((HROWS, LANES)...  9.88 us
    pallas_call x1, Pallas kernels, local_step(): pl.pallas_call(near_kernel, out_shape=(pltpu.VMEM((HROWS, LANES), f32), j...  8.01 us
    ppermute x1, starting transfers between devices, local_step(): o_got = lax.ppermute(o_far, 'sp', [(0, 2), (1, 3), (2, 0), (3, 1)])  3.09 us
    pallas_call x1, Pallas kernels, local_step(): pl.pallas_call(finish_kernel, out_shape=jax.ShapeDtypeStruct((ROWS, DM),...  1.21 us
  transfers between devices with their start and end apart: 1, of which 0 were waited for; matrix products, arithmetic and copies ran while one was open for 0% of the time, Pallas kernels for 16%

profile of v20, /device:TPU:0, one launch (start us, length us, event | category | flops | bytes accessed | tf_op | source)
XLA Modules:
  0.0 49.8 jit_solution(12385358657039529385)
XLA Ops:
  0.6 9.9 %attend_far.1 = (f32[520,128]{1,0:T(8,128)S(1)}, bf16[64,256,128]{2,1,0:T(8,128)(2,1)S(1)}, bf16[64,256,128]{2,1,0:T(8,128)(2,1)S(1)}, f32[1088,128]{1,0:T(8,128...) custom-call(s32[128]{0:T(128)} %pos_h.3, s32[1,128]{1,0:T(1,128)} %bitcast.29, f32[1,128]{1,0:T(1,128)} %constant.5.freq_h, ...), custom_call_target="tpu_custom_call" | custom-call | flops 2000000000 | bytes 25000000 | tf_op jit(solution)/shard_map/attend_far/pallas_call | solution.py:509
  10.5 3.1 %collective-permute-start = (f32[520,128]{1,0:T(8,128)S(1)}, f32[520,128]{1,0:T(8,128)S(1)}, u32[]{:S(2)}, u32[]{:S(2)}) collective-permute-start(f32[520,128]{1,0:T(8,128)S(1)} %get-tuple-element.18), channel_id=1, source_target_pairs={{0,2},{1,3},{2,0},{3,1},{4,6},{5,7},{6,4},{7,5},{8,10},{9,11},{10,... | collective-permute-start | bytes 798728 | tf_op jit(solution)/shard_map/ppermute | solution.py:528
  13.6 8.0 %attend_near.1 = (f32[520,128]{1,0:T(8,128)S(1)}, bf16[128,256,128]{2,1,0:T(8,128)(2,1)}, bf16[128,256,128]{2,1,0:T(8,128)(2,1)}) custom-call(s32[128]{0:T(128)} %pos_h.3, f32[1088,128]{1,0:T(8,128)S(1)} %get-tuple-element.12.qs, f32[1088,128]{1,0:T(8,128)S(1)} %get-tuple-element.13.ks, f32[1088,128]{1,0:T(8,128)S(1)} %get-tuple-element.14.vs, ...), custom_call_target="tpu_custom_call" | custom-call | flops 10000000000 | bytes 25000000 | tf_op jit(solution)/shard_map/attend_near/pallas_call | solution.py:529
  21.6 0.0 copy-start
  21.6 0.0 copy-start.1
  21.7 0.0 collective-permute-done.o_got
  21.7 26.9 %combine.1.s_all = f32[4,15,32,256]{3,2,1,0:T(8,128)S(1)} custom-call(f32[520,128]{1,0:T(8,128)S(1)} %get-tuple-element.17.o_own, f32[520,128]{1,0:T(8,128)S(1)} %collective-permute-done.o_got, bf16[1024,3840]{1,0:T(8,128)(2,1)} %wo_h.1), custom_call_target="tpu_custom_call" | custom-call | tf_op jit(solution)/shard_map/combine/pallas_call | solution.py:544
  48.6 0.0 copy-done
  48.6 0.0 copy-done.1
  48.6 1.2 %finish.1 = bf16[128,3840]{1,0:T(8,128)(2,1)} custom-call(f32[4,15,32,256]{3,2,1,0:T(8,128)S(1)} %combine.1.s_all, bf16[128,3840]{1,0:T(8,128)(2,1)S(1)} %copy-done, f32[30,128]{1,0:T(8,128)S(1)} %bitcast.23), custom_call_target="tpu_custom_call" | custom-call | tf_op jit(solution)/shard_map/finish/pallas_call | solution.py:560
Async XLA Ops:
  10.5 11.1 %collective-permute-start = (f32[520,128]{1,0:T(8,128)S(1)}, f32[520,128]{1,0:T(8,128)S(1)}, u32[]{:S(2)}, u32[]{:S(2)}) collective-permute-start(f32[520,128]{1,0:T(8,128)S(1)} %get-tuple-element.18), channel_id=1, source_target_pairs={{0,2},{1,3},{2,0},{3,1},{4,6},{5,7},{6,4},{7,5},{8,10},{9,11},{10,... | collective-permute-start | bytes 798728 | tf_op jit(solution)/shard_map/ppermute | solution.py:528
  21.6 27.0 %copy-start = (bf16[128,3840]{1,0:T(8,128)(2,1)S(1)}, bf16[128,3840]{1,0:T(8,128)(2,1)}, u32[]{:S(2)}) copy-start(bf16[128,3840]{1,0:T(8,128)(2,1)} %x_ref.1) | copy-start | bytes 2949124
  21.6 27.0 %copy-start.1 = (f32[3840]{0:T(1024)S(1)}, f32[3840]{0:T(1024)}, u32[]{:S(2)}) copy-start(f32[3840]{0:T(1024)} %param.18) | copy-start | bytes 46084
